TPU v7x, 32 devices: a whole 2x2x4 slice. The times are simulated.
32 devices in a mesh: rows: 8 (over z, y), feat: 4 (over x, core).
Axes of the slice: x: 2, y: 2, z: 4, core: 2. Of those that a mesh axis runs over, the one named last changes fastest.
Arguments:
- cells: bfloat16 [1024, 80, 128], P('rows', 'feat'), may hold values from -19 to 19
- block_table: int32 [8], replicated, may hold values from 0 to 7, as said below
- row_live: int32 [1024], replicated, may hold values from 0 to 1, as said below
- row_train: int32 [1024], replicated, may hold values from 0 to 1, as said below
- feat_qkv: bfloat16 [128, 384], replicated, may hold values from -0.5 to 0.5
- feat_out: bfloat16 [128, 128], replicated, may hold values from -0.5 to 0.5
- item_qkv: bfloat16 [128, 384], replicated, may hold values from -0.5 to 0.5
- item_out: bfloat16 [128, 128], replicated, may hold values from -0.5 to 0.5
Outputs:
- layer_output: bfloat16 [1024, 80, 128], P(('rows', 'feat'))
Inputs may be any that keep to these rules, and one draw needn't show every extreme that they name: `block_table`: every table number appears in some block. `row_live`: every training row is live. `row_train`: each aligned group of 32 rows holds 1 to 4 training rows; some group holds exactly 4.
All inputs are finite; a program needn't handle non-finite values.
Results may differ from a plain program's by a relative error of at most 0.014.
Values may be sent and summed in bfloat16 or wider, within the bound.
No kernel may reach another device: no remote copies, remote signals or barrier semaphores. Data moves between devices by JAX's collectives and lax.ppermute only.
A program may use at most 64 MiB of HBM per device.

v0:
```python
import jax
import jax.numpy as jnp
from jax import lax
from jax.sharding import PartitionSpec as P

HEADS = 4
HEAD_DIM = 32
KEEP = 4
TABLES = 8


EPSILON = 1e-05
MASKED = -1e30


def compact_train(train_rows):
    positions = jnp.arange(train_rows.shape[-1], dtype=jnp.int32)
    ordinal = jnp.cumsum(train_rows, axis=-1) - 1
    slot_ids = jnp.arange(KEEP, dtype=jnp.int32)
    matched = (train_rows[..., None, :] == 1) & (ordinal[..., None, :] == slot_ids[:, None])
    return jnp.sum(jnp.where(matched, positions, 0), axis=-1)


def into_heads(tensor):
    return tensor.reshape(tensor.shape[:-1] + (HEADS, HEAD_DIM))


def attend_features(queries, key_part, value_part):
    row_count, query_feats = (queries.shape[0], queries.shape[1])
    blocks = max(1, row_count * query_feats // 1280)
    while row_count % blocks:
        blocks -= 1
    scaling = HEAD_DIM ** (-0.5)

    def attend_one_block(block_parts):
        block_query, block_key, block_value = block_parts
        scores = (
            jnp.einsum(
                "rqhd,rkhd->rhqk", block_query, block_key, preferred_element_type=jnp.float32
            )
            * scaling
        )
        shares = jax.nn.softmax(scores, axis=-1).astype(jnp.bfloat16)
        return jnp.einsum(
            "rhqk,rkhd->rqhd", shares, block_value, preferred_element_type=jnp.float32
        ).astype(jnp.bfloat16)

    def by_block(tensor):
        return tensor.reshape((blocks, row_count // blocks) + tensor.shape[1:])

    result = lax.map(
        attend_one_block, (by_block(queries), by_block(key_part), by_block(value_part))
    )
    return result.reshape(row_count, query_feats, HEADS * HEAD_DIM)


def feature_layer(normed_cells, feat_out, key_part, value_part, queries):
    attended = attend_features(queries, key_part, value_part)
    update = jnp.dot(attended, feat_out, preferred_element_type=jnp.float32)
    return (normed_cells.astype(jnp.float32) + update).astype(jnp.bfloat16)


def on_device(cells, block_table, row_live, row_train, feat_qkv, feat_out, item_qkv, item_out):
    rows_here, feats_here, width_all = cells.shape
    row_index = lax.axis_index("rows")
    feat_index = lax.axis_index("feat")
    row_devices = lax.axis_size("rows")
    feat_devices = lax.axis_size("feat")
    my_table = lax.dynamic_index_in_dim(block_table, row_index, keepdims=False)
    live_rows = lax.dynamic_slice_in_dim(row_live, row_index * rows_here, rows_here).astype(
        jnp.float32
    )
    values = cells.astype(jnp.float32)
    table_hot = (jnp.arange(TABLES, dtype=jnp.int32) == my_table).astype(jnp.float32)
    first_local = jnp.sum(values * live_rows[:, None, None], axis=(0, 2))
    count_local = jnp.sum(live_rows) * width_all
    first_sum, count_sum = lax.psum(
        (table_hot[:, None] * first_local[None, :], table_hot * count_local), "rows"
    )
    table_mean = first_sum / count_sum[:, None]
    mine_mean = lax.dynamic_index_in_dim(table_mean, my_table, keepdims=False)
    centred = values - mine_mean[None, :, None]
    second_local = jnp.sum(centred * centred * live_rows[:, None, None], axis=(0, 2))
    second_sum = lax.psum(table_hot[:, None] * second_local[None, :], "rows")
    table_spread = second_sum / count_sum[:, None]
    mine_spread = lax.dynamic_index_in_dim(table_spread, my_table, keepdims=False)
    normed = (centred * lax.rsqrt(mine_spread + EPSILON)[None, :, None]).astype(jnp.bfloat16)
    normed_rows = lax.all_to_all(normed, "feat", split_axis=0, concat_axis=1, tiled=True)
    projected = jnp.dot(normed_rows, feat_qkv, preferred_element_type=jnp.float32).astype(
        jnp.bfloat16
    )
    queries = into_heads(projected[..., :width_all])
    key_part = into_heads(projected[..., width_all : 2 * width_all])
    value_part = into_heads(projected[..., 2 * width_all :])
    mixed_rows = feature_layer(normed_rows, feat_out, key_part, value_part, queries)
    group_rows, total_feats = (mixed_rows.shape[0], mixed_rows.shape[1])
    per_device = total_feats * HEADS // row_devices
    first_row = row_index * rows_here + feat_index * group_rows
    train_here = lax.dynamic_slice_in_dim(row_train, first_row, group_rows)
    places = compact_train(train_here)
    chosen = jnp.take(mixed_rows, places, axis=0)
    item_query = jnp.dot(
        mixed_rows, item_qkv[:, :width_all], preferred_element_type=jnp.float32
    ).astype(jnp.bfloat16)
    item_query = item_query.reshape(group_rows, row_devices, per_device, HEAD_DIM)
    key_value = jnp.dot(chosen, item_qkv[:, width_all:], preferred_element_type=jnp.float32).astype(
        jnp.bfloat16
    )
    item_key = key_value[..., :width_all].reshape(KEEP, row_devices, per_device, HEAD_DIM)
    item_value = key_value[..., width_all:].reshape(KEEP, row_devices, per_device, HEAD_DIM)
    query_table = jnp.repeat(block_table, group_rows)
    groups_all = row_train.reshape(row_devices, feat_devices, group_rows)
    group_counts = jnp.sum(groups_all, axis=2)
    slot_ids = jnp.arange(KEEP, dtype=jnp.int32)
    key_valid = slot_ids[None, None, :] < jnp.transpose(group_counts)[:, :, None]
    key_table = jnp.broadcast_to(block_table[None, :, None], key_valid.shape)
    allowed = (query_table[:, None] == key_table.reshape(-1)[None, :]) & key_valid.reshape(-1)[
        None, :
    ]
    query_count = query_table.shape[0]
    key_count = allowed.shape[1]
    query_blocks = max(1, query_count // 512)
    while query_count % query_blocks:
        query_blocks -= 1
    scaling = HEAD_DIM ** (-0.5)
    blocked_allowed = allowed.reshape(query_blocks, query_count // query_blocks, key_count)
    local_query = lax.all_to_all(item_query, "rows", split_axis=1, concat_axis=0, tiled=True)
    local_key = lax.all_to_all(item_key, "rows", split_axis=1, concat_axis=0, tiled=True)
    local_value = lax.all_to_all(item_value, "rows", split_axis=1, concat_axis=0, tiled=True)
    every_key = lax.all_gather(local_key, "feat", axis=0, tiled=True)
    every_value = lax.all_gather(local_value, "feat", axis=0, tiled=True)

    def one_item(item_parts):
        single_query, single_key, single_value = item_parts

        def one_one_block(block_parts):
            block_query, block_allowed = block_parts
            scores = (
                jnp.dot(block_query, single_key.T, preferred_element_type=jnp.float32) * scaling
            )
            scores = jnp.where(block_allowed, scores, MASKED)
            shares = jax.nn.softmax(scores, axis=-1).astype(jnp.bfloat16)
            return jnp.dot(shares, single_value, preferred_element_type=jnp.float32).astype(
                jnp.bfloat16
            )

        blocked_query = single_query.reshape(query_blocks, query_count // query_blocks, HEAD_DIM)
        return lax.map(one_one_block, (blocked_query, blocked_allowed)).reshape(
            query_count, HEAD_DIM
        )

    by_item = (
        jnp.moveaxis(local_query[:, 0], 1, 0),
        jnp.moveaxis(every_key[:, 0], 1, 0),
        jnp.moveaxis(every_value[:, 0], 1, 0),
    )
    result = jnp.moveaxis(lax.map(one_item, by_item), 0, 1)[:, None]
    attended = lax.all_to_all(result, "rows", split_axis=0, concat_axis=1, tiled=True)
    attended = attended.reshape(group_rows, total_feats, width_all)
    update = jnp.dot(attended, item_out, preferred_element_type=jnp.float32)
    return (mixed_rows.astype(jnp.float32) + update).astype(jnp.bfloat16)


def solution(mesh):
    return jax.shard_map(
        on_device,
        mesh=mesh,
        in_specs=(P("rows", "feat", None), P(), P(), P(), P(), P(), P(), P()),
        out_specs=P(("rows", "feat"), None, None),
        check_vma=False,
    )
```

profile of v0, /device:TPU:0, one launch (start us, length us, event | category | flops | bytes accessed | tf_op | source)
XLA Modules:
  0.0 317.5 jit_solution(12919230653871559837)
XLA Ops:
  5.5 1.6 fusion.40
  7.2 23.4 %all-reduce = (f32[8,20]{1,0:T(8,128)S(1)}, f32[8]{0:T(128)S(1)}) all-reduce(f32[8,20]{1,0:T(8,128)S(1)} %broadcast_multiply_fusion.1, f32[8]{0:T(128)S(1)} %compare_select_fusion.2), channel_id=1, replica_groups=mesh['rows'=8,'feat'=4] {'rows'}, use_global_device_ids=true, to_apply=%region_1.2 | all-reduce | flops 168 | bytes 1344 | tf_op jit(solution)/shard_map/psum | solution.py:77
  31.2 1.7 fusion.38
  33.0 17.1 %psum.23 = f32[8,20]{1,0:T(8,128)S(1)} all-reduce(f32[8,20]{1,0:T(8,128)S(1)} %broadcast_multiply_fusion), channel_id=1, replica_groups=mesh['rows'=8,'feat'=4] {'rows'}, use_global_device_ids=true, to_apply=%region_5.6 | all-reduce | flops 160 | bytes 1280 | tf_op jit(solution)/shard_map/psum | solution.py:84
  50.2 2.5 fusion.39
  52.6 3.5 %all-to-all-start = ((bf16[128,20,128]{2,1,0:T(8,128)(2,1)}), bf16[128,20,128]{2,1,0:T(8,128)(2,1)S(1)}, u32[]{:S(2)}, u32[]{:S(2)}) async-start(bf16[128,20,128]{2,1,0:T(8,128)(2,1)} %fusion.39), calls=%async_computation | async-start | bytes 1572864 | tf_op jit(solution)/shard_map/all_to_all | solution.py:88
  56.7 11.0 %all-to-all-done = bf16[128,20,128]{2,1,0:T(8,128)(2,1)S(1)} async-done(((bf16[128,20,128]{2,1,0:T(8,128)(2,1)}), bf16[128,20,128]{2,1,0:T(8,128)(2,1)S(1)}, u32[]{:S(2)}, u32[]{:S(2)}) %all-to-all-start) | async-done | bytes 655392 | tf_op jit(solution)/shard_map/all_to_all | solution.py:88
  72.3 11.1 %while.25 = (s32[]{:T(128)}, bf16[2,16,80,4,32]{2,4,3,1,0:T(8,128)(2,1)}, bf16[2,16,80,4,32]{2,4,3,1,0:T(8,128)(2,1)}, bf16[2,16,80,4,32]{2,4,3,1,0:T(8,128)(2,1...) while((s32[]{:T(128)}, bf16[2,16,80,4,32]{2,4,3,1,0:T(8,128)(2,1)}, ...), condition=%wide.region_9.10_spmd, body=%wide.region_6.9_spmd.sunk | while | flops 55050320 | bytes 17553560 | solution.py:51
  72.9 3.4 %fusion.79 = (f32[16,4,80]{2,1,0:T(4,128)S(1)}, f32[16,4,80,80]{2,3,1,0:T(8,128)S(1)}) fusion(f32[16,4,80,80]{2,3,1,0:T(8,128)S(1)} %fusion.78), kind=kOutput, calls=%fused_computation.89.clone.1 | output fusion | flops 1638479 | bytes 3297280 | tf_op jit(solution)/shard_map/while/body/eval_jaxpr/sub | solution.py:43
  78.5 3.4 %fusion.79 = (f32[16,4,80]{2,1,0:T(4,128)S(1)}, f32[16,4,80,80]{2,3,1,0:T(8,128)S(1)}) fusion(f32[16,4,80,80]{2,3,1,0:T(8,128)S(1)} %fusion.78), kind=kOutput, calls=%fused_computation.89.clone.1 | output fusion | flops 1638479 | bytes 3297280 | tf_op jit(solution)/shard_map/while/body/eval_jaxpr/sub | solution.py:43
  83.4 1.9 fusion.41
  87.6 3.4 %all-to-all-start.2 = ((bf16[8,2,2560]{2,1,0:T(2,128)(2,1)}), bf16[8,2,2560]{2,1,0:T(2,128)(2,1)S(1)}, u32[]{:S(2)}, u32[]{:S(2)}) async-start(bf16[8,2,2560]{2,1,0:T(2,128)(2,1)} %reshape.214), calls=%async_computation.2 | async-start | bytes 163840 | tf_op jit(solution)/shard_map/all_to_all | solution.py:128
  92.3 5.6 %all-to-all-done.2 = bf16[8,2,2560]{2,1,0:T(2,128)(2,1)S(1)} async-done(((bf16[8,2,2560]{2,1,0:T(2,128)(2,1)}), bf16[8,2,2560]{2,1,0:T(2,128)(2,1)S(1)}, u32[]{:S(2)}, u32[]{:S(2)}) %all-to-all-start.2) | async-done | bytes 81952 | tf_op jit(solution)/shard_map/all_to_all | solution.py:128
  97.9 3.4 %all-to-all-start.3 = ((bf16[8,2,2560]{2,1,0:T(2,128)(2,1)}), bf16[8,2,2560]{2,1,0:T(2,128)(2,1)S(1)}, u32[]{:S(2)}, u32[]{:S(2)}) async-start(bf16[8,2,2560]{2,1,0:T(2,128)(2,1)} %reshape.216), calls=%async_computation.3 | async-start | bytes 163840 | tf_op jit(solution)/shard_map/all_to_all | solution.py:129
  102.4 3.1 reshape.193
  105.5 2.5 copy.118
  107.9 5.7 %reshape.212 = bf16[8,2,20480]{2,1,0:T(2,128)(2,1)} reshape(bf16[8,32,32,40]{3,2,1,0:T(8,128)(2,1)} %bitcast.134) | data formatting | bytes 1310720
  113.7 5.9 %all-to-all-start.1 = ((bf16[8,2,20480]{2,1,0:T(2,128)(2,1)}), bf16[8,2,20480]{2,1,0:T(2,128)(2,1)}, u32[]{:S(2)}, u32[]{:S(2)}) async-start(bf16[8,2,20480]{2,1,0:T(2,128)(2,1)} %reshape.212), calls=%async_computation.1 | async-start | bytes 1310720 | tf_op jit(solution)/shard_map/all_to_all | solution.py:127
  120.9 9.1 %all_gather.6 = bf16[128,1,40,32]{2,3,1,0:T(8,128)(2,1)S(1)} all-gather(bf16[32,1,40,32]{2,3,1,0:T(8,128)(2,1)S(1)} %bitcast.143), channel_id=1, replica_groups=mesh['rows'=8,'feat'=4] {'feat'}, dimensions={0}, use_global_device_ids=true | all-gather | bytes 409600 | tf_op jit(solution)/shard_map/all_gather | solution.py:130
  130.0 2.9 copy.125
  133.3 10.2 %all_gather.7 = bf16[128,1,40,32]{2,3,1,0:T(8,128)(2,1)S(1)} all-gather(bf16[32,1,40,32]{2,3,1,0:T(8,128)(2,1)S(1)} %bitcast.144), channel_id=1, replica_groups=mesh['rows'=8,'feat'=4] {'feat'}, dimensions={0}, use_global_device_ids=true | all-gather | bytes 409600 | tf_op jit(solution)/shard_map/all_gather | solution.py:131
  143.5 2.9 copy.126
  146.3 5.0 %reshape.213 = bf16[8,32,32,40]{3,2,1,0:T(8,128)(2,1)S(1)} reshape(bf16[8,2,20480]{2,1,0:T(2,128)(2,1)} %all-to-all-done.1) | data formatting | bytes 1310720
  151.4 4.9 %copy.124 = bf16[40,256,32]{2,1,0:T(8,128)(2,1)} copy(bf16[40,256,32]{0,2,1:T(8,128)(2,1)S(1)} %bitcast.135) | data formatting | bytes 1310720
  156.3 105.4 %while.26 = (s32[]{:T(128)}, bf16[40,256,32]{1,2,0:T(8,128)(2,1)}, bf16[40,256,32]{2,1,0:T(8,128)(2,1)}, bf16[40,128,32]{2,1,0:T(8,128)(2,1)}, bf16[40,128,32]{2...) while((s32[]{:T(128)}, bf16[40,256,32]{1,2,0:T(8,128)(2,1)}, ...), condition=%wide.region_16.17_spmd.clone, body=%wide.region_13.16_spmd.clone.sunk | while | flops 4529666 | bytes 549597 | solution.py:157
  157.4 1.6 fusion.84
  160.0 1.6 fusion.84
  162.6 1.6 fusion.84
  165.3 1.6 fusion.84
  167.9 1.6 fusion.84
  170.5 1.6 fusion.84
  173.2 1.6 fusion.84
  175.8 1.6 fusion.84
  178.4 1.6 fusion.84
  181.1 1.6 fusion.84
  183.7 1.6 fusion.84
  186.4 1.6 fusion.84
  189.0 1.6 fusion.84
  191.6 1.6 fusion.84
  194.3 1.6 fusion.84
  196.9 1.6 fusion.84
  199.5 1.6 fusion.84
  202.2 1.6 fusion.84
  204.8 1.6 fusion.84
  207.4 1.6 fusion.84
  210.1 1.6 fusion.84
  212.7 1.6 fusion.84
  215.3 1.6 fusion.84
  218.0 1.6 fusion.84
  220.6 1.6 fusion.84
  223.3 1.6 fusion.84
  225.9 1.6 fusion.84
  228.5 1.6 fusion.84
  231.2 1.6 fusion.84
  233.8 1.6 fusion.84
  257.5 1.6 fusion.84
  261.7 4.5 %copy.127 = bf16[40,256,32]{0,2,1:T(8,128)(2,1)S(1)} copy(bf16[40,256,32]{1,2,0:T(8,128)(2,1)} %get-tuple-element.83) | data formatting | bytes 1310720 | tf_op jit(solution)/shard_map/while | solution.py:157
  266.2 1.7 bitcast_bitcast_fusion
  267.9 5.0 %reshape.218 = bf16[8,2,20480]{2,1,0:T(2,128)(2,1)S(1)} reshape(bf16[256,1,32,40]{3,2,1,0:T(8,128)(2,1)} %bitcast_bitcast_fusion) | data formatting | bytes 1310720
  273.0 24.0 %all_to_all.84 = bf16[8,2,20480]{2,1,0:T(2,128)(2,1)S(1)} all-to-all(bf16[8,2,20480]{2,1,0:T(2,128)(2,1)S(1)} %reshape.218), channel_id=1, replica_groups=mesh['rows'=8,'feat'=4] {'rows'}, dimensions={0} | all-to-all | bytes 1310720 | tf_op jit(solution)/shard_map/all_to_all | solution.py:158
  297.0 4.3 %reshape.219 = bf16[256,1,32,40]{3,2,1,0:T(8,128)(2,1)} reshape(bf16[8,2,20480]{2,1,0:T(2,128)(2,1)S(1)} %all_to_all.84) | data formatting | bytes 1310720
  301.3 5.9 %copy.135 = bf16[8,32,1,40,32]{1,0,4,3,2:T(8,128)(2,1)S(1)} copy(bf16[8,32,1,40,32]{3,4,1,0,2:T(8,128)(2,1)} %bitcast.136) | data formatting | bytes 1310720 | tf_op jit(solution)/shard_map/all_to_all | solution.py:158
  307.2 5.6 %copy.129 = bf16[32,8,1,40,32]{4,3,1,0,2:T(8,128)(2,1)} copy(bf16[32,8,1,40,32]{0,1,4,3,2:T(8,128)(2,1)S(1)} %bitcast.133) | data formatting | bytes 1310720 | tf_op jit(solution)/shard_map/all_to_all | solution.py:158
  312.8 3.6 %reshape.197 = bf16[32,80,128]{2,1,0:T(8,128)(2,1)S(1)} reshape(bf16[32,8,1,40,32]{4,3,1,0,2:T(8,128)(2,1)} %copy.129) | data formatting | bytes 1310720 | tf_op jit(solution)/shard_map/reshape | solution.py:159
  (170 shorter events, 77.9 us)
Async XLA Ops:
  0.0 68.7 %copy-start = (bf16[128,384]{1,0:T(8,128)(2,1)S(1)}, bf16[128,384]{1,0:T(8,128)(2,1)}, u32[]{:S(2)}) copy-start(bf16[128,384]{1,0:T(8,128)(2,1)} %param.16) | copy-start | bytes 294916
  7.1 49.0 %copy-start.8 = (s32[1024]{0:T(1024)S(1)}, s32[1024]{0:T(1024)}, u32[]{:S(2)}) copy-start(s32[1024]{0:T(1024)} %param.15) | copy-start | bytes 12292
  52.6 15.1 %all-to-all-start = ((bf16[128,20,128]{2,1,0:T(8,128)(2,1)}), bf16[128,20,128]{2,1,0:T(8,128)(2,1)S(1)}, u32[]{:S(2)}, u32[]{:S(2)}) async-start(bf16[128,20,128]{2,1,0:T(8,128)(2,1)} %fusion.39), calls=%async_computation | async-start | bytes 1572864 | tf_op jit(solution)/shard_map/all_to_all | solution.py:88
  67.9 0.8 copy-start.1
  72.3 11.1 %copy-start.6 = (bf16[128,128]{1,0:T(8,128)(2,1)S(1)}, bf16[128,128]{1,0:T(8,128)(2,1)}, u32[]{:S(2)}) copy-start(bf16[128,128]{1,0:T(8,128)(2,1)} %param.17) | copy-start | bytes 98308
  72.9 3.5 %copy-start.2 = (bf16[2,16,80,4,32]{2,4,3,1,0:T(8,128)(2,1)S(1)}, bf16[2,16,80,4,32]{2,4,3,1,0:T(8,128)(2,1)}, u32[]{:S(2)}) copy-start(bf16[2,16,80,4,32]{2,4,3,1,0:T(8,128)(2,1)} %get-tuple-element.284) | copy-start | bytes 1966084 | tf_op jit(solution)/shard_map/while
  72.9 3.5 %copy-start.4 = (bf16[2,16,80,4,32]{2,4,3,1,0:T(8,128)(2,1)S(1)}, bf16[2,16,80,4,32]{2,4,3,1,0:T(8,128)(2,1)}, u32[]{:S(2)}) copy-start(bf16[2,16,80,4,32]{2,4,3,1,0:T(8,128)(2,1)} %get-tuple-element.291) | copy-start | bytes 1966084 | tf_op jit(solution)/shard_map/while
  76.9 1.0 copy-start.3
  78.4 3.5 %copy-start.2 = (bf16[2,16,80,4,32]{2,4,3,1,0:T(8,128)(2,1)S(1)}, bf16[2,16,80,4,32]{2,4,3,1,0:T(8,128)(2,1)}, u32[]{:S(2)}) copy-start(bf16[2,16,80,4,32]{2,4,3,1,0:T(8,128)(2,1)} %get-tuple-element.284) | copy-start | bytes 1966084 | tf_op jit(solution)/shard_map/while
  78.4 3.5 %copy-start.4 = (bf16[2,16,80,4,32]{2,4,3,1,0:T(8,128)(2,1)S(1)}, bf16[2,16,80,4,32]{2,4,3,1,0:T(8,128)(2,1)}, u32[]{:S(2)}) copy-start(bf16[2,16,80,4,32]{2,4,3,1,0:T(8,128)(2,1)} %get-tuple-element.291) | copy-start | bytes 1966084 | tf_op jit(solution)/shard_map/while
  82.4 1.0 copy-start.3
  83.4 2.5 copy-start.5
  87.6 10.3 %all-to-all-start.2 = ((bf16[8,2,2560]{2,1,0:T(2,128)(2,1)}), bf16[8,2,2560]{2,1,0:T(2,128)(2,1)S(1)}, u32[]{:S(2)}, u32[]{:S(2)}) async-start(bf16[8,2,2560]{2,1,0:T(2,128)(2,1)} %reshape.214), calls=%async_computation.2 | async-start | bytes 163840 | tf_op jit(solution)/shard_map/all_to_all | solution.py:128
  97.9 15.8 %all-to-all-start.3 = ((bf16[8,2,2560]{2,1,0:T(2,128)(2,1)}), bf16[8,2,2560]{2,1,0:T(2,128)(2,1)S(1)}, u32[]{:S(2)}, u32[]{:S(2)}) async-start(bf16[8,2,2560]{2,1,0:T(2,128)(2,1)} %reshape.216), calls=%async_computation.3 | async-start | bytes 163840 | tf_op jit(solution)/shard_map/all_to_all | solution.py:129
  107.9 12.2 %copy-start.9 = (s32[8]{0:T(128)S(1)}, s32[8]{0:T(128)}, u32[]{:S(2)}) copy-start(s32[8]{0:T(128)} %param.13) | copy-start | bytes 100
  113.7 32.7 %all-to-all-start.1 = ((bf16[8,2,20480]{2,1,0:T(2,128)(2,1)}), bf16[8,2,20480]{2,1,0:T(2,128)(2,1)}, u32[]{:S(2)}, u32[]{:S(2)}) async-start(bf16[8,2,20480]{2,1,0:T(2,128)(2,1)} %reshape.212), calls=%async_computation.1 | async-start | bytes 1310720 | tf_op jit(solution)/shard_map/all_to_all | solution.py:127
  312.8 3.6 %copy-start.7 = (bf16[128,128]{1,0:T(8,128)(2,1)S(1)}, bf16[128,128]{1,0:T(8,128)(2,1)}, u32[]{:S(2)}) copy-start(bf16[128,128]{1,0:T(8,128)(2,1)} %param.19) | copy-start | bytes 98308
where the time goes:
time: 323 us; the launch traced here: 318 us
  matrix products  111 us (34%)
  blocking collectives  83.7 us (26%)
  local copies, waits for them, and re-layouts  69.6 us (22%)
  other arithmetic  18 us (6%)
  waiting for transfers between devices  16.6 us (5%)
  starting transfers between devices  16.1 us (5%)
    dot_general x40, matrix products, one_one_block(): jnp.dot(shares, single_value, preferred_element_type=jnp.float32)  62.3 us
    dot_general x40, matrix products, one_one_block(): jnp.dot(block_query, single_key.T, preferred_element_type=jnp.float32)  41.1 us
    unnamed x27, local copies, waits for them, and re-layouts  36.2 us
    all_to_all x1, blocking collectives, on_device(): lax.all_to_all(result, 'rows', split_axis=0, concat_axis=1, tiled=True)  24 us
    psum x1, blocking collectives, on_device(): lax.psum((table_hot[:, None] * first_local[None, :], table_hot * count_lo...  23.4 us
    psum x1, blocking collectives, on_device(): second_sum = lax.psum(table_hot[:, None] * second_local[None, :], 'rows')  17.1 us
    all_to_all x2, local copies, waits for them, and re-layouts, on_device(): lax.all_to_all(result, 'rows', split_axis=0, concat_axis=1, tiled=True)  11.5 us
    all_to_all x1, waiting for transfers between devices, on_device(): lax.all_to_all(normed, 'feat', split_axis=0, concat_axis=1, tiled=True)  11 us
  transfers between devices with their start and end apart: 4, of which 2 were waited for; matrix products, arithmetic and copies ran while one was open for 7% of the time, Pallas kernels for 0%

commit v1 on v0

--- a/solution.py
+++ b/solution.py
@@ -1,6 +1,11 @@
+import functools
+import math
+
 import jax
 import jax.numpy as jnp
 from jax import lax
+from jax.experimental import pallas as pl
+from jax.experimental.pallas import tpu as pltpu
 from jax.sharding import PartitionSpec as P
 
 HEADS = 4
@@ -11,6 +16,7 @@
 
 EPSILON = 1e-05
 MASKED = -1e30
+SCALE2 = HEAD_DIM ** (-0.5) * math.log2(math.e)
 
 
 def compact_train(train_rows):
@@ -161,9 +167,326 @@
     return (mixed_rows.astype(jnp.float32) + update).astype(jnp.bfloat16)
 
 
+def prepare_kernel(chunks, live_ref, train_ref, cells_ref, bias_ref, train_out, *refs):
+    place = refs[-1]
+    outs = refs[:-1]
+    rows_here, feats_here, width = cells_ref.shape
+    feat_devices = lax.axis_size("feat")
+    group_rows = rows_here // feat_devices
+    feat_index = lax.axis_index("feat")
+    base = lax.axis_index("rows") * rows_here
+
+    def first(step, carry):
+        total, count = carry
+        for inner in range(8):
+            row = step * 8 + inner
+            weight = live_ref[base + row].astype(jnp.float32)
+            total = total + cells_ref[row].astype(jnp.float32) * weight
+            count = count + weight
+        return total, count
+
+    zeros = jnp.zeros((feats_here, width), jnp.float32)
+    total, count = lax.fori_loop(0, rows_here // 8, first, (zeros, jnp.float32(0)))
+    entries = jnp.full((feats_here, 1), count * width, jnp.float32)
+    mean = jnp.broadcast_to(jnp.sum(total, axis=1, keepdims=True) / entries, (feats_here, width))
+
+    def second(step, total):
+        for inner in range(8):
+            row = step * 8 + inner
+            weight = live_ref[base + row].astype(jnp.float32)
+            centred = cells_ref[row].astype(jnp.float32) - mean
+            total = total + centred * centred * weight
+        return total
+
+    total = lax.fori_loop(0, rows_here // 8, second, zeros)
+    spread = jnp.sum(total, axis=1, keepdims=True) / entries
+    factor = jnp.broadcast_to(lax.rsqrt(spread + EPSILON), (feats_here, width))
+
+    def normed(row):
+        return ((cells_ref[row].astype(jnp.float32) - mean) * factor).astype(jnp.bfloat16)
+
+    lane = lax.broadcasted_iota(jnp.int32, bias_ref.shape, 1)
+    counts = jnp.zeros(bias_ref.shape, jnp.int32)
+    for group in range(feat_devices):
+        for slot in range(KEEP):
+            place[group * (KEEP + 1) + slot] = group * group_rows
+
+        def scan(row, count):
+            place[group * (KEEP + 1) + count] = group * group_rows + row
+            return count + train_ref[base + group * group_rows + row]
+
+        found = lax.fori_loop(0, group_rows, scan, jnp.int32(0), unroll=True)
+        counts = jnp.where(lane // KEEP == group, found, counts)
+    bias_ref[...] = jnp.where(lane % KEEP < counts, 0.0, MASKED)
+
+    for group in range(feat_devices):
+        for slot in range(KEEP):
+            key = group * KEEP + slot
+            train_out[pl.ds(key * feats_here, feats_here), :] = normed(
+                place[group * (KEEP + 1) + slot]
+            )
+    for step in range(feat_devices):
+        first_row = (feat_index ^ step) * group_rows
+        done = 0
+        for at, size in enumerate(chunks):
+            out = outs[step * len(chunks) + at]
+            for row in range(size):
+                out[pl.ds(row * feats_here, feats_here), :] = normed(first_row + done + row)
+            done += size
+
+
+def prepare(cells, row_live, row_train, chunks):
+    rows_here, feats_here, width = cells.shape
+    feat_devices = lax.axis_size("feat")
+    keys = feat_devices * KEEP
+    shapes = [
+        jax.ShapeDtypeStruct((8, 128), jnp.float32),
+        jax.ShapeDtypeStruct((keys * feats_here, width), jnp.bfloat16),
+    ]
+    for _ in range(feat_devices):
+        for size in chunks:
+            shapes.append(jax.ShapeDtypeStruct((size * feats_here, width), jnp.bfloat16))
+    outs = pl.pallas_call(
+        functools.partial(prepare_kernel, chunks),
+        out_shape=shapes,
+        in_specs=[
+            pl.BlockSpec(memory_space=pltpu.SMEM),
+            pl.BlockSpec(memory_space=pltpu.SMEM),
+            pl.BlockSpec(memory_space=pltpu.VMEM),
+        ],
+        out_specs=[pl.BlockSpec(memory_space=pltpu.VMEM)] * len(shapes),
+        scratch_shapes=[pltpu.SMEM((feat_devices * (KEEP + 1),), jnp.int32)],
+        name="prepare",
+    )(row_live, row_train, cells)
+    bias, train_rows = outs[0], outs[1]
+    sends = [
+        [outs[2 + step * len(chunks) + at] for at in range(len(chunks))]
+        for step in range(feat_devices)
+    ]
+    return bias, train_rows, sends
+
+
+def assemble(parts, held, joined, rows):
+    feat_devices = len(parts)
+    feats_here = parts[0].shape[0] // rows
+    total_feats = feat_devices * feats_here
+    feat_index = lax.axis_index("feat")
+    for step in range(feat_devices):
+        held[feat_index ^ step] = parts[step][...]
+    for row in range(rows):
+        for source in range(feat_devices):
+            joined[pl.ds(row * total_feats + source * feats_here, feats_here), :] = held[
+                source, pl.ds(row * feats_here, feats_here), :
+            ]
+
+
+def head_masks(rows, width):
+    lane = lax.broadcasted_iota(jnp.int32, (rows, width), 1)
+    return [(lane // HEAD_DIM) == head for head in range(HEADS)]
+
+
+def attend(queries, keys, values, masks, bias):
+    count, width = queries.shape
+    stacked = jnp.concatenate(
+        [jnp.where(mask, queries, jnp.zeros_like(queries)) for mask in masks[0]], axis=0
+    )
+    scores = lax.dot_general(
+        stacked, keys, (((1,), (1,)), ((), ())), preferred_element_type=jnp.float32
+    )
+    if bias is not None:
+        scores = scores + bias
+    top = jnp.max(scores, axis=1, keepdims=True)
+    shares = jnp.exp2((scores - top) * SCALE2).astype(jnp.bfloat16)
+    both = jnp.concatenate([values, jnp.ones_like(values)], axis=1)
+    mixed = jnp.dot(shares, both, preferred_element_type=jnp.float32)
+    out, total = mixed[:count, :width], mixed[:count, width:]
+    for head in range(1, HEADS):
+        block = mixed[head * count : (head + 1) * count]
+        out = jnp.where(masks[1][head], block[:, :width], out)
+        total = jnp.where(masks[1][head], block[:, width:], total)
+    return out / total
+
+
+def feature_rows(joined, base, rows, feats, qkv_ref, out_ref):
+    width = joined.shape[1]
+    cells = joined[pl.ds(base, rows * feats), :]
+    projected = jnp.dot(cells, qkv_ref[...], preferred_element_type=jnp.float32).astype(
+        jnp.bfloat16
+    )
+    masks = head_masks(feats, width)
+    attended = []
+    for row in range(rows):
+        block = projected[row * feats : (row + 1) * feats]
+        attended.append(
+            attend(
+                block[:, :width],
+                block[:, width : 2 * width],
+                block[:, 2 * width :],
+                (masks, masks),
+                None,
+            ).astype(jnp.bfloat16)
+        )
+    attended = jnp.concatenate(attended, axis=0)
+    update = jnp.dot(attended, out_ref[...], preferred_element_type=jnp.float32)
+    return (cells.astype(jnp.float32) + update).astype(jnp.bfloat16)
+
+
+STEP = 4
+
+
+def key_kernel(rows, *refs):
+    feat_devices = lax.axis_size("feat")
+    parts = refs[:feat_devices]
+    feat_qkv, feat_out, item_qkv, out_ref, held, joined, key_ref, value_ref = refs[feat_devices:]
+    feats = joined.shape[0] // rows
+    width = joined.shape[1]
+    assemble(parts, held, joined, rows)
+
+    def one(step, carry):
+        base = pl.multiple_of(step * (STEP * feats), STEP * feats)
+        mixed = feature_rows(joined, base, STEP, feats, feat_qkv, feat_out)
+        both = jnp.dot(mixed, item_qkv[:, width:], preferred_element_type=jnp.float32)
+        key_ref[pl.ds(base, STEP * feats), :] = both[:, :width]
+        value_ref[pl.ds(base, STEP * feats), :] = both[:, width:]
+        return carry
+
+    lax.fori_loop(0, rows // STEP, one, 0)
+    for feat in range(feats):
+        here = pl.ds(feat, rows, stride=feats)
+        out_ref[feat, :, :width] = key_ref[here, :].astype(jnp.bfloat16)
+        out_ref[feat, :, width:] = value_ref[here, :].astype(jnp.bfloat16)
+
+
+def key_rows(parts, feat_qkv, feat_out, item_qkv):
+    feat_devices = len(parts)
+    rows = feat_devices * KEEP
+    feats_here = parts[0].shape[0] // rows
+    feats = feat_devices * feats_here
+    width = parts[0].shape[1]
+    return pl.pallas_call(
+        functools.partial(key_kernel, rows),
+        out_shape=jax.ShapeDtypeStruct((feats, rows, 2 * width), jnp.bfloat16),
+        in_specs=[pl.BlockSpec(memory_space=pltpu.VMEM)] * (feat_devices + 3),
+        out_specs=pl.BlockSpec(memory_space=pltpu.VMEM),
+        scratch_shapes=[
+            pltpu.VMEM((feat_devices, rows * feats_here, width), jnp.bfloat16),
+            pltpu.VMEM((rows * feats, width), jnp.bfloat16),
+            pltpu.VMEM((rows * feats, width), jnp.float32),
+            pltpu.VMEM((rows * feats, width), jnp.float32),
+        ],
+        name="keys",
+    )(*parts, feat_qkv, feat_out, item_qkv)
+
+
+def row_kernel(rows, *refs):
+    feat_devices = lax.axis_size("feat")
+    parts = refs[:feat_devices]
+    (feat_qkv, feat_out, item_qkv, item_out, keys_ref, bias_ref, out_ref) = refs[
+        feat_devices : feat_devices + 7
+    ]
+    held, joined, mixed_ref, query_ref, item_ref = refs[feat_devices + 7 :]
+    feats = joined.shape[0] // rows
+    width = joined.shape[1]
+    key_count = keys_ref.shape[1]
+    assemble(parts, held, joined, rows)
+
+    def one(step, carry):
+        base = pl.multiple_of(step * (STEP * feats), STEP * feats)
+        mixed = feature_rows(joined, base, STEP, feats, feat_qkv, feat_out)
+        mixed_ref[pl.ds(base, STEP * feats), :] = mixed
+        query_ref[pl.ds(base, STEP * feats), :] = jnp.dot(
+            mixed, item_qkv[:, :width], preferred_element_type=jnp.float32
+        )
+        return carry
+
+    lax.fori_loop(0, rows // STEP, one, 0)
+    bias = bias_ref[:1, :key_count]
+    masks = head_masks(rows, width)
+
+    def item(step, carry):
+        for inner in range(8):
+            feat = step * 8 + inner
+            queries = query_ref[pl.ds(feat, rows, stride=feats), :].astype(jnp.bfloat16)
+            both = keys_ref[feat]
+            item_ref[pl.ds(feat, rows, stride=feats), :] = attend(
+                queries, both[:, :width], both[:, width:], (masks, masks), bias
+            )
+        return carry
+
+    lax.fori_loop(0, feats // 8, item, 0)
+
+    def last(step, carry):
+        base = pl.multiple_of(step * (STEP * feats), STEP * feats)
+        attended = item_ref[pl.ds(base, STEP * feats), :].astype(jnp.bfloat16)
+        update = jnp.dot(attended, item_out[...], preferred_element_type=jnp.float32)
+        result = (mixed_ref[pl.ds(base, STEP * feats), :].astype(jnp.float32) + update).astype(
+            jnp.bfloat16
+        )
+        for row in range(STEP):
+            out_ref[step * STEP + row] = result[row * feats : (row + 1) * feats]
+        return carry
+
+    lax.fori_loop(0, rows // STEP, last, 0)
+
+
+def own_rows(parts, rows, feat_qkv, feat_out, item_qkv, item_out, keys, bias):
+    feat_devices = len(parts)
+    feats_here = parts[0].shape[0] // rows
+    feats = feat_devices * feats_here
+    width = parts[0].shape[1]
+    return pl.pallas_call(
+        functools.partial(row_kernel, rows),
+        out_shape=jax.ShapeDtypeStruct((rows, feats, width), jnp.bfloat16),
+        in_specs=[pl.BlockSpec(memory_space=pltpu.VMEM)] * (feat_devices + 6),
+        out_specs=pl.BlockSpec(memory_space=pltpu.VMEM),
+        scratch_shapes=[
+            pltpu.VMEM((feat_devices, rows * feats_here, width), jnp.bfloat16),
+            pltpu.VMEM((rows * feats, width), jnp.bfloat16),
+            pltpu.VMEM((rows * feats, width), jnp.bfloat16),
+            pltpu.VMEM((rows * feats, width), jnp.float32),
+            pltpu.VMEM((rows * feats, width), jnp.float32),
+        ],
+        name="rows",
+    )(*parts, feat_qkv, feat_out, item_qkv, item_out, keys, bias)
+
+
+def swap(tensor, step):
+    devices = lax.axis_size("feat")
+    return lax.ppermute(tensor, "feat", [(one, one ^ step) for one in range(devices)])
+
+
+CHUNKS = 1
+
+
+def one_block_per_table(
+    cells, block_table, row_live, row_train, feat_qkv, feat_out, item_qkv, item_out
+):
+    feat_devices = lax.axis_size("feat")
+    group_rows = cells.shape[0] // feat_devices
+    chunks = [group_rows // CHUNKS] * CHUNKS
+    bias, train_rows, sends = prepare(cells, row_live, row_train, chunks)
+    train_parts = [train_rows] + [swap(train_rows, step) for step in range(1, feat_devices)]
+    row_parts = [
+        [sends[0][at]] + [swap(sends[step][at], step) for step in range(1, feat_devices)]
+        for at in range(len(chunks))
+    ]
+    keys = key_rows(train_parts, feat_qkv, feat_out, item_qkv)
+    results = [
+        own_rows(parts, size, feat_qkv, feat_out, item_qkv, item_out, keys, bias)
+        for parts, size in zip(row_parts, chunks)
+    ]
+    return results[0] if len(results) == 1 else jnp.concatenate(results, axis=0)
+
+
+def layer(cells, block_table, *rest):
+    if block_table.shape[0] == TABLES:
+        return one_block_per_table(cells, block_table, *rest)
+    return on_device(cells, block_table, *rest)
+
+
 def solution(mesh):
     return jax.shard_map(
-        on_device,
+        layer,
         mesh=mesh,
         in_specs=(P("rows", "feat", None), P(), P(), P(), P(), P(), P(), P()),
         out_specs=P(("rows", "feat"), None, None),

time: 323 us -> 54.6 us (0.17); the launches traced: 318 us -> 54.4 us
  matrix products: 111 us -> 0 us
  blocking collectives: 83.7 us -> 0 us
  local copies, waits for them, and re-layouts: 69.6 us -> 4.43 us
  Pallas kernels: 0 us -> 35.2 us
  other arithmetic: 18 us -> 0 us
  starting transfers between devices: 16.1 us -> 5.2 us
  waiting for transfers between devices: 16.6 us -> 9.47 us
    dot_general x89 -> x0, matrix products: 111 us -> none  [the longest x40 62.3 us: one_one_block(): jnp.dot(shares, single_value, preferred_element_type=jnp.float32)]
    psum x2 -> x0, blocking collectives: 40.5 us -> none  [the longest x1 23.4 us: on_device(): lax.psum((table_hot[:, None] * first_local[None, :], table_hot * count_lo...]
    pallas_call x0 -> x3, Pallas kernels: none -> 35.2 us  [the longest x1 24.9 us: own_rows(): pl.pallas_call(functools.partial(row_kernel, rows), out_shape=jax.ShapeDt...]
    unnamed x27 -> x13, local copies, waits for them, and re-layouts: 36.2 us -> 4.43 us
    all_to_all x1 -> x0, blocking collectives: 24 us -> none  [on_device(): lax.all_to_all(result, 'rows', split_axis=0, concat_axis=1, tiled=True)]
    all_gather x2 -> x0, blocking collectives: 19.3 us -> none  [the longest x1 10.2 us: on_device(): every_value = lax.all_gather(local_value, 'feat', axis=0, tiled=True)]
    all_to_all x4 -> x0, waiting for transfers between devices: 16.6 us -> none  [the longest x1 11 us: on_device(): lax.all_to_all(normed, 'feat', split_axis=0, concat_axis=1, tiled=True)]
    all_to_all x4 -> x0, starting transfers between devices: 16.1 us -> none  [the longest x1 5.94 us: on_device(): lax.all_to_all(item_query, 'rows', split_axis=1, concat_axis=0, tiled=True)]
  transfers between devices with their start and end apart: 4 -> 6, of which waited for: 2 -> 2; matrix products, arithmetic and copies ran while one was open for 7% -> 0% of each run, Pallas kernels for 0% -> 13%
where the time goes in v1:
time: 54.6 us; the launch traced here: 54.4 us
  Pallas kernels  35.2 us (64%)
  waiting for transfers between devices  9.47 us (17%)
  starting transfers between devices  5.2 us (10%)
  local copies, waits for them, and re-layouts  4.43 us (8%)
    pallas_call x1, Pallas kernels, own_rows(): pl.pallas_call(functools.partial(row_kernel, rows), out_shape=jax.ShapeDt...  24.9 us
    ppermute x6, waiting for transfers between devices, swap(): lax.ppermute(tensor, 'feat', [(one, one ^ step) for one in range(devices)])  9.47 us
    pallas_call x1, Pallas kernels, key_rows(): pl.pallas_call(functools.partial(key_kernel, rows), out_shape=jax.ShapeDt...  7.22 us
    ppermute x6, starting transfers between devices, swap(): lax.ppermute(tensor, 'feat', [(one, one ^ step) for one in range(devices)])  5.2 us
    unnamed x13, local copies, waits for them, and re-layouts  4.43 us
    pallas_call x1, Pallas kernels, prepare(): pl.pallas_call(functools.partial(prepare_kernel, chunks), out_shape=shape...  3.07 us
  transfers between devices with their start and end apart: 6, of which 2 were waited for; matrix products, arithmetic and copies ran while one was open for 0% of the time, Pallas kernels for 13%

profile of v1, /device:TPU:0, one launch (start us, length us, event | category | flops | bytes accessed | tf_op | source)
XLA Modules:
  0.0 54.4 jit_solution(2997270132597794060)
XLA Ops:
  0.0 2.4 %copy.8.cells_ref = bf16[128,20,128]{2,1,0:T(8,128)(2,1)} copy(bf16[128,20,128]{2,0,1:T(8,128)(2,1)} %param.8) | data formatting | bytes 1310720 | tf_op args[0]
  2.4 3.1 %prepare.1 = (f32[8,128]{1,0:T(8,128)}, bf16[320,128]{1,0:T(8,128)(2,1)}, bf16[640,128]{1,0:T(8,128)(2,1)}, bf16[640,128]{1,0:T(8,128)(2,1)}, bf16[640,128]{1,0:T(8,128)(2,1)}, /*index=5*/bf16[640,128]{1,0:T(8,128)(2,1)}) custom-call(s32[1024]{0:T(1024)} %live_ref.1, s32[1024]{0:T(1024)} %train_ref.1, bf16[128,20,128]{2,1,0:T(8,128)(2,1)} %copy.8.cells_ref), custom_call_target="tpu_custom_call" | custom-call | tf_op jit(solution)/shard_map/prepare/pallas_call | solution.py:249
  5.5 2.4 %collective-permute-start.5 = (bf16[320,128]{1,0:T(8,128)(2,1)}, bf16[320,128]{1,0:T(8,128)(2,1)S(1)}, u32[]{:S(2)}, u32[]{:S(2)}) collective-permute-start(bf16[320,128]{1,0:T(8,128)(2,1)} %get-tuple-element.15.refs_0_), channel_id=1, source_target_pairs={{0,3},{1,2},{2,1},{3,0},{4,7},{5,6},{6,5},{7,4},{8,11},{9,10},{10,... | collective-permute-start | bytes 245768 | tf_op jit(solution)/shard_map/ppermute | solution.py:455
  7.9 0.7 %collective-permute-start = (bf16[640,128]{1,0:T(8,128)(2,1)}, bf16[640,128]{1,0:T(8,128)(2,1)S(1)}, u32[]{:S(2)}, u32[]{:S(2)}) collective-permute-start(bf16[640,128]{1,0:T(8,128)(2,1)} %get-tuple-element.12), channel_id=1, source_target_pairs={{0,1},{1,0},{2,3},{3,2},{4,5},{5,4},{6,7},{7,6},{8,9},{9,8},{10,11... | collective-permute-start | bytes 491528 | tf_op jit(solution)/shard_map/ppermute | solution.py:455
  8.6 0.0 collective-permute-start.1
  8.6 1.4 %collective-permute-start.2 = (bf16[640,128]{1,0:T(8,128)(2,1)}, bf16[640,128]{1,0:T(8,128)(2,1)S(1)}, u32[]{:S(2)}, u32[]{:S(2)}) collective-permute-start(bf16[640,128]{1,0:T(8,128)(2,1)} %get-tuple-element.14), channel_id=1, source_target_pairs={{0,3},{1,2},{2,1},{3,0},{4,7},{5,6},{6,5},{7,4},{8,11},{9,10},{10,... | collective-permute-start | bytes 491528 | tf_op jit(solution)/shard_map/ppermute | solution.py:455
  9.9 0.7 %collective-permute-start.4 = (bf16[320,128]{1,0:T(8,128)(2,1)}, bf16[320,128]{1,0:T(8,128)(2,1)S(1)}, u32[]{:S(2)}, u32[]{:S(2)}) collective-permute-start(bf16[320,128]{1,0:T(8,128)(2,1)} %get-tuple-element.15.refs_0_), channel_id=1, source_target_pairs={{0,2},{1,3},{2,0},{3,1},{4,6},{5,7},{6,4},{7,5},{8,10},{9,11},{10,... | collective-permute-start | bytes 245768 | tf_op jit(solution)/shard_map/ppermute | solution.py:455
  10.6 0.4 collective-permute-done.5.refs_3_
  11.0 0.0 copy-start.3
  11.0 0.1 collective-permute-start.3
  11.1 9.0 %collective-permute-done.4.refs_2_ = bf16[320,128]{1,0:T(8,128)(2,1)S(1)} collective-permute-done((bf16[320,128]{1,0:T(8,128)(2,1)}, bf16[320,128]{1,0:T(8,128)(2,1)S(1)}, u32[]{:S(2)}, u32[]{:S(2)}) %collective-permute-start.4) | collective-permute-done | bytes 81952 | tf_op jit(solution)/shard_map/ppermute | solution.py:455
  20.2 0.0 copy-start.4
  20.2 0.0 collective-permute-done.3.refs_1_
  20.2 0.0 copy-done.3
  20.2 0.6 %copy-done.4 = bf16[320,128]{1,0:T(8,128)(2,1)} copy-done((bf16[320,128]{1,0:T(8,128)(2,1)}, bf16[320,128]{1,0:T(8,128)(2,1)S(1)}, u32[]{:S(2)}) %copy-start.4) | copy-done | bytes 81944
  20.8 0.0 copy-start.5
  20.8 0.6 %copy-done.5 = bf16[320,128]{1,0:T(8,128)(2,1)} copy-done((bf16[320,128]{1,0:T(8,128)(2,1)}, bf16[320,128]{1,0:T(8,128)(2,1)S(1)}, u32[]{:S(2)}) %copy-start.5) | copy-done | bytes 81944
  21.4 7.2 %keys.1.refs_8_ = bf16[80,16,256]{2,1,0:T(8,128)(2,1)} custom-call(bf16[320,128]{1,0:T(8,128)(2,1)} %get-tuple-element.15.refs_0_, bf16[320,128]{1,0:T(8,128)(2,1)} %copy-done.5, bf16[320,128]{1,0:T(8,128)(2,1)} %copy-done.4, bf16[320,128]{1,0:T(8,128)(2,1)} %copy-done.3, bf16[128,384]{1,0:T(8,128)(2,1)} %refs_4_.3, bf16[128,128]{1,0:T(8,128)(2,1)} %refs_5_.3, ...), custom_call_target="tpu_custom_call" | custom-call | tf_op jit(solution)/shard_map/keys/pallas_call | solution.py:366
  28.6 0.0 collective-permute-done.refs_1_
  28.6 0.0 copy-start
  28.6 0.0 collective-permute-done.1.refs_2_
  28.6 0.0 copy-start.1
  28.6 0.0 collective-permute-done.2.refs_3_
  28.7 0.0 copy-start.2
  28.7 0.6 %copy-done = bf16[640,128]{1,0:T(8,128)(2,1)} copy-done((bf16[640,128]{1,0:T(8,128)(2,1)}, bf16[640,128]{1,0:T(8,128)(2,1)S(1)}, u32[]{:S(2)}) %copy-start) | copy-done | bytes 163864
  29.3 0.1 copy-done.1
  29.4 0.1 copy-done.2
  29.4 24.9 %rows.1 = bf16[32,80,128]{2,1,0:T(8,128)(2,1)} custom-call(bf16[640,128]{1,0:T(8,128)(2,1)} %get-tuple-element.11.refs_0_, bf16[640,128]{1,0:T(8,128)(2,1)} %copy-done, bf16[640,128]{1,0:T(8,128)(2,1)} %copy-done.1, bf16[640,128]{1,0:T(8,128)(2,1)} %copy-done.2, bf16[128,384]{1,0:T(8,128)(2,1)} %refs_4_.3, bf16[128,128]{1,0:T(8,128)(2,1)} %refs_5_.3, ...), custom_call_target="tpu_custom_call" | custom-call | tf_op jit(solution)/shard_map/rows/pallas_call | solution.py:437
Async XLA Ops:
  5.5 5.6 %collective-permute-start.5 = (bf16[320,128]{1,0:T(8,128)(2,1)}, bf16[320,128]{1,0:T(8,128)(2,1)S(1)}, u32[]{:S(2)}, u32[]{:S(2)}) collective-permute-start(bf16[320,128]{1,0:T(8,128)(2,1)} %get-tuple-element.15.refs_0_), channel_id=1, source_target_pairs={{0,3},{1,2},{2,1},{3,0},{4,7},{5,6},{6,5},{7,4},{8,11},{9,10},{10,... | collective-permute-start | bytes 245768 | tf_op jit(solution)/shard_map/ppermute | solution.py:455
  7.9 20.7 %collective-permute-start = (bf16[640,128]{1,0:T(8,128)(2,1)}, bf16[640,128]{1,0:T(8,128)(2,1)S(1)}, u32[]{:S(2)}, u32[]{:S(2)}) collective-permute-start(bf16[640,128]{1,0:T(8,128)(2,1)} %get-tuple-element.12), channel_id=1, source_target_pairs={{0,1},{1,0},{2,3},{3,2},{4,5},{5,4},{6,7},{7,6},{8,9},{9,8},{10,11... | collective-permute-start | bytes 491528 | tf_op jit(solution)/shard_map/ppermute | solution.py:455
  8.6 20.1 %collective-permute-start.1 = (bf16[640,128]{1,0:T(8,128)(2,1)}, bf16[640,128]{1,0:T(8,128)(2,1)S(1)}, u32[]{:S(2)}, u32[]{:S(2)}) collective-permute-start(bf16[640,128]{1,0:T(8,128)(2,1)} %get-tuple-element.13), channel_id=1, source_target_pairs={{0,2},{1,3},{2,0},{3,1},{4,6},{5,7},{6,4},{7,5},{8,10},{9,11},{10,... | collective-permute-start | bytes 491528 | tf_op jit(solution)/shard_map/ppermute | solution.py:455
  8.6 20.1 %collective-permute-start.2 = (bf16[640,128]{1,0:T(8,128)(2,1)}, bf16[640,128]{1,0:T(8,128)(2,1)S(1)}, u32[]{:S(2)}, u32[]{:S(2)}) collective-permute-start(bf16[640,128]{1,0:T(8,128)(2,1)} %get-tuple-element.14), channel_id=1, source_target_pairs={{0,3},{1,2},{2,1},{3,0},{4,7},{5,6},{6,5},{7,4},{8,11},{9,10},{10,... | collective-permute-start | bytes 491528 | tf_op jit(solution)/shard_map/ppermute | solution.py:455
  9.9 10.2 %collective-permute-start.4 = (bf16[320,128]{1,0:T(8,128)(2,1)}, bf16[320,128]{1,0:T(8,128)(2,1)S(1)}, u32[]{:S(2)}, u32[]{:S(2)}) collective-permute-start(bf16[320,128]{1,0:T(8,128)(2,1)} %get-tuple-element.15.refs_0_), channel_id=1, source_target_pairs={{0,2},{1,3},{2,0},{3,1},{4,6},{5,7},{6,4},{7,5},{8,10},{9,11},{10,... | collective-permute-start | bytes 245768 | tf_op jit(solution)/shard_map/ppermute | solution.py:455
  11.0 9.1 %copy-start.3 = (bf16[320,128]{1,0:T(8,128)(2,1)}, bf16[320,128]{1,0:T(8,128)(2,1)S(1)}, u32[]{:S(2)}) copy-start(bf16[320,128]{1,0:T(8,128)(2,1)S(1)} %collective-permute-done.5.refs_3_) | copy-start | bytes 245764
  11.0 9.1 %collective-permute-start.3 = (bf16[320,128]{1,0:T(8,128)(2,1)}, bf16[320,128]{1,0:T(8,128)(2,1)S(1)}, u32[]{:S(2)}, u32[]{:S(2)}) collective-permute-start(bf16[320,128]{1,0:T(8,128)(2,1)} %get-tuple-element.15.refs_0_), channel_id=1, source_target_pairs={{0,1},{1,0},{2,3},{3,2},{4,5},{5,4},{6,7},{7,6},{8,9},{9,8},{10,11... | collective-permute-start | bytes 245768 | tf_op jit(solution)/shard_map/ppermute | solution.py:455
  20.2 0.6 %copy-start.4 = (bf16[320,128]{1,0:T(8,128)(2,1)}, bf16[320,128]{1,0:T(8,128)(2,1)S(1)}, u32[]{:S(2)}) copy-start(bf16[320,128]{1,0:T(8,128)(2,1)S(1)} %collective-permute-done.4.refs_2_) | copy-start | bytes 245764
  20.8 0.6 %copy-start.5 = (bf16[320,128]{1,0:T(8,128)(2,1)}, bf16[320,128]{1,0:T(8,128)(2,1)S(1)}, u32[]{:S(2)}) copy-start(bf16[320,128]{1,0:T(8,128)(2,1)S(1)} %collective-permute-done.3.refs_1_) | copy-start | bytes 245764
  28.6 0.7 %copy-start = (bf16[640,128]{1,0:T(8,128)(2,1)}, bf16[640,128]{1,0:T(8,128)(2,1)S(1)}, u32[]{:S(2)}) copy-start(bf16[640,128]{1,0:T(8,128)(2,1)S(1)} %collective-permute-done.refs_1_) | copy-start | bytes 491524
  28.6 0.7 %copy-start.1 = (bf16[640,128]{1,0:T(8,128)(2,1)}, bf16[640,128]{1,0:T(8,128)(2,1)S(1)}, u32[]{:S(2)}) copy-start(bf16[640,128]{1,0:T(8,128)(2,1)S(1)} %collective-permute-done.1.refs_2_) | copy-start | bytes 491524
  28.7 0.8 %copy-start.2 = (bf16[640,128]{1,0:T(8,128)(2,1)}, bf16[640,128]{1,0:T(8,128)(2,1)S(1)}, u32[]{:S(2)}) copy-start(bf16[640,128]{1,0:T(8,128)(2,1)S(1)} %collective-permute-done.2.refs_3_) | copy-start | bytes 491524

commit v2 on v0

--- a/solution.py
+++ b/solution.py
@@ -1,6 +1,11 @@
+import functools
+import math
+
 import jax
 import jax.numpy as jnp
 from jax import lax
+from jax.experimental import pallas as pl
+from jax.experimental.pallas import tpu as pltpu
 from jax.sharding import PartitionSpec as P
 
 HEADS = 4
@@ -11,6 +16,7 @@
 
 EPSILON = 1e-05
 MASKED = -1e30
+SCALE2 = HEAD_DIM ** (-0.5) * math.log2(math.e)
 
 
 def compact_train(train_rows):
@@ -161,9 +167,361 @@
     return (mixed_rows.astype(jnp.float32) + update).astype(jnp.bfloat16)
 
 
+def vmem_kernel(body, shapes, count, scratch, name, limit):
+    many = isinstance(shapes, list)
+    block = pl.BlockSpec(memory_space=pltpu.VMEM)
+    return pl.pallas_call(
+        body,
+        out_shape=shapes,
+        in_specs=[block] * count,
+        out_specs=[block] * len(shapes) if many else block,
+        scratch_shapes=scratch,
+        compiler_params=pltpu.CompilerParams(vmem_limit_bytes=limit << 20),
+        name=name,
+    )
+
+
+def prepare_kernel(chunks, live_ref, train_ref, cells_ref, bias_ref, train_out, *outs):
+    feats_here, rows_here, width = cells_ref.shape
+    feat_devices = lax.axis_size("feat")
+    group_rows = rows_here // feat_devices
+    feat_index = lax.axis_index("feat")
+    row_index = lax.axis_index("rows")
+    keys = train_out.shape[1]
+
+    live = live_ref[pl.ds(row_index, 1), :].astype(jnp.float32)
+    count = jnp.sum(live, axis=1, keepdims=True) * width
+    weight = jnp.transpose(jnp.broadcast_to(live, (width, rows_here)))
+
+    def total(values):
+        return jnp.sum(jnp.sum(values, axis=0, keepdims=True), axis=1, keepdims=True)
+
+    means = []
+    for feat in range(feats_here):
+        values = cells_ref[feat].astype(jnp.float32)
+        means.append(jnp.broadcast_to(total(values * weight) / count, (1, width)))
+    factors = []
+    for feat in range(feats_here):
+        centred = cells_ref[feat].astype(jnp.float32) - means[feat]
+        spread = total(centred * centred * weight) / count
+        factors.append(jnp.broadcast_to(lax.rsqrt(spread + EPSILON), (1, width)))
+
+    train = jnp.broadcast_to(train_ref[pl.ds(row_index, 1), :], (keys, rows_here))
+    before = lax.broadcasted_iota(jnp.int32, (rows_here, rows_here), 0)
+    after = lax.broadcasted_iota(jnp.int32, (rows_here, rows_here), 1)
+    ladder = (before <= after) & (before // group_rows == after // group_rows)
+    ordinal = jnp.dot(
+        train.astype(jnp.float32).astype(jnp.bfloat16),
+        jnp.where(ladder, 1.0, 0.0).astype(jnp.bfloat16),
+        preferred_element_type=jnp.float32,
+    )
+    key = lax.broadcasted_iota(jnp.int32, (keys, rows_here), 0)
+    row = lax.broadcasted_iota(jnp.int32, (keys, rows_here), 1)
+    here = (
+        (train == 1)
+        & (row // group_rows == key // KEEP)
+        & (ordinal == (key % KEEP + 1).astype(jnp.float32))
+    )
+    chosen = jnp.where(here, 1.0, 0.0)
+    found = jnp.sum(chosen, axis=1, keepdims=True)
+    bias_ref[...] = jnp.broadcast_to(jnp.where(found > 0.5, 0.0, MASKED), bias_ref.shape)
+    chosen = chosen.astype(jnp.bfloat16)
+
+    def normed(feat, values):
+        centred = values.astype(jnp.float32) - means[feat]
+        return (centred * factors[feat]).astype(jnp.bfloat16)
+
+    for feat in range(feats_here):
+        train_out[feat] = jnp.dot(
+            chosen, normed(feat, cells_ref[feat]), preferred_element_type=jnp.float32
+        ).astype(jnp.bfloat16)
+    for step in range(feat_devices):
+        done = 0
+        for at, size in enumerate(chunks):
+            first_row = pl.multiple_of((feat_index ^ step) * group_rows + done, 16)
+            for feat in range(feats_here):
+                outs[step * len(chunks) + at][feat] = normed(
+                    feat, cells_ref[feat, pl.ds(first_row, size), :]
+                )
+            done += size
+
+
+def prepare(cells, row_live, row_train, chunks):
+    rows_here, feats_here, width = cells.shape
+    feat_devices = lax.axis_size("feat")
+    keys = feat_devices * KEEP
+    shapes = [
+        jax.ShapeDtypeStruct((keys, 128), jnp.float32),
+        jax.ShapeDtypeStruct((feats_here, keys, width), jnp.bfloat16),
+    ]
+    for _ in range(feat_devices):
+        for size in chunks:
+            shapes.append(jax.ShapeDtypeStruct((feats_here, size, width), jnp.bfloat16))
+    outs = vmem_kernel(
+        functools.partial(prepare_kernel, chunks), shapes, 3, [], "prepare", 8
+    )(
+        row_live.reshape(-1, rows_here),
+        row_train.reshape(-1, rows_here),
+        jnp.transpose(cells, (1, 0, 2)),
+    )
+    sends = [
+        [outs[2 + step * len(chunks) + at] for at in range(len(chunks))]
+        for step in range(feat_devices)
+    ]
+    return outs[0], outs[1], sends
+
+
+def gather_parts(parts, held):
+    feat_index = lax.axis_index("feat")
+    feats_here, rows, width = parts[0].shape
+    size = feats_here * rows
+    for step, part in enumerate(parts):
+        start = pl.multiple_of((feat_index ^ step) * size, size)
+        held[pl.ds(start, size), :] = part[...].reshape(size, width).astype(jnp.float32)
+
+
+def head_masks(rows, width):
+    lane = lax.broadcasted_iota(jnp.int32, (rows, width), 1)
+    return [(lane // HEAD_DIM) == head for head in range(HEADS)]
+
+
+def by_head(tensor, masks):
+    return [jnp.where(mask, tensor, jnp.zeros_like(tensor)) for mask in masks]
+
+
+def attend(queries, keys, values, masks):
+    count, width = queries.shape
+    scores = lax.dot_general(
+        jnp.concatenate(by_head(queries, masks), axis=0),
+        keys,
+        (((1,), (1,)), ((), ())),
+        preferred_element_type=jnp.float32,
+    )
+    top = jnp.max(scores, axis=1, keepdims=True)
+    shares = jnp.exp2((scores - top) * SCALE2).astype(jnp.bfloat16)
+    both = jnp.concatenate([values, jnp.ones_like(values)], axis=1)
+    mixed = jnp.dot(shares, both, preferred_element_type=jnp.float32)
+    out, total = mixed[:count, :width], mixed[:count, width:]
+    for head in range(1, HEADS):
+        block = mixed[head * count : (head + 1) * count]
+        out = jnp.where(masks[head], block[:, :width], out)
+        total = jnp.where(masks[head], block[:, width:], total)
+    return out / total
+
+
+def feature_rows(held, first, rows, stride, qkv_ref, out_ref):
+    feats = held.shape[0] // stride
+    width = held.shape[1]
+    cells = jnp.concatenate(
+        [held[pl.ds(first + row, feats, stride=stride), :] for row in range(rows)], axis=0
+    )
+    projected = jnp.dot(
+        cells.astype(jnp.bfloat16), qkv_ref[...], preferred_element_type=jnp.float32
+    ).astype(jnp.bfloat16)
+    masks = head_masks(feats, width)
+    attended = []
+    for row in range(rows):
+        block = projected[row * feats : (row + 1) * feats]
+        attended.append(
+            attend(
+                block[:, :width],
+                block[:, width : 2 * width],
+                block[:, 2 * width :],
+                masks,
+            ).astype(jnp.bfloat16)
+        )
+    attended = jnp.concatenate(attended, axis=0)
+    update = jnp.dot(attended, out_ref[...], preferred_element_type=jnp.float32)
+    return (cells + update).astype(jnp.bfloat16)
+
+
+STEP = 16
+
+
+def key_kernel(*refs):
+    feat_devices = lax.axis_size("feat")
+    parts = refs[:feat_devices]
+    feat_qkv, feat_out, item_qkv, out_ref, held, key_ref, value_ref = refs[feat_devices:]
+    rows = parts[0].shape[1]
+    feats, width = held.shape[0] // rows, held.shape[1]
+    step_rows = math.gcd(rows, STEP)
+    gather_parts(parts, held)
+
+    def one(step, carry):
+        mixed = feature_rows(held, step * step_rows, step_rows, rows, feat_qkv, feat_out)
+        both = jnp.dot(mixed, item_qkv[:, width:], preferred_element_type=jnp.float32)
+        here = pl.ds(pl.multiple_of(step * (step_rows * feats), step_rows * feats), step_rows * feats)
+        key_ref[here, :] = both[:, :width]
+        value_ref[here, :] = both[:, width:]
+        return carry
+
+    lax.fori_loop(0, rows // step_rows, one, 0)
+    for feat in range(feats):
+        here = pl.ds(feat, rows, stride=feats)
+        out_ref[feat, :, :width] = key_ref[here, :].astype(jnp.bfloat16)
+        out_ref[feat, :, width:] = value_ref[here, :].astype(jnp.bfloat16)
+
+
+def key_rows(parts, feat_qkv, feat_out, item_qkv):
+    feats_here, rows, width = parts[0].shape
+    feats = len(parts) * feats_here
+    table = pltpu.VMEM((rows * feats, width), jnp.float32)
+    return vmem_kernel(
+        key_kernel,
+        jax.ShapeDtypeStruct((feats, rows, 2 * width), jnp.bfloat16),
+        len(parts) + 3,
+        [table, table, table],
+        "keys",
+        24,
+    )(*parts, feat_qkv, feat_out, item_qkv)
+
+
+def row_kernel(*refs):
+    feat_devices = lax.axis_size("feat")
+    parts = refs[:feat_devices]
+    (feat_qkv, feat_out, item_qkv, item_out, keys_ref, bias_ref, out_ref) = refs[
+        feat_devices : feat_devices + 7
+    ]
+    held, mixed_ref, query_ref, item_ref = refs[feat_devices + 7 :]
+    rows = parts[0].shape[1]
+    feats, width = held.shape[0] // rows, held.shape[1]
+    step_rows = math.gcd(rows, STEP)
+    keys = keys_ref.shape[1]
+    gather_parts(parts, held)
+
+    def span(step):
+        return pl.ds(pl.multiple_of(step * (step_rows * feats), step_rows * feats), step_rows * feats)
+
+    def one(step, carry):
+        mixed = feature_rows(held, step * step_rows, step_rows, rows, feat_qkv, feat_out)
+        mixed_ref[span(step), :] = mixed
+        query_ref[span(step), :] = jnp.dot(
+            mixed, item_qkv[:, :width], preferred_element_type=jnp.float32
+        )
+        return carry
+
+    lax.fori_loop(0, rows // step_rows, one, 0)
+
+    together = 128 // rows
+    lanes = together * rows
+    pairs = together // 2
+    key_masks = head_masks(keys, width)
+    bias = jnp.concatenate([bias_ref[:, :lanes]] * HEADS, axis=0)
+    lane_owner = lax.broadcasted_iota(jnp.int32, (HEADS * keys, lanes), 1) // rows
+    pair_row = lax.broadcasted_iota(jnp.int32, (2 * rows, 2 * HEADS * keys), 0) // rows
+    pair_lane = lax.broadcasted_iota(jnp.int32, (2 * rows, 2 * HEADS * keys), 1) // (HEADS * keys)
+    pair_mask = pair_row == pair_lane
+
+    def item(step):
+        queries, stacked_keys, stacked_values = [], [], []
+        for inner in range(together):
+            feat = step * together + inner
+            queries.append(query_ref[pl.ds(feat, rows, stride=feats), :].astype(jnp.bfloat16))
+            stacked_keys += by_head(keys_ref[feat, :, :width], key_masks)
+            stacked_values += by_head(keys_ref[feat, :, width:], key_masks)
+        every = lax.dot_general(
+            jnp.concatenate(stacked_keys, axis=0),
+            jnp.concatenate(queries, axis=0),
+            (((1,), (1,)), ((), ())),
+            preferred_element_type=jnp.float32,
+        )
+        size = HEADS * keys
+        scores = every[:size]
+        for inner in range(1, together):
+            scores = jnp.where(lane_owner == inner, every[inner * size : (inner + 1) * size], scores)
+        scores = (scores + bias).reshape(HEADS, keys, lanes)
+        top = jnp.max(scores, axis=1, keepdims=True)
+        powers = jnp.exp2((scores - top) * SCALE2)
+        shares = powers / jnp.sum(powers, axis=1, keepdims=True)
+        shares = shares.reshape(size, lanes)
+        shares = jnp.transpose(jnp.concatenate([shares, shares], axis=0)).astype(jnp.bfloat16)
+        for pair in range(pairs):
+            block = shares[pair * 2 * rows : (pair + 1) * 2 * rows]
+            result = jnp.dot(
+                jnp.where(pair_mask, block, jnp.zeros_like(block)),
+                jnp.concatenate(
+                    stacked_values[pair * 2 * HEADS : (pair + 1) * 2 * HEADS], axis=0
+                ),
+                preferred_element_type=jnp.float32,
+            )
+            for inner in range(2):
+                feat = step * together + pair * 2 + inner
+                item_ref[pl.ds(feat, rows, stride=feats), :] = result[
+                    inner * rows : (inner + 1) * rows
+                ]
+
+    def items(step, carry):
+        for inner in range(ITEM_STEP):
+            item(step * ITEM_STEP + inner)
+        return carry
+
+    lax.fori_loop(0, feats // (together * ITEM_STEP), items, 0)
+
+    def last(step, carry):
+        attended = item_ref[span(step), :].astype(jnp.bfloat16)
+        update = jnp.dot(attended, item_out[...], preferred_element_type=jnp.float32)
+        result = (mixed_ref[span(step), :].astype(jnp.float32) + update).astype(jnp.bfloat16)
+        for row in range(step_rows):
+            out_ref[step * step_rows + row] = result[row * feats : (row + 1) * feats]
+        return carry
+
+    lax.fori_loop(0, rows // step_rows, last, 0)
+
+
+ITEM_STEP = 4
+
+
+def own_rows(parts, feat_qkv, feat_out, item_qkv, item_out, keys, bias):
+    feats_here, rows, width = parts[0].shape
+    feats = len(parts) * feats_here
+    table = pltpu.VMEM((rows * feats, width), jnp.float32)
+    return vmem_kernel(
+        row_kernel,
+        jax.ShapeDtypeStruct((rows, feats, width), jnp.bfloat16),
+        len(parts) + 6,
+        [table, pltpu.VMEM((rows * feats, width), jnp.bfloat16), table, table],
+        "rows",
+        24,
+    )(*parts, feat_qkv, feat_out, item_qkv, item_out, keys, bias)
+
+
+def swap(tensor, step):
+    devices = lax.axis_size("feat")
+    return lax.ppermute(tensor, "feat", [(one, one ^ step) for one in range(devices)])
+
+
+CHUNKS = 1
+
+
+def one_block_per_table(
+    cells, block_table, row_live, row_train, feat_qkv, feat_out, item_qkv, item_out
+):
+    feat_devices = lax.axis_size("feat")
+    group_rows = cells.shape[0] // feat_devices
+    chunks = [group_rows // CHUNKS] * CHUNKS
+    bias, train_rows, sends = prepare(cells, row_live, row_train, chunks)
+    train_parts = [train_rows] + [swap(train_rows, step) for step in range(1, feat_devices)]
+    row_parts = [
+        [sends[0][at]] + [swap(sends[step][at], step) for step in range(1, feat_devices)]
+        for at in range(len(chunks))
+    ]
+    keys = key_rows(train_parts, feat_qkv, feat_out, item_qkv)
+    results = [
+        own_rows(parts, feat_qkv, feat_out, item_qkv, item_out, keys, bias)
+        for parts in row_parts
+    ]
+    return results[0] if len(results) == 1 else jnp.concatenate(results, axis=0)
+
+
+def layer(cells, block_table, *rest):
+    if block_table.shape[0] == TABLES:
+        return one_block_per_table(cells, block_table, *rest)
+    return on_device(cells, block_table, *rest)
+
+
 def solution(mesh):
     return jax.shard_map(
-        on_device,
+        layer,
         mesh=mesh,
         in_specs=(P("rows", "feat", None), P(), P(), P(), P(), P(), P(), P()),
         out_specs=P(("rows", "feat"), None, None),

time: 323 us -> 33.3 us (0.10); the launches traced: 318 us -> 33.1 us
  matrix products: 111 us -> 0 us
  blocking collectives: 83.7 us -> 0 us
  local copies, waits for them, and re-layouts: 69.6 us -> 2.47 us
  other arithmetic: 18 us -> 0 us
  Pallas kernels: 0 us -> 16 us
  starting transfers between devices: 16.1 us -> 5.23 us
  waiting for transfers between devices: 16.6 us -> 9.26 us
    dot_general x89 -> x0, matrix products: 111 us -> none  [the longest x40 62.3 us: one_one_block(): jnp.dot(shares, single_value, preferred_element_type=jnp.float32)]
    psum x2 -> x0, blocking collectives: 40.5 us -> none  [the longest x1 23.4 us: on_device(): lax.psum((table_hot[:, None] * first_local[None, :], table_hot * count_lo...]
    unnamed x27 -> x14, local copies, waits for them, and re-layouts: 36.2 us -> 2.47 us
    all_to_all x1 -> x0, blocking collectives: 24 us -> none  [on_device(): lax.all_to_all(result, 'rows', split_axis=0, concat_axis=1, tiled=True)]
    all_gather x2 -> x0, blocking collectives: 19.3 us -> none  [the longest x1 10.2 us: on_device(): every_value = lax.all_gather(local_value, 'feat', axis=0, tiled=True)]
    all_to_all x4 -> x0, waiting for transfers between devices: 16.6 us -> none  [the longest x1 11 us: on_device(): lax.all_to_all(normed, 'feat', split_axis=0, concat_axis=1, tiled=True)]
    all_to_all x4 -> x0, starting transfers between devices: 16.1 us -> none  [the longest x1 5.94 us: on_device(): lax.all_to_all(item_query, 'rows', split_axis=1, concat_axis=0, tiled=True)]
    pallas_call x0 -> x3, Pallas kernels: none -> 16 us  [the longest x1 11.3 us: own_rows(): vmem_kernel(row_kernel, jax.ShapeDtypeStruct((rows, feats, width), jnp.bf...]
  transfers between devices with their start and end apart: 4 -> 6, of which waited for: 2 -> 2; matrix products, arithmetic and copies ran while one was open for 7% -> 0% of each run, Pallas kernels for 0% -> 12%
where the time goes in v2:
time: 33.3 us; the launch traced here: 33.1 us
  Pallas kernels  16 us (48%)
  waiting for transfers between devices  9.26 us (28%)
  starting transfers between devices  5.23 us (16%)
  local copies, waits for them, and re-layouts  2.47 us (7%)
    pallas_call x1, Pallas kernels, own_rows(): vmem_kernel(row_kernel, jax.ShapeDtypeStruct((rows, feats, width), jnp.bf...  11.3 us
    ppermute x6, waiting for transfers between devices, swap(): lax.ppermute(tensor, 'feat', [(one, one ^ step) for one in range(devices)])  9.26 us
    ppermute x6, starting transfers between devices, swap(): lax.ppermute(tensor, 'feat', [(one, one ^ step) for one in range(devices)])  5.23 us
    pallas_call x1, Pallas kernels, key_rows(): vmem_kernel(key_kernel, jax.ShapeDtypeStruct((feats, rows, 2 * width), jn...  3.86 us
    unnamed x14, local copies, waits for them, and re-layouts  2.47 us
    pallas_call x1, Pallas kernels, prepare(): vmem_kernel(functools.partial(prepare_kernel, chunks), shapes, 3, [], 'pr...  0.92 us
  transfers between devices with their start and end apart: 6, of which 2 were waited for; matrix products, arithmetic and copies ran while one was open for 0% of the time, Pallas kernels for 12%

profile of v2, /device:TPU:0, one launch (start us, length us, event | category | flops | bytes accessed | tf_op | source)
XLA Modules:
  0.0 33.1 jit_solution(1774197764221881838)
XLA Ops:
  0.0 0.0 copy-start.5
  0.0 0.7 %copy-done.5 = s32[1024]{0:T(1024)S(1)} copy-done((s32[1024]{0:T(1024)S(1)}, s32[1024]{0:T(1024)}, u32[]{:S(2)}) %copy-start.5) | copy-done | bytes 4120
  0.7 0.0 copy-start
  0.7 1.1 %copy-done = bf16[128,20,128]{2,0,1:T(8,128)(2,1)S(1)} copy-done((bf16[128,20,128]{2,0,1:T(8,128)(2,1)S(1)}, bf16[128,20,128]{2,0,1:T(8,128)(2,1)}, u32[]{:S(2)}) %copy-start) | copy-done | bytes 655384
  1.8 0.0 copy-start.6
  1.8 0.7 %copy-done.6 = s32[1024]{0:T(1024)S(1)} copy-done((s32[1024]{0:T(1024)S(1)}, s32[1024]{0:T(1024)}, u32[]{:S(2)}) %copy-start.6) | copy-done | bytes 4120
  2.5 0.0 copy-start.1
  2.5 0.0 copy-start.2
  2.5 0.0 copy-start.3
  2.5 0.9 %prepare.1 = (f32[16,128]{1,0:T(8,128)S(1)}, bf16[20,16,128]{2,1,0:T(8,128)(2,1)S(1)}, bf16[20,32,128]{2,1,0:T(8,128)(2,1)S(1)}, bf16[20,32,128]{2,1,0:T(8,128)(...) custom-call(s32[8,128]{1,0:T(8,128)S(1)} %bitcast.4, s32[8,128]{1,0:T(8,128)S(1)} %bitcast.5, ...), custom_call_target="tpu_custom_call" | custom-call | tf_op jit(solution)/shard_map/prepare/pallas_call | solution.py:260
  3.4 2.4 %collective-permute-start.5 = (bf16[20,16,128]{2,1,0:T(8,128)(2,1)S(1)}, bf16[20,16,128]{2,1,0:T(8,128)(2,1)S(1)}, u32[]{:S(2)}, u32[]{:S(2)}) collective-permute-start(bf16[20,16,128]{2,1,0:T(8,128)(2,1)S(1)} %get-tuple-element.15.refs_0_), channel_id=1, source_target_pairs={{0,3},{1,2},{2,1},{3,0},{4,7},{5,6},{6,5},{7,4},{8,11},{9,10},{10,... | collective-permute-start | bytes 245768 | tf_op jit(solution)/shard_map/ppermute | solution.py:490
  5.8 0.7 %collective-permute-start = (bf16[20,32,128]{2,1,0:T(8,128)(2,1)S(1)}, bf16[20,32,128]{2,1,0:T(8,128)(2,1)S(1)}, u32[]{:S(2)}, u32[]{:S(2)}) collective-permute-start(bf16[20,32,128]{2,1,0:T(8,128)(2,1)S(1)} %get-tuple-element.12), channel_id=1, source_target_pairs={{0,1},{1,0},{2,3},{3,2},{4,5},{5,4},{6,7},{7,6},{8,9},{9,8},{10,11... | collective-permute-start | bytes 491528 | tf_op jit(solution)/shard_map/ppermute | solution.py:490
  6.5 0.0 collective-permute-start.1
  6.5 0.0 copy-start.4
  6.5 1.3 %collective-permute-start.2 = (bf16[20,32,128]{2,1,0:T(8,128)(2,1)S(1)}, bf16[20,32,128]{2,1,0:T(8,128)(2,1)S(1)}, u32[]{:S(2)}, u32[]{:S(2)}) collective-permute-start(bf16[20,32,128]{2,1,0:T(8,128)(2,1)S(1)} %get-tuple-element.14), channel_id=1, source_target_pairs={{0,3},{1,2},{2,1},{3,0},{4,7},{5,6},{6,5},{7,4},{8,11},{9,10},{10,... | collective-permute-start | bytes 491528 | tf_op jit(solution)/shard_map/ppermute | solution.py:490
  7.9 0.7 %collective-permute-start.4 = (bf16[20,16,128]{2,1,0:T(8,128)(2,1)S(1)}, bf16[20,16,128]{2,1,0:T(8,128)(2,1)S(1)}, u32[]{:S(2)}, u32[]{:S(2)}) collective-permute-start(bf16[20,16,128]{2,1,0:T(8,128)(2,1)S(1)} %get-tuple-element.15.refs_0_), channel_id=1, source_target_pairs={{0,2},{1,3},{2,0},{3,1},{4,6},{5,7},{6,4},{7,5},{8,10},{9,11},{10,... | collective-permute-start | bytes 245768 | tf_op jit(solution)/shard_map/ppermute | solution.py:490
  8.5 0.1 collective-permute-done.5.refs_3_
  8.7 0.1 collective-permute-start.3
  8.7 9.1 %collective-permute-done.4.refs_2_ = bf16[20,16,128]{2,1,0:T(8,128)(2,1)S(1)} collective-permute-done((bf16[20,16,128]{2,1,0:T(8,128)(2,1)S(1)}, bf16[20,16,128]{2,1,0:T(8,128)(2,1)S(1)}, u32[]{:S(2)}, u32[]{:S(2)}) %collective-permute-start.4) | collective-permute-done | bytes 81952 | tf_op jit(solution)/shard_map/ppermute | solution.py:490
  17.9 0.0 collective-permute-done.3.refs_1_
  17.9 0.0 copy-done.1
  17.9 0.0 copy-done.2
  17.9 0.0 copy-done.3
  17.9 3.9 %keys.1.refs_8_ = bf16[80,16,256]{2,1,0:T(8,128)(2,1)S(1)} custom-call(bf16[20,16,128]{2,1,0:T(8,128)(2,1)S(1)} %get-tuple-element.15.refs_0_, bf16[20,16,128]{2,1,0:T(8,128)(2,1)S(1)} %collective-permute-done.3.refs_1_, bf16[20,16,128]{2,1,0:T(8,128)(2,1)S(1)} %collective-permute-done.4.refs_2_, bf16[20,16,128]{2,1,0:T(8,128)(2,1)S(1)} %collective-permute-done.5.refs_3_, ...), custom_call_target="tpu_custom_call" | custom-call | tf_op jit(solution)/shard_map/keys/pallas_call | solution.py:369
  21.8 0.0 collective-permute-done.refs_1_
  21.8 0.0 collective-permute-done.1.refs_2_
  21.8 0.0 collective-permute-done.2.refs_3_
  21.8 0.0 copy-done.4
  21.8 11.3 %rows.1 = bf16[32,80,128]{2,1,0:T(8,128)(2,1)} custom-call(bf16[20,32,128]{2,1,0:T(8,128)(2,1)S(1)} %get-tuple-element.11.refs_0_, bf16[20,32,128]{2,1,0:T(8,128)(2,1)S(1)} %collective-permute-done.refs_1_, bf16[20,32,128]{2,1,0:T(8,128)(2,1)S(1)} %collective-permute-done.1.refs_2_, bf16[20,32,128]{2,1,0:T(8,128)(2,1)S(1)} %collective-permute-done.2.refs_3_, ...), custom_call_target="tpu_custom_call" | custom-call | tf_op jit(solution)/shard_map/rows/pallas_call | solution.py:478
Async XLA Ops:
  0.0 0.7 %copy-start.5 = (s32[1024]{0:T(1024)S(1)}, s32[1024]{0:T(1024)}, u32[]{:S(2)}) copy-start(s32[1024]{0:T(1024)} %param.9) | copy-start | bytes 12292
  0.7 1.1 %copy-start = (bf16[128,20,128]{2,0,1:T(8,128)(2,1)S(1)}, bf16[128,20,128]{2,0,1:T(8,128)(2,1)}, u32[]{:S(2)}) copy-start(bf16[128,20,128]{2,0,1:T(8,128)(2,1)} %param.8) | copy-start | bytes 1966084
  1.8 0.7 %copy-start.6 = (s32[1024]{0:T(1024)S(1)}, s32[1024]{0:T(1024)}, u32[]{:S(2)}) copy-start(s32[1024]{0:T(1024)} %param.10) | copy-start | bytes 12292
  2.5 15.4 %copy-start.1 = (bf16[128,384]{1,0:T(8,128)(2,1)S(1)}, bf16[128,384]{1,0:T(8,128)(2,1)}, u32[]{:S(2)}) copy-start(bf16[128,384]{1,0:T(8,128)(2,1)} %refs_4_.3) | copy-start | bytes 294916
  2.5 15.4 %copy-start.2 = (bf16[128,384]{1,0:T(8,128)(2,1)S(1)}, bf16[128,384]{1,0:T(8,128)(2,1)}, u32[]{:S(2)}) copy-start(bf16[128,384]{1,0:T(8,128)(2,1)} %refs_6_.3) | copy-start | bytes 294916
  2.5 15.4 %copy-start.3 = (bf16[128,128]{1,0:T(8,128)(2,1)S(1)}, bf16[128,128]{1,0:T(8,128)(2,1)}, u32[]{:S(2)}) copy-start(bf16[128,128]{1,0:T(8,128)(2,1)} %refs_5_.3) | copy-start | bytes 98308
  3.4 5.3 %collective-permute-start.5 = (bf16[20,16,128]{2,1,0:T(8,128)(2,1)S(1)}, bf16[20,16,128]{2,1,0:T(8,128)(2,1)S(1)}, u32[]{:S(2)}, u32[]{:S(2)}) collective-permute-start(bf16[20,16,128]{2,1,0:T(8,128)(2,1)S(1)} %get-tuple-element.15.refs_0_), channel_id=1, source_target_pairs={{0,3},{1,2},{2,1},{3,0},{4,7},{5,6},{6,5},{7,4},{8,11},{9,10},{10,... | collective-permute-start | bytes 245768 | tf_op jit(solution)/shard_map/ppermute | solution.py:490
  5.8 15.9 %collective-permute-start = (bf16[20,32,128]{2,1,0:T(8,128)(2,1)S(1)}, bf16[20,32,128]{2,1,0:T(8,128)(2,1)S(1)}, u32[]{:S(2)}, u32[]{:S(2)}) collective-permute-start(bf16[20,32,128]{2,1,0:T(8,128)(2,1)S(1)} %get-tuple-element.12), channel_id=1, source_target_pairs={{0,1},{1,0},{2,3},{3,2},{4,5},{5,4},{6,7},{7,6},{8,9},{9,8},{10,11... | collective-permute-start | bytes 491528 | tf_op jit(solution)/shard_map/ppermute | solution.py:490
  6.5 15.3 %collective-permute-start.1 = (bf16[20,32,128]{2,1,0:T(8,128)(2,1)S(1)}, bf16[20,32,128]{2,1,0:T(8,128)(2,1)S(1)}, u32[]{:S(2)}, u32[]{:S(2)}) collective-permute-start(bf16[20,32,128]{2,1,0:T(8,128)(2,1)S(1)} %get-tuple-element.13), channel_id=1, source_target_pairs={{0,2},{1,3},{2,0},{3,1},{4,6},{5,7},{6,4},{7,5},{8,10},{9,11},{10,... | collective-permute-start | bytes 491528 | tf_op jit(solution)/shard_map/ppermute | solution.py:490
  6.5 15.3 %copy-start.4 = (bf16[128,128]{1,0:T(8,128)(2,1)S(1)}, bf16[128,128]{1,0:T(8,128)(2,1)}, u32[]{:S(2)}) copy-start(bf16[128,128]{1,0:T(8,128)(2,1)} %refs_7_.1) | copy-start | bytes 98308
  6.5 15.2 %collective-permute-start.2 = (bf16[20,32,128]{2,1,0:T(8,128)(2,1)S(1)}, bf16[20,32,128]{2,1,0:T(8,128)(2,1)S(1)}, u32[]{:S(2)}, u32[]{:S(2)}) collective-permute-start(bf16[20,32,128]{2,1,0:T(8,128)(2,1)S(1)} %get-tuple-element.14), channel_id=1, source_target_pairs={{0,3},{1,2},{2,1},{3,0},{4,7},{5,6},{6,5},{7,4},{8,11},{9,10},{10,... | collective-permute-start | bytes 491528 | tf_op jit(solution)/shard_map/ppermute | solution.py:490
  7.9 10.0 %collective-permute-start.4 = (bf16[20,16,128]{2,1,0:T(8,128)(2,1)S(1)}, bf16[20,16,128]{2,1,0:T(8,128)(2,1)S(1)}, u32[]{:S(2)}, u32[]{:S(2)}) collective-permute-start(bf16[20,16,128]{2,1,0:T(8,128)(2,1)S(1)} %get-tuple-element.15.refs_0_), channel_id=1, source_target_pairs={{0,2},{1,3},{2,0},{3,1},{4,6},{5,7},{6,4},{7,5},{8,10},{9,11},{10,... | collective-permute-start | bytes 245768 | tf_op jit(solution)/shard_map/ppermute | solution.py:490
  8.7 9.2 %collective-permute-start.3 = (bf16[20,16,128]{2,1,0:T(8,128)(2,1)S(1)}, bf16[20,16,128]{2,1,0:T(8,128)(2,1)S(1)}, u32[]{:S(2)}, u32[]{:S(2)}) collective-permute-start(bf16[20,16,128]{2,1,0:T(8,128)(2,1)S(1)} %get-tuple-element.15.refs_0_), channel_id=1, source_target_pairs={{0,1},{1,0},{2,3},{3,2},{4,5},{5,4},{6,7},{7,6},{8,9},{9,8},{10,11... | collective-permute-start | bytes 245768 | tf_op jit(solution)/shard_map/ppermute | solution.py:490

commit v3 on v2

--- a/solution.py
+++ b/solution.py
@@ -67,7 +67,7 @@
 
 
 def on_device(cells, block_table, row_live, row_train, feat_qkv, feat_out, item_qkv, item_out):
-    rows_here, feats_here, width_all = cells.shape
+    rows_here, _, width_all = cells.shape
     row_index = lax.axis_index("rows")
     feat_index = lax.axis_index("feat")
     row_devices = lax.axis_size("rows")
@@ -167,7 +167,7 @@
     return (mixed_rows.astype(jnp.float32) + update).astype(jnp.bfloat16)
 
 
-def vmem_kernel(body, shapes, count, scratch, name, limit):
+def vmem_kernel(body, shapes, count, scratch, limit):
     many = isinstance(shapes, list)
     block = pl.BlockSpec(memory_space=pltpu.VMEM)
     return pl.pallas_call(
@@ -177,17 +177,35 @@
         out_specs=[block] * len(shapes) if many else block,
         scratch_shapes=scratch,
         compiler_params=pltpu.CompilerParams(vmem_limit_bytes=limit << 20),
-        name=name,
-    )
-
-
-def prepare_kernel(chunks, live_ref, train_ref, cells_ref, bias_ref, train_out, *outs):
+    )
+
+
+PIECES = 4
+
+
+def prepare_kernel(chunks, live_in, train_in, cells_in, bias_ref, train_out, *refs):
+    outs, (live_ref, train_ref, cells_ref, sems) = refs[:-4], refs[-4:]
     feats_here, rows_here, width = cells_ref.shape
     feat_devices = lax.axis_size("feat")
     group_rows = rows_here // feat_devices
     feat_index = lax.axis_index("feat")
     row_index = lax.axis_index("rows")
     keys = train_out.shape[1]
+    piece = feats_here // math.gcd(feats_here, PIECES)
+
+    copies = [
+        pltpu.make_async_copy(live_in, live_ref, sems.at[0]),
+        pltpu.make_async_copy(train_in, train_ref, sems.at[1]),
+    ]
+    for at, feat in enumerate(range(0, feats_here, piece)):
+        here = pl.ds(feat, piece)
+        copies.append(
+            pltpu.make_async_copy(cells_in.at[here], cells_ref.at[here], sems.at[2 + at])
+        )
+    for copy in copies:
+        copy.start()
+    for copy in copies[:2]:
+        copy.wait()
 
     live = live_ref[pl.ds(row_index, 1), :].astype(jnp.float32)
     count = jnp.sum(live, axis=1, keepdims=True) * width
@@ -198,6 +216,8 @@
 
     means = []
     for feat in range(feats_here):
+        if feat % piece == 0:
+            copies[2 + feat // piece].wait()
         values = cells_ref[feat].astype(jnp.float32)
         means.append(jnp.broadcast_to(total(values * weight) / count, (1, width)))
     factors = []
@@ -231,19 +251,23 @@
         centred = values.astype(jnp.float32) - means[feat]
         return (centred * factors[feat]).astype(jnp.bfloat16)
 
+    near_out = outs[0]
     for feat in range(feats_here):
-        train_out[feat] = jnp.dot(
+        rows = jnp.dot(
             chosen, normed(feat, cells_ref[feat]), preferred_element_type=jnp.float32
         ).astype(jnp.bfloat16)
+        train_out[feat] = rows
+        near_out[0, feat] = rows
     for step in range(feat_devices):
-        done = 0
-        for at, size in enumerate(chunks):
-            first_row = pl.multiple_of((feat_index ^ step) * group_rows + done, 16)
+        for at in range(chunks):
+            size = group_rows // chunks
+            first_row = pl.multiple_of((feat_index ^ step) * group_rows + at * size, size)
             for feat in range(feats_here):
-                outs[step * len(chunks) + at][feat] = normed(
-                    feat, cells_ref[feat, pl.ds(first_row, size), :]
-                )
-            done += size
+                rows = normed(feat, cells_ref[feat, pl.ds(first_row, size), :])
+                if step == 1:
+                    near_out[1 + at, feat] = rows
+                else:
+                    outs[1 + max(step - 1, 0) * chunks + at][feat] = rows
 
 
 def prepare(cells, row_live, row_train, chunks):
@@ -254,30 +278,46 @@
         jax.ShapeDtypeStruct((keys, 128), jnp.float32),
         jax.ShapeDtypeStruct((feats_here, keys, width), jnp.bfloat16),
     ]
-    for _ in range(feat_devices):
-        for size in chunks:
-            shapes.append(jax.ShapeDtypeStruct((feats_here, size, width), jnp.bfloat16))
-    outs = vmem_kernel(
-        functools.partial(prepare_kernel, chunks), shapes, 3, [], "prepare", 8
+    size = rows_here // feat_devices // chunks
+    assert size == keys
+    part = jax.ShapeDtypeStruct((feats_here, size, width), jnp.bfloat16)
+    shapes.append(jax.ShapeDtypeStruct((1 + chunks,) + part.shape, jnp.bfloat16))
+    shapes += [part] * ((feat_devices - 1) * chunks)
+    blocks = row_live.shape[0] // rows_here
+    block = pl.BlockSpec(memory_space=pltpu.VMEM)
+    outs = pl.pallas_call(
+        functools.partial(prepare_kernel, chunks),
+        out_shape=shapes,
+        in_specs=[pl.BlockSpec(memory_space=pltpu.HBM)] * 3,
+        out_specs=[block] * len(shapes),
+        scratch_shapes=[
+            pltpu.VMEM((blocks, rows_here), jnp.int32),
+            pltpu.VMEM((blocks, rows_here), jnp.int32),
+            pltpu.VMEM((feats_here, rows_here, width), jnp.bfloat16),
+            pltpu.SemaphoreType.DMA((2 + math.gcd(feats_here, PIECES),)),
+        ],
+        compiler_params=pltpu.CompilerParams(vmem_limit_bytes=8 << 20),
+        name="prepare",
     )(
-        row_live.reshape(-1, rows_here),
-        row_train.reshape(-1, rows_here),
-        jnp.transpose(cells, (1, 0, 2)),
-    )
-    sends = [
-        [outs[2 + step * len(chunks) + at] for at in range(len(chunks))]
-        for step in range(feat_devices)
-    ]
-    return outs[0], outs[1], sends
-
-
-def gather_parts(parts, held):
+        pltpu.with_memory_space_constraint(row_live.reshape(-1, rows_here), pltpu.HBM),
+        pltpu.with_memory_space_constraint(row_train.reshape(-1, rows_here), pltpu.HBM),
+        pltpu.with_memory_space_constraint(jnp.transpose(cells, (1, 0, 2)), pltpu.HBM),
+    )
+    sends = {
+        step: outs[3 + at * chunks : 3 + (at + 1) * chunks]
+        for at, step in enumerate([0, *range(2, feat_devices)])
+    }
+    return outs[0], outs[1], outs[2], sends
+
+
+def gather_parts(parts, at, held):
     feat_index = lax.axis_index("feat")
     feats_here, rows, width = parts[0].shape
     size = feats_here * rows
     for step, part in enumerate(parts):
         start = pl.multiple_of((feat_index ^ step) * size, size)
-        held[pl.ds(start, size), :] = part[...].reshape(size, width).astype(jnp.float32)
+        values = part[at] if step == 1 else part[...]
+        held[pl.ds(start, size), :] = values.reshape(size, width).astype(jnp.float32)
 
 
 def head_masks(rows, width):
@@ -291,6 +331,7 @@
 
 def attend(queries, keys, values, masks):
     count, width = queries.shape
+    half = width // 2
     scores = lax.dot_general(
         jnp.concatenate(by_head(queries, masks), axis=0),
         keys,
@@ -299,13 +340,24 @@
     )
     top = jnp.max(scores, axis=1, keepdims=True)
     shares = jnp.exp2((scores - top) * SCALE2).astype(jnp.bfloat16)
-    both = jnp.concatenate([values, jnp.ones_like(values)], axis=1)
-    mixed = jnp.dot(shares, both, preferred_element_type=jnp.float32)
-    out, total = mixed[:count, :width], mixed[:count, width:]
-    for head in range(1, HEADS):
-        block = mixed[head * count : (head + 1) * count]
-        out = jnp.where(masks[head], block[:, :width], out)
-        total = jnp.where(masks[head], block[:, width:], total)
+    lane = lax.broadcasted_iota(jnp.int32, (count, width), 1)
+    low, ones = lane < half, jnp.ones_like(values)
+    sides = []
+    for side in range(2):
+        first = side * (HEADS // 2)
+        both = jnp.where(low, values, ones) if side == 0 else jnp.where(low, ones, values)
+        mixed = jnp.dot(
+            shares[first * count : (first + HEADS // 2) * count],
+            both,
+            preferred_element_type=jnp.float32,
+        )
+        picked = mixed[:count]
+        for head in range(1, HEADS // 2):
+            mine = (lane % half) // HEAD_DIM == head
+            picked = jnp.where(mine, mixed[head * count : (head + 1) * count], picked)
+        sides.append(picked)
+    out = jnp.where(low, sides[0], sides[1])
+    total = pltpu.roll(jnp.where(low, sides[1], sides[0]), half, 1)
     return out / total
 
 
@@ -345,7 +397,7 @@
     rows = parts[0].shape[1]
     feats, width = held.shape[0] // rows, held.shape[1]
     step_rows = math.gcd(rows, STEP)
-    gather_parts(parts, held)
+    gather_parts(parts, 0, held)
 
     def one(step, carry):
         mixed = feature_rows(held, step * step_rows, step_rows, rows, feat_qkv, feat_out)
@@ -371,23 +423,24 @@
         jax.ShapeDtypeStruct((feats, rows, 2 * width), jnp.bfloat16),
         len(parts) + 3,
         [table, table, table],
-        "keys",
         24,
     )(*parts, feat_qkv, feat_out, item_qkv)
 
 
-def row_kernel(*refs):
+def row_kernel(first_row, aliased, *refs):
     feat_devices = lax.axis_size("feat")
     parts = refs[:feat_devices]
-    (feat_qkv, feat_out, item_qkv, item_out, keys_ref, bias_ref, out_ref) = refs[
-        feat_devices : feat_devices + 7
+    (feat_qkv, feat_out, item_qkv, item_out, keys_ref, bias_ref) = refs[
+        feat_devices : feat_devices + 6
     ]
-    held, mixed_ref, query_ref, item_ref = refs[feat_devices + 7 :]
+    out_ref, held, mixed_ref, query_ref, item_ref, result_ref, sem = refs[
+        feat_devices + 6 + aliased :
+    ]
     rows = parts[0].shape[1]
     feats, width = held.shape[0] // rows, held.shape[1]
     step_rows = math.gcd(rows, STEP)
     keys = keys_ref.shape[1]
-    gather_parts(parts, held)
+    gather_parts(parts, 1 + first_row // parts[0].shape[1], held)
 
     def span(step):
         return pl.ds(pl.multiple_of(step * (step_rows * feats), step_rows * feats), step_rows * feats)
@@ -462,27 +515,42 @@
         update = jnp.dot(attended, item_out[...], preferred_element_type=jnp.float32)
         result = (mixed_ref[span(step), :].astype(jnp.float32) + update).astype(jnp.bfloat16)
         for row in range(step_rows):
-            out_ref[step * step_rows + row] = result[row * feats : (row + 1) * feats]
+            result_ref[step * step_rows + row] = result[row * feats : (row + 1) * feats]
         return carry
 
     lax.fori_loop(0, rows // step_rows, last, 0)
-
-
-ITEM_STEP = 4
-
-
-def own_rows(parts, feat_qkv, feat_out, item_qkv, item_out, keys, bias):
+    copy = pltpu.make_async_copy(result_ref, out_ref.at[pl.ds(first_row, rows)], sem)
+    copy.start()
+    copy.wait()
+
+
+ITEM_STEP = 5
+
+
+def own_rows(parts, feat_qkv, feat_out, item_qkv, item_out, keys, bias, total, first, before):
     feats_here, rows, width = parts[0].shape
     feats = len(parts) * feats_here
     table = pltpu.VMEM((rows * feats, width), jnp.float32)
-    return vmem_kernel(
-        row_kernel,
-        jax.ShapeDtypeStruct((rows, feats, width), jnp.bfloat16),
-        len(parts) + 6,
-        [table, pltpu.VMEM((rows * feats, width), jnp.bfloat16), table, table],
-        "rows",
-        24,
-    )(*parts, feat_qkv, feat_out, item_qkv, item_out, keys, bias)
+    block = pl.BlockSpec(memory_space=pltpu.VMEM)
+    anywhere = pl.BlockSpec(memory_space=pltpu.HBM)
+    aliased = [] if before is None else [before]
+    return pl.pallas_call(
+        functools.partial(row_kernel, first, len(aliased)),
+        out_shape=jax.ShapeDtypeStruct((total, feats, width), jnp.bfloat16),
+        in_specs=[block] * (len(parts) + 6) + [anywhere] * len(aliased),
+        out_specs=anywhere,
+        scratch_shapes=[
+            table,
+            pltpu.VMEM((rows * feats, width), jnp.bfloat16),
+            table,
+            table,
+            pltpu.VMEM((rows, feats, width), jnp.bfloat16),
+            pltpu.SemaphoreType.DMA,
+        ],
+        input_output_aliases={len(parts) + 6: 0} if aliased else {},
+        compiler_params=pltpu.CompilerParams(vmem_limit_bytes=24 << 20),
+        name="rows",
+    )(*parts, feat_qkv, feat_out, item_qkv, item_out, keys, bias, *aliased)
 
 
 def swap(tensor, step):
@@ -490,32 +558,47 @@
     return lax.ppermute(tensor, "feat", [(one, one ^ step) for one in range(devices)])
 
 
-CHUNKS = 1
-
-
-def one_block_per_table(
-    cells, block_table, row_live, row_train, feat_qkv, feat_out, item_qkv, item_out
-):
+CHUNKS = 2
+
+
+def one_block_per_table(cells, row_live, row_train, feat_qkv, feat_out, item_qkv, item_out):
     feat_devices = lax.axis_size("feat")
     group_rows = cells.shape[0] // feat_devices
-    chunks = [group_rows // CHUNKS] * CHUNKS
-    bias, train_rows, sends = prepare(cells, row_live, row_train, chunks)
-    train_parts = [train_rows] + [swap(train_rows, step) for step in range(1, feat_devices)]
+    bias, train_rows, near, sends = prepare(cells, row_live, row_train, CHUNKS)
+    near_part = swap(near, 1)
+    train_parts = [train_rows, near_part]
+    for step in range(2, feat_devices):
+        low = step & -step
+        if low == step:
+            train_parts.append(swap(train_rows, step))
+        else:
+            train_parts.append(swap(train_parts[step - low], low))
     row_parts = [
-        [sends[0][at]] + [swap(sends[step][at], step) for step in range(1, feat_devices)]
-        for at in range(len(chunks))
+        [sends[0][at], near_part]
+        + [swap(sends[step][at], step) for step in range(2, feat_devices)]
+        for at in range(CHUNKS)
     ]
     keys = key_rows(train_parts, feat_qkv, feat_out, item_qkv)
-    results = [
-        own_rows(parts, feat_qkv, feat_out, item_qkv, item_out, keys, bias)
-        for parts in row_parts
-    ]
-    return results[0] if len(results) == 1 else jnp.concatenate(results, axis=0)
+    result = None
+    for at, parts in enumerate(row_parts):
+        result = own_rows(
+            parts,
+            feat_qkv,
+            feat_out,
+            item_qkv,
+            item_out,
+            keys,
+            bias,
+            group_rows,
+            at * (group_rows // CHUNKS),
+            result,
+        )
+    return result
 
 
 def layer(cells, block_table, *rest):
     if block_table.shape[0] == TABLES:
-        return one_block_per_table(cells, block_table, *rest)
+        return one_block_per_table(cells, *rest)
     return on_device(cells, block_table, *rest)
 
 

time: 33.3 us -> 24.2 us (0.73)
  waiting for transfers between devices: 9.26 us -> 3.05 us
  local copies, waits for them, and re-layouts: 2.47 us -> 0.01 us
  Pallas kernels: 16 us -> 14.2 us
  starting transfers between devices: 5.23 us -> 6.72 us
    ppermute x6 -> x7, waiting for transfers between devices: 9.26 us -> 3.05 us  [swap(): lax.ppermute(tensor, 'feat', [(one, one ^ step) for one in range(devices)])]
    unnamed x14 -> x8, local copies, waits for them, and re-layouts: 2.47 us -> 0.01 us
    ppermute x6 -> x7, starting transfers between devices: 5.23 us -> 6.72 us  [swap(): lax.ppermute(tensor, 'feat', [(one, one ^ step) for one in range(devices)])]
    pallas_call x2 -> x3, Pallas kernels: 12.2 us -> 11.1 us  [the longest x2 8.98 us: own_rows(): pl.pallas_call(functools.partial(row_kernel, first, len(aliased)), out_sh...]
    pallas_call x1, Pallas kernels: 3.86 us -> 3.08 us  [key_rows(): vmem_kernel(key_kernel, jax.ShapeDtypeStruct((feats, rows, 2 * width), jn...]
  transfers between devices with their start and end apart: 6 -> 7, of which waited for: 2 -> 1; matrix products, arithmetic and copies ran while one was open for 0% -> 0% of each run, Pallas kernels for 12% -> 31%
where the time goes in v3:
time: 24.2 us; the launch traced here: 24.1 us
  Pallas kernels  14.2 us (59%)
  starting transfers between devices  6.72 us (28%)
  waiting for transfers between devices  3.05 us (13%)
    pallas_call x2, Pallas kernels, own_rows(): pl.pallas_call(functools.partial(row_kernel, first, len(aliased)), out_sh...  8.98 us
    ppermute x7, starting transfers between devices, swap(): lax.ppermute(tensor, 'feat', [(one, one ^ step) for one in range(devices)])  6.72 us
    pallas_call x1, Pallas kernels, key_rows(): vmem_kernel(key_kernel, jax.ShapeDtypeStruct((feats, rows, 2 * width), jn...  3.08 us
    ppermute x7, waiting for transfers between devices, swap(): lax.ppermute(tensor, 'feat', [(one, one ^ step) for one in range(devices)])  3.05 us
    pallas_call x1, Pallas kernels, prepare(): pl.pallas_call(functools.partial(prepare_kernel, chunks), out_shape=shape...  2.14 us
  transfers between devices with their start and end apart: 7, of which 1 were waited for; matrix products, arithmetic and copies ran while one was open for 0% of the time, Pallas kernels for 31%

profile of v3, /device:TPU:0, one launch (start us, length us, event | category | flops | bytes accessed | tf_op | source)
XLA Modules:
  0.0 24.1 jit_solution(9823527125413439679)
XLA Ops:
  0.0 0.0 copy-start
  0.0 0.0 copy-start.1
  0.0 0.0 copy-start.2
  0.0 2.1 %prepare.1 = (f32[16,128]{1,0:T(8,128)S(1)}, bf16[20,16,128]{2,1,0:T(8,128)(2,1)S(1)}, bf16[3,20,16,128]{3,2,1,0:T(8,128)(2,1)S(1)}, bf16[20,16,128]{2,1,0:T(8,1...) custom-call(s32[8,128]{1,0:T(8,128)} %bitcast.4, ...), custom_call_target="tpu_custom_call" | custom-call | tf_op jit(solution)/shard_map/prepare/pallas_call | solution.py:288
  2.2 0.6 %collective-permute-start = (bf16[3,20,16,128]{3,2,1,0:T(8,128)(2,1)S(1)}, bf16[3,20,16,128]{3,2,1,0:T(8,128)(2,1)S(1)}, u32[]{:S(2)}, u32[]{:S(2)}) collective-permute-start(bf16[3,20,16,128]{3,2,1,0:T(8,128)(2,1)S(1)} %get-tuple-element.15), channel_id=1, source_target_pairs={{0,1},{1,0},{2,3},{3,2},{4,5},{5,4},{6,7},{7,6},{8,9},{9,8},{10,11... | collective-permute-start | bytes 737288 | tf_op jit(solution)/shard_map/ppermute | solution.py:558
  2.7 2.6 %collective-permute-start.3 = (bf16[20,16,128]{2,1,0:T(8,128)(2,1)S(1)}, bf16[20,16,128]{2,1,0:T(8,128)(2,1)S(1)}, u32[]{:S(2)}, u32[]{:S(2)}) collective-permute-start(bf16[20,16,128]{2,1,0:T(8,128)(2,1)S(1)} %get-tuple-element.18.refs_0_), channel_id=1, source_target_pairs={{0,2},{1,3},{2,0},{3,1},{4,6},{5,7},{6,4},{7,5},{8,10},{9,11},{10,... | collective-permute-start | bytes 245768 | tf_op jit(solution)/shard_map/ppermute | solution.py:558
  5.3 3.0 %collective-permute-done.3.refs_2_ = bf16[20,16,128]{2,1,0:T(8,128)(2,1)S(1)} collective-permute-done((bf16[20,16,128]{2,1,0:T(8,128)(2,1)S(1)}, bf16[20,16,128]{2,1,0:T(8,128)(2,1)S(1)}, u32[]{:S(2)}, u32[]{:S(2)}) %collective-permute-start.3) | collective-permute-done | bytes 81952 | tf_op jit(solution)/shard_map/ppermute | solution.py:558
  8.3 0.0 collective-permute-start.4
  8.3 1.7 %collective-permute-start.5 = (bf16[20,16,128]{2,1,0:T(8,128)(2,1)S(1)}, bf16[20,16,128]{2,1,0:T(8,128)(2,1)S(1)}, u32[]{:S(2)}, u32[]{:S(2)}) collective-permute-start(bf16[20,16,128]{2,1,0:T(8,128)(2,1)S(1)} %get-tuple-element.21), channel_id=1, source_target_pairs={{0,2},{1,3},{2,0},{3,1},{4,6},{5,7},{6,4},{7,5},{8,10},{9,11},{10,... | collective-permute-start | bytes 245768 | tf_op jit(solution)/shard_map/ppermute | solution.py:558
  10.1 0.1 collective-permute-start.6
  10.2 1.7 %collective-permute-start.1 = (bf16[20,16,128]{2,1,0:T(8,128)(2,1)S(1)}, bf16[20,16,128]{2,1,0:T(8,128)(2,1)S(1)}, u32[]{:S(2)}, u32[]{:S(2)}) collective-permute-start(bf16[20,16,128]{2,1,0:T(8,128)(2,1)S(1)} %get-tuple-element.16), channel_id=1, source_target_pairs={{0,2},{1,3},{2,0},{3,1},{4,6},{5,7},{6,4},{7,5},{8,10},{9,11},{10,... | collective-permute-start | bytes 245768 | tf_op jit(solution)/shard_map/ppermute | solution.py:558
  11.9 0.0 collective-permute-done.4.refs_3_
  11.9 0.0 copy-start.3
  11.9 0.0 collective-permute-start.2
  11.9 0.0 collective-permute-done.refs_1_
  11.9 0.0 copy-done
  11.9 0.0 copy-done.1
  12.0 0.0 copy-done.2
  12.0 3.1 %shard_map.73.refs_8_ = bf16[80,16,256]{2,1,0:T(8,128)(2,1)S(1)} custom-call(bf16[20,16,128]{2,1,0:T(8,128)(2,1)S(1)} %get-tuple-element.18.refs_0_, bf16[3,20,16,128]{3,2,1,0:T(8,128)(2,1)S(1)} %collective-permute-done.refs_1_, bf16[20,16,128]{2,1,0:T(8,128)(2,1)S(1)} %collective-permute-done.3.refs_2_, ...), custom_call_target="tpu_custom_call" | custom-call | tf_op jit(solution)/shard_map/pallas_call | solution.py:421
  15.0 0.0 collective-permute-done.5.refs_2_
  15.1 0.0 collective-permute-done.6.refs_3_
  15.1 0.0 copy-done.3
  15.1 4.5 %rows.2.refs_10_ = bf16[32,80,128]{2,1,0:T(8,128)(2,1)} custom-call(bf16[20,16,128]{2,1,0:T(8,128)(2,1)S(1)} %get-tuple-element.20.refs_0_, bf16[3,20,16,128]{3,2,1,0:T(8,128)(2,1)S(1)} %collective-permute-done.refs_1_, bf16[20,16,128]{2,1,0:T(8,128)(2,1)S(1)} %collective-permute-done.5.refs_2_, bf16[20,16,128]{2,1,0:T(8,128)(2,1)S(1)} %collective-permute-done.6.refs_3_, ...), custom_call_target="tpu_custom_call" | custom-call | tf_op jit(solution)/shard_map/rows/pallas_call | solution.py:537
  19.6 0.0 collective-permute-done.1.refs_2_
  19.6 0.0 collective-permute-done.2.refs_3_
  19.6 4.5 %rows.3 = bf16[32,80,128]{2,1,0:T(8,128)(2,1)} custom-call(bf16[20,16,128]{2,1,0:T(8,128)(2,1)S(1)} %get-tuple-element.14.refs_0_, bf16[3,20,16,128]{3,2,1,0:T(8,128)(2,1)S(1)} %collective-permute-done.refs_1_, bf16[20,16,128]{2,1,0:T(8,128)(2,1)S(1)} %collective-permute-done.1.refs_2_, ...), custom_call_target="tpu_custom_call", output_to_operand_aliasing={{}: (10, {})} | custom-call | tf_op jit(solution)/shard_map/rows/pallas_call | solution.py:537
Async XLA Ops:
  0.0 11.9 %copy-start = (bf16[128,384]{1,0:T(8,128)(2,1)S(1)}, bf16[128,384]{1,0:T(8,128)(2,1)}, u32[]{:S(2)}) copy-start(bf16[128,384]{1,0:T(8,128)(2,1)} %refs_4_.5) | copy-start | bytes 294916
  0.0 11.9 %copy-start.1 = (bf16[128,384]{1,0:T(8,128)(2,1)S(1)}, bf16[128,384]{1,0:T(8,128)(2,1)}, u32[]{:S(2)}) copy-start(bf16[128,384]{1,0:T(8,128)(2,1)} %refs_6_.5) | copy-start | bytes 294916
  0.0 12.0 %copy-start.2 = (bf16[128,128]{1,0:T(8,128)(2,1)S(1)}, bf16[128,128]{1,0:T(8,128)(2,1)}, u32[]{:S(2)}) copy-start(bf16[128,128]{1,0:T(8,128)(2,1)} %refs_5_.5) | copy-start | bytes 98308
  2.2 9.8 %collective-permute-start = (bf16[3,20,16,128]{3,2,1,0:T(8,128)(2,1)S(1)}, bf16[3,20,16,128]{3,2,1,0:T(8,128)(2,1)S(1)}, u32[]{:S(2)}, u32[]{:S(2)}) collective-permute-start(bf16[3,20,16,128]{3,2,1,0:T(8,128)(2,1)S(1)} %get-tuple-element.15), channel_id=1, source_target_pairs={{0,1},{1,0},{2,3},{3,2},{4,5},{5,4},{6,7},{7,6},{8,9},{9,8},{10,11... | collective-permute-start | bytes 737288 | tf_op jit(solution)/shard_map/ppermute | solution.py:558
  2.7 5.6 %collective-permute-start.3 = (bf16[20,16,128]{2,1,0:T(8,128)(2,1)S(1)}, bf16[20,16,128]{2,1,0:T(8,128)(2,1)S(1)}, u32[]{:S(2)}, u32[]{:S(2)}) collective-permute-start(bf16[20,16,128]{2,1,0:T(8,128)(2,1)S(1)} %get-tuple-element.18.refs_0_), channel_id=1, source_target_pairs={{0,2},{1,3},{2,0},{3,1},{4,6},{5,7},{6,4},{7,5},{8,10},{9,11},{10,... | collective-permute-start | bytes 245768 | tf_op jit(solution)/shard_map/ppermute | solution.py:558
  8.3 3.6 %collective-permute-start.4 = (bf16[20,16,128]{2,1,0:T(8,128)(2,1)S(1)}, bf16[20,16,128]{2,1,0:T(8,128)(2,1)S(1)}, u32[]{:S(2)}, u32[]{:S(2)}) collective-permute-start(bf16[20,16,128]{2,1,0:T(8,128)(2,1)S(1)} %collective-permute-done.3.refs_2_), channel_id=1, source_target_pairs={{0,1},{1,0},{2,3},{3,2},{4,5},{5,4},{6,7},{7,6},{8,9},{9,8},{10,11... | collective-permute-start | bytes 245768 | tf_op jit(solution)/shard_map/ppermute | solution.py:558
  8.3 6.7 %collective-permute-start.5 = (bf16[20,16,128]{2,1,0:T(8,128)(2,1)S(1)}, bf16[20,16,128]{2,1,0:T(8,128)(2,1)S(1)}, u32[]{:S(2)}, u32[]{:S(2)}) collective-permute-start(bf16[20,16,128]{2,1,0:T(8,128)(2,1)S(1)} %get-tuple-element.21), channel_id=1, source_target_pairs={{0,2},{1,3},{2,0},{3,1},{4,6},{5,7},{6,4},{7,5},{8,10},{9,11},{10,... | collective-permute-start | bytes 245768 | tf_op jit(solution)/shard_map/ppermute | solution.py:558
  10.1 5.0 %collective-permute-start.6 = (bf16[20,16,128]{2,1,0:T(8,128)(2,1)S(1)}, bf16[20,16,128]{2,1,0:T(8,128)(2,1)S(1)}, u32[]{:S(2)}, u32[]{:S(2)}) collective-permute-start(bf16[20,16,128]{2,1,0:T(8,128)(2,1)S(1)} %get-tuple-element.22), channel_id=1, source_target_pairs={{0,3},{1,2},{2,1},{3,0},{4,7},{5,6},{6,5},{7,4},{8,11},{9,10},{10,... | collective-permute-start | bytes 245768 | tf_op jit(solution)/shard_map/ppermute | solution.py:558
  10.2 9.4 %collective-permute-start.1 = (bf16[20,16,128]{2,1,0:T(8,128)(2,1)S(1)}, bf16[20,16,128]{2,1,0:T(8,128)(2,1)S(1)}, u32[]{:S(2)}, u32[]{:S(2)}) collective-permute-start(bf16[20,16,128]{2,1,0:T(8,128)(2,1)S(1)} %get-tuple-element.16), channel_id=1, source_target_pairs={{0,2},{1,3},{2,0},{3,1},{4,6},{5,7},{6,4},{7,5},{8,10},{9,11},{10,... | collective-permute-start | bytes 245768 | tf_op jit(solution)/shard_map/ppermute | solution.py:558
  11.9 3.2 %copy-start.3 = (bf16[128,128]{1,0:T(8,128)(2,1)S(1)}, bf16[128,128]{1,0:T(8,128)(2,1)}, u32[]{:S(2)}) copy-start(bf16[128,128]{1,0:T(8,128)(2,1)} %refs_7_.3) | copy-start | bytes 98308
  11.9 7.7 %collective-permute-start.2 = (bf16[20,16,128]{2,1,0:T(8,128)(2,1)S(1)}, bf16[20,16,128]{2,1,0:T(8,128)(2,1)S(1)}, u32[]{:S(2)}, u32[]{:S(2)}) collective-permute-start(bf16[20,16,128]{2,1,0:T(8,128)(2,1)S(1)} %get-tuple-element.17), channel_id=1, source_target_pairs={{0,3},{1,2},{2,1},{3,0},{4,7},{5,6},{6,5},{7,4},{8,11},{9,10},{10,... | collective-permute-start | bytes 245768 | tf_op jit(solution)/shard_map/ppermute | solution.py:558

commit v4 on v3

--- a/solution.py
+++ b/solution.py
@@ -211,21 +211,6 @@
     count = jnp.sum(live, axis=1, keepdims=True) * width
     weight = jnp.transpose(jnp.broadcast_to(live, (width, rows_here)))
 
-    def total(values):
-        return jnp.sum(jnp.sum(values, axis=0, keepdims=True), axis=1, keepdims=True)
-
-    means = []
-    for feat in range(feats_here):
-        if feat % piece == 0:
-            copies[2 + feat // piece].wait()
-        values = cells_ref[feat].astype(jnp.float32)
-        means.append(jnp.broadcast_to(total(values * weight) / count, (1, width)))
-    factors = []
-    for feat in range(feats_here):
-        centred = cells_ref[feat].astype(jnp.float32) - means[feat]
-        spread = total(centred * centred * weight) / count
-        factors.append(jnp.broadcast_to(lax.rsqrt(spread + EPSILON), (1, width)))
-
     train = jnp.broadcast_to(train_ref[pl.ds(row_index, 1), :], (keys, rows_here))
     before = lax.broadcasted_iota(jnp.int32, (rows_here, rows_here), 0)
     after = lax.broadcasted_iota(jnp.int32, (rows_here, rows_here), 1)
@@ -245,7 +230,24 @@
     chosen = jnp.where(here, 1.0, 0.0)
     found = jnp.sum(chosen, axis=1, keepdims=True)
     bias_ref[...] = jnp.broadcast_to(jnp.where(found > 0.5, 0.0, MASKED), bias_ref.shape)
-    chosen = chosen.astype(jnp.bfloat16)
+    picks = jnp.concatenate(
+        [chosen, jnp.broadcast_to(live, (keys, rows_here))], axis=0
+    ).astype(jnp.bfloat16)
+
+    means, train_rows = [], []
+    for feat in range(feats_here):
+        if feat % piece == 0:
+            copies[2 + feat // piece].wait()
+        picked = jnp.dot(picks, cells_ref[feat], preferred_element_type=jnp.float32)
+        train_rows.append(picked[:keys])
+        total = jnp.sum(picked[keys : keys + 1], axis=1, keepdims=True)
+        means.append(jnp.broadcast_to(total / count, (1, width)))
+    factors = []
+    for feat in range(feats_here):
+        centred = cells_ref[feat].astype(jnp.float32) - means[feat]
+        total = jnp.sum(centred * centred * weight, axis=0, keepdims=True)
+        spread = jnp.sum(total, axis=1, keepdims=True) / count
+        factors.append(jnp.broadcast_to(lax.rsqrt(spread + EPSILON), (1, width)))
 
     def normed(feat, values):
         centred = values.astype(jnp.float32) - means[feat]
@@ -253,9 +255,7 @@
 
     near_out = outs[0]
     for feat in range(feats_here):
-        rows = jnp.dot(
-            chosen, normed(feat, cells_ref[feat]), preferred_element_type=jnp.float32
-        ).astype(jnp.bfloat16)
+        rows = normed(feat, train_rows[feat])
         train_out[feat] = rows
         near_out[0, feat] = rows
     for step in range(feat_devices):
@@ -310,14 +310,18 @@
     return outs[0], outs[1], outs[2], sends
 
 
+def pitch(count):
+    return count + 4 if count % 8 == 0 else count
+
+
 def gather_parts(parts, at, held):
     feat_index = lax.axis_index("feat")
-    feats_here, rows, width = parts[0].shape
-    size = feats_here * rows
+    feats_here, rows, _ = parts[0].shape
     for step, part in enumerate(parts):
-        start = pl.multiple_of((feat_index ^ step) * size, size)
+        first = (feat_index ^ step) * (feats_here * pitch(rows))
         values = part[at] if step == 1 else part[...]
-        held[pl.ds(start, size), :] = values.reshape(size, width).astype(jnp.float32)
+        for feat in range(feats_here):
+            held[pl.ds(first + feat * pitch(rows), rows), :] = values[feat].astype(jnp.float32)
 
 
 def head_masks(rows, width):
@@ -330,45 +334,32 @@
 
 
 def attend(queries, keys, values, masks):
-    count, width = queries.shape
-    half = width // 2
+    count = queries.shape[0]
     scores = lax.dot_general(
-        jnp.concatenate(by_head(queries, masks), axis=0),
-        keys,
+        jnp.concatenate(by_head(keys, masks), axis=0),
+        queries,
         (((1,), (1,)), ((), ())),
         preferred_element_type=jnp.float32,
-    )
+    ).reshape(HEADS, count, count)
     top = jnp.max(scores, axis=1, keepdims=True)
-    shares = jnp.exp2((scores - top) * SCALE2).astype(jnp.bfloat16)
-    lane = lax.broadcasted_iota(jnp.int32, (count, width), 1)
-    low, ones = lane < half, jnp.ones_like(values)
-    sides = []
-    for side in range(2):
-        first = side * (HEADS // 2)
-        both = jnp.where(low, values, ones) if side == 0 else jnp.where(low, ones, values)
-        mixed = jnp.dot(
-            shares[first * count : (first + HEADS // 2) * count],
-            both,
-            preferred_element_type=jnp.float32,
-        )
-        picked = mixed[:count]
-        for head in range(1, HEADS // 2):
-            mine = (lane % half) // HEAD_DIM == head
-            picked = jnp.where(mine, mixed[head * count : (head + 1) * count], picked)
-        sides.append(picked)
-    out = jnp.where(low, sides[0], sides[1])
-    total = pltpu.roll(jnp.where(low, sides[1], sides[0]), half, 1)
-    return out / total
-
-
-def feature_rows(held, first, rows, stride, qkv_ref, out_ref):
-    feats = held.shape[0] // stride
-    width = held.shape[1]
-    cells = jnp.concatenate(
-        [held[pl.ds(first + row, feats, stride=stride), :] for row in range(rows)], axis=0
-    )
+    powers = jnp.exp2((scores - top) * SCALE2)
+    shares = powers * (1.0 / jnp.sum(powers, axis=1, keepdims=True))
+    shares = shares.reshape(HEADS * count, count).astype(jnp.bfloat16)
+    return lax.dot_general(
+        shares,
+        jnp.concatenate(by_head(values, masks), axis=0),
+        (((0,), (0,)), ((), ())),
+        preferred_element_type=jnp.float32,
+    )
+
+
+def feature_rows(held, mixed_ref, rows, qkv_ref, out_ref):
+    feats, width = held.shape[0] // pitch(rows), held.shape[1]
+    cells = [held[pl.ds(row, feats, stride=pitch(rows)), :] for row in range(rows)]
     projected = jnp.dot(
-        cells.astype(jnp.bfloat16), qkv_ref[...], preferred_element_type=jnp.float32
+        jnp.concatenate(cells, axis=0).astype(jnp.bfloat16),
+        qkv_ref[...],
+        preferred_element_type=jnp.float32,
     ).astype(jnp.bfloat16)
     masks = head_masks(feats, width)
     attended = []
@@ -382,175 +373,175 @@
                 masks,
             ).astype(jnp.bfloat16)
         )
-    attended = jnp.concatenate(attended, axis=0)
-    update = jnp.dot(attended, out_ref[...], preferred_element_type=jnp.float32)
-    return (cells + update).astype(jnp.bfloat16)
-
-
-STEP = 16
+    update = jnp.dot(
+        jnp.concatenate(attended, axis=0), out_ref[...], preferred_element_type=jnp.float32
+    )
+    for row in range(rows):
+        mixed = (cells[row] + update[row * feats : (row + 1) * feats]).astype(jnp.bfloat16)
+        mixed_ref[pl.ds(row * pitch(feats), feats), :] = mixed.astype(jnp.float32)
+
+
+def by_feature(mixed_ref, first, count, rows, stride):
+    return jnp.concatenate(
+        [mixed_ref[pl.ds(first + feat, rows, stride=stride), :] for feat in range(count)], axis=0
+    )
 
 
 def key_kernel(*refs):
     feat_devices = lax.axis_size("feat")
     parts = refs[:feat_devices]
-    feat_qkv, feat_out, item_qkv, out_ref, held, key_ref, value_ref = refs[feat_devices:]
-    rows = parts[0].shape[1]
-    feats, width = held.shape[0] // rows, held.shape[1]
-    step_rows = math.gcd(rows, STEP)
+    feat_qkv, feat_out, item_qkv, out_ref, held, mixed_ref = refs[feat_devices:]
+    feats, rows, width = out_ref.shape[0], out_ref.shape[1], held.shape[1]
     gather_parts(parts, 0, held)
-
-    def one(step, carry):
-        mixed = feature_rows(held, step * step_rows, step_rows, rows, feat_qkv, feat_out)
+    feature_rows(held, mixed_ref, rows, feat_qkv, feat_out)
+    together = 128 // rows
+    for feat in range(0, feats, together):
+        mixed = by_feature(mixed_ref, feat, together, rows, pitch(feats)).astype(jnp.bfloat16)
         both = jnp.dot(mixed, item_qkv[:, width:], preferred_element_type=jnp.float32)
-        here = pl.ds(pl.multiple_of(step * (step_rows * feats), step_rows * feats), step_rows * feats)
-        key_ref[here, :] = both[:, :width]
-        value_ref[here, :] = both[:, width:]
-        return carry
-
-    lax.fori_loop(0, rows // step_rows, one, 0)
-    for feat in range(feats):
-        here = pl.ds(feat, rows, stride=feats)
-        out_ref[feat, :, :width] = key_ref[here, :].astype(jnp.bfloat16)
-        out_ref[feat, :, width:] = value_ref[here, :].astype(jnp.bfloat16)
+        out_ref[pl.ds(feat, together)] = both.astype(jnp.bfloat16).reshape(
+            together, rows, 2 * width
+        )
 
 
 def key_rows(parts, feat_qkv, feat_out, item_qkv):
     feats_here, rows, width = parts[0].shape
     feats = len(parts) * feats_here
-    table = pltpu.VMEM((rows * feats, width), jnp.float32)
     return vmem_kernel(
         key_kernel,
         jax.ShapeDtypeStruct((feats, rows, 2 * width), jnp.bfloat16),
         len(parts) + 3,
-        [table, table, table],
+        [
+            pltpu.VMEM((feats * pitch(rows), width), jnp.float32),
+            pltpu.VMEM((rows * pitch(feats), width), jnp.float32),
+        ],
         24,
     )(*parts, feat_qkv, feat_out, item_qkv)
 
 
-def row_kernel(first_row, aliased, *refs):
+def row_kernel(first_row, earlier, last, *refs):
     feat_devices = lax.axis_size("feat")
     parts = refs[:feat_devices]
     (feat_qkv, feat_out, item_qkv, item_out, keys_ref, bias_ref) = refs[
         feat_devices : feat_devices + 6
     ]
-    out_ref, held, mixed_ref, query_ref, item_ref, result_ref, sem = refs[
-        feat_devices + 6 + aliased :
+    results = refs[feat_devices + 6 : feat_devices + 6 + earlier]
+    out_ref, held, mixed_ref, query_ref, item_ref, total_ref, *own = refs[
+        feat_devices + 6 + earlier :
     ]
-    rows = parts[0].shape[1]
-    feats, width = held.shape[0] // rows, held.shape[1]
-    step_rows = math.gcd(rows, STEP)
-    keys = keys_ref.shape[1]
-    gather_parts(parts, 1 + first_row // parts[0].shape[1], held)
-
-    def span(step):
-        return pl.ds(pl.multiple_of(step * (step_rows * feats), step_rows * feats), step_rows * feats)
-
-    def one(step, carry):
-        mixed = feature_rows(held, step * step_rows, step_rows, rows, feat_qkv, feat_out)
-        mixed_ref[span(step), :] = mixed
-        query_ref[span(step), :] = jnp.dot(
-            mixed, item_qkv[:, :width], preferred_element_type=jnp.float32
-        )
-        return carry
-
-    lax.fori_loop(0, rows // step_rows, one, 0)
-
+    rows, width = parts[0].shape[1], held.shape[1]
+    feats, keys = keys_ref.shape[0], keys_ref.shape[1]
+    copies = []
+
+    def send(source, at, count):
+        copy = pltpu.make_async_copy(source, out_ref.at[pl.ds(at, count)], own[1].at[len(copies)])
+        copy.start()
+        copies.append(copy)
+
+    for at, result in enumerate(results):
+        send(result, at * rows, rows)
+    gather_parts(parts, 1 + first_row // rows, held)
+    feature_rows(held, mixed_ref, rows, feat_qkv, feat_out)
+
+    stride = pitch(feats)
     together = 128 // rows
     lanes = together * rows
-    pairs = together // 2
+    size = HEADS * keys
     key_masks = head_masks(keys, width)
     bias = jnp.concatenate([bias_ref[:, :lanes]] * HEADS, axis=0)
-    lane_owner = lax.broadcasted_iota(jnp.int32, (HEADS * keys, lanes), 1) // rows
-    pair_row = lax.broadcasted_iota(jnp.int32, (2 * rows, 2 * HEADS * keys), 0) // rows
-    pair_lane = lax.broadcasted_iota(jnp.int32, (2 * rows, 2 * HEADS * keys), 1) // (HEADS * keys)
+    lane_owner = lax.broadcasted_iota(jnp.int32, (size, lanes), 1) // rows
+    pair_row = lax.broadcasted_iota(jnp.int32, (2 * rows, 2 * size), 0) // rows
+    pair_lane = lax.broadcasted_iota(jnp.int32, (2 * rows, 2 * size), 1) // size
     pair_mask = pair_row == pair_lane
 
-    def item(step):
-        queries, stacked_keys, stacked_values = [], [], []
+    for first in range(0, feats, together):
+        mixed = by_feature(mixed_ref, first, together, rows, stride)
+        query_ref[pl.ds(first * rows, lanes), :] = jnp.dot(
+            mixed.astype(jnp.bfloat16), item_qkv[:, :width], preferred_element_type=jnp.float32
+        ).astype(jnp.bfloat16)
+
+    def item(first):
+        stacked_keys, stacked_values = [], []
         for inner in range(together):
-            feat = step * together + inner
-            queries.append(query_ref[pl.ds(feat, rows, stride=feats), :].astype(jnp.bfloat16))
-            stacked_keys += by_head(keys_ref[feat, :, :width], key_masks)
-            stacked_values += by_head(keys_ref[feat, :, width:], key_masks)
+            stacked_keys += by_head(keys_ref[first + inner, :, :width], key_masks)
+            stacked_values += by_head(keys_ref[first + inner, :, width:], key_masks)
         every = lax.dot_general(
             jnp.concatenate(stacked_keys, axis=0),
-            jnp.concatenate(queries, axis=0),
+            query_ref[pl.ds(pl.multiple_of(first * rows, lanes), lanes), :],
             (((1,), (1,)), ((), ())),
             preferred_element_type=jnp.float32,
         )
-        size = HEADS * keys
         scores = every[:size]
         for inner in range(1, together):
             scores = jnp.where(lane_owner == inner, every[inner * size : (inner + 1) * size], scores)
         scores = (scores + bias).reshape(HEADS, keys, lanes)
         top = jnp.max(scores, axis=1, keepdims=True)
         powers = jnp.exp2((scores - top) * SCALE2)
-        shares = powers / jnp.sum(powers, axis=1, keepdims=True)
+        shares = powers * (1.0 / jnp.sum(powers, axis=1, keepdims=True))
         shares = shares.reshape(size, lanes)
         shares = jnp.transpose(jnp.concatenate([shares, shares], axis=0)).astype(jnp.bfloat16)
-        for pair in range(pairs):
+        for pair in range(together // 2):
             block = shares[pair * 2 * rows : (pair + 1) * 2 * rows]
-            result = jnp.dot(
+            here = pl.multiple_of((first + pair * 2) * rows, 2 * rows)
+            item_ref[pl.ds(here, 2 * rows), :] = jnp.dot(
                 jnp.where(pair_mask, block, jnp.zeros_like(block)),
                 jnp.concatenate(
                     stacked_values[pair * 2 * HEADS : (pair + 1) * 2 * HEADS], axis=0
                 ),
                 preferred_element_type=jnp.float32,
-            )
-            for inner in range(2):
-                feat = step * together + pair * 2 + inner
-                item_ref[pl.ds(feat, rows, stride=feats), :] = result[
-                    inner * rows : (inner + 1) * rows
-                ]
+            ).astype(jnp.bfloat16)
 
     def items(step, carry):
         for inner in range(ITEM_STEP):
-            item(step * ITEM_STEP + inner)
+            item((step * ITEM_STEP + inner) * together)
         return carry
 
     lax.fori_loop(0, feats // (together * ITEM_STEP), items, 0)
-
-    def last(step, carry):
-        attended = item_ref[span(step), :].astype(jnp.bfloat16)
-        update = jnp.dot(attended, item_out[...], preferred_element_type=jnp.float32)
-        result = (mixed_ref[span(step), :].astype(jnp.float32) + update).astype(jnp.bfloat16)
-        for row in range(step_rows):
-            result_ref[step * step_rows + row] = result[row * feats : (row + 1) * feats]
-        return carry
-
-    lax.fori_loop(0, rows // step_rows, last, 0)
-    copy = pltpu.make_async_copy(result_ref, out_ref.at[pl.ds(first_row, rows)], sem)
-    copy.start()
-    copy.wait()
-
-
-ITEM_STEP = 5
-
-
-def own_rows(parts, feat_qkv, feat_out, item_qkv, item_out, keys, bias, total, first, before):
+    for first in range(0, feats, together):
+        update = jnp.dot(
+            item_ref[pl.ds(first * rows, lanes), :],
+            item_out[...],
+            preferred_element_type=jnp.float32,
+        )
+        total = by_feature(mixed_ref, first, together, rows, stride) + update
+        for inner in range(together):
+            total_ref[pl.ds(first + inner, rows, stride=stride), :] = total[
+                inner * rows : (inner + 1) * rows
+            ]
+    result_ref = own[0] if last else out_ref
+    for row in range(rows):
+        result_ref[row] = total_ref[pl.ds(row * stride, feats), :].astype(jnp.bfloat16)
+        if last and (row + 1) % OUT_ROWS == 0:
+            first = row + 1 - OUT_ROWS
+            send(result_ref.at[pl.ds(first, OUT_ROWS)], first_row + first, OUT_ROWS)
+    for copy in copies:
+        copy.wait()
+
+
+OUT_ROWS = 4
+ITEM_STEP = 10
+
+
+def own_rows(parts, feat_qkv, feat_out, item_qkv, item_out, keys, bias, total, first, results):
     feats_here, rows, width = parts[0].shape
     feats = len(parts) * feats_here
-    table = pltpu.VMEM((rows * feats, width), jnp.float32)
+    last = first + rows == total
+    results = results if last else []
+    table = pltpu.VMEM((rows * pitch(feats), width), jnp.float32)
+    packed = pltpu.VMEM((rows * feats, width), jnp.bfloat16)
+    scratch = [pltpu.VMEM((feats * pitch(rows), width), jnp.float32), table, packed, packed, table]
+    if last:
+        scratch.append(pltpu.VMEM((rows, feats, width), jnp.bfloat16))
+        scratch.append(pltpu.SemaphoreType.DMA((len(results) + rows // OUT_ROWS,)))
     block = pl.BlockSpec(memory_space=pltpu.VMEM)
-    anywhere = pl.BlockSpec(memory_space=pltpu.HBM)
-    aliased = [] if before is None else [before]
     return pl.pallas_call(
-        functools.partial(row_kernel, first, len(aliased)),
-        out_shape=jax.ShapeDtypeStruct((total, feats, width), jnp.bfloat16),
-        in_specs=[block] * (len(parts) + 6) + [anywhere] * len(aliased),
-        out_specs=anywhere,
-        scratch_shapes=[
-            table,
-            pltpu.VMEM((rows * feats, width), jnp.bfloat16),
-            table,
-            table,
-            pltpu.VMEM((rows, feats, width), jnp.bfloat16),
-            pltpu.SemaphoreType.DMA,
-        ],
-        input_output_aliases={len(parts) + 6: 0} if aliased else {},
+        functools.partial(row_kernel, first, len(results), last),
+        out_shape=jax.ShapeDtypeStruct((total if last else rows, feats, width), jnp.bfloat16),
+        in_specs=[block] * (len(parts) + 6 + len(results)),
+        out_specs=pl.BlockSpec(memory_space=pltpu.HBM) if last else block,
+        scratch_shapes=scratch,
         compiler_params=pltpu.CompilerParams(vmem_limit_bytes=24 << 20),
         name="rows",
-    )(*parts, feat_qkv, feat_out, item_qkv, item_out, keys, bias, *aliased)
+    )(*parts, feat_qkv, feat_out, item_qkv, item_out, keys, bias, *results)
 
 
 def swap(tensor, step):
@@ -579,7 +570,7 @@
         for at in range(CHUNKS)
     ]
     keys = key_rows(train_parts, feat_qkv, feat_out, item_qkv)
-    result = None
+    results = []
     for at, parts in enumerate(row_parts):
         result = own_rows(
             parts,
@@ -591,9 +582,10 @@
             bias,
             group_rows,
             at * (group_rows // CHUNKS),
-            result,
-        )
-    return result
+            results,
+        )
+        results.append(result)
+    return results[-1]
 
 
 def layer(cells, block_table, *rest):

time: 24.2 us -> 22.4 us (0.926)
  Pallas kernels: 14.2 us -> 11.8 us
  waiting for transfers between devices: 3.05 us -> 3.72 us
    pallas_call x2, Pallas kernels: 8.98 us -> 7.24 us  [own_rows(): pl.pallas_call(functools.partial(row_kernel, first, len(results), last),...]
    pallas_call x1, Pallas kernels: 3.08 us -> 2.25 us  [key_rows(): vmem_kernel(key_kernel, jax.ShapeDtypeStruct((feats, rows, 2 * width), jn...]
    ppermute x7, waiting for transfers between devices: 3.05 us -> 3.72 us  [swap(): lax.ppermute(tensor, 'feat', [(one, one ^ step) for one in range(devices)])]
  transfers between devices with their start and end apart: 7 -> 7, of which waited for: 1 -> 3; matrix products, arithmetic and copies ran while one was open for 0% -> 0% of each run, Pallas kernels for 31% -> 25%
where the time goes in v4:
time: 22.4 us; the launch traced here: 22.3 us
  Pallas kernels  11.8 us (53%)
  starting transfers between devices  6.72 us (30%)
  waiting for transfers between devices  3.72 us (17%)
    pallas_call x2, Pallas kernels, own_rows(): pl.pallas_call(functools.partial(row_kernel, first, len(results), last),...  7.24 us
    ppermute x7, starting transfers between devices, swap(): lax.ppermute(tensor, 'feat', [(one, one ^ step) for one in range(devices)])  6.72 us
    ppermute x7, waiting for transfers between devices, swap(): lax.ppermute(tensor, 'feat', [(one, one ^ step) for one in range(devices)])  3.72 us
    pallas_call x1, Pallas kernels, prepare(): pl.pallas_call(functools.partial(prepare_kernel, chunks), out_shape=shape...  2.29 us
    pallas_call x1, Pallas kernels, key_rows(): vmem_kernel(key_kernel, jax.ShapeDtypeStruct((feats, rows, 2 * width), jn...  2.25 us
  transfers between devices with their start and end apart: 7, of which 3 were waited for; matrix products, arithmetic and copies ran while one was open for 0% of the time, Pallas kernels for 25%

profile of v4, /device:TPU:0, one launch (start us, length us, event | category | flops | bytes accessed | tf_op | source)
XLA Modules:
  0.0 22.3 jit_solution(13706869722979290181)
XLA Ops:
  0.0 0.0 copy-start
  0.0 0.0 copy-start.1
  0.0 0.0 copy-start.2
  0.0 2.3 %prepare.1 = (f32[16,128]{1,0:T(8,128)S(1)}, bf16[20,16,128]{2,1,0:T(8,128)(2,1)S(1)}, bf16[3,20,16,128]{3,2,1,0:T(8,128)(2,1)S(1)}, bf16[20,16,128]{2,1,0:T(8,1...) custom-call(s32[8,128]{1,0:T(8,128)} %bitcast.4, ...), custom_call_target="tpu_custom_call" | custom-call | tf_op jit(solution)/shard_map/prepare/pallas_call | solution.py:288
  2.3 0.6 %collective-permute-start = (bf16[3,20,16,128]{3,2,1,0:T(8,128)(2,1)S(1)}, bf16[3,20,16,128]{3,2,1,0:T(8,128)(2,1)S(1)}, u32[]{:S(2)}, u32[]{:S(2)}) collective-permute-start(bf16[3,20,16,128]{3,2,1,0:T(8,128)(2,1)S(1)} %get-tuple-element.15), channel_id=1, source_target_pairs={{0,1},{1,0},{2,3},{3,2},{4,5},{5,4},{6,7},{7,6},{8,9},{9,8},{10,11... | collective-permute-start | bytes 737288 | tf_op jit(solution)/shard_map/ppermute | solution.py:549
  2.9 2.6 %collective-permute-start.3 = (bf16[20,16,128]{2,1,0:T(8,128)(2,1)S(1)}, bf16[20,16,128]{2,1,0:T(8,128)(2,1)S(1)}, u32[]{:S(2)}, u32[]{:S(2)}) collective-permute-start(bf16[20,16,128]{2,1,0:T(8,128)(2,1)S(1)} %get-tuple-element.18.refs_0_), channel_id=1, source_target_pairs={{0,2},{1,3},{2,0},{3,1},{4,6},{5,7},{6,4},{7,5},{8,10},{9,11},{10,... | collective-permute-start | bytes 245768 | tf_op jit(solution)/shard_map/ppermute | solution.py:549
  5.4 3.0 %collective-permute-done.3.refs_2_ = bf16[20,16,128]{2,1,0:T(8,128)(2,1)S(1)} collective-permute-done((bf16[20,16,128]{2,1,0:T(8,128)(2,1)S(1)}, bf16[20,16,128]{2,1,0:T(8,128)(2,1)S(1)}, u32[]{:S(2)}, u32[]{:S(2)}) %collective-permute-start.3) | collective-permute-done | bytes 81952 | tf_op jit(solution)/shard_map/ppermute | solution.py:549
  8.5 0.0 collective-permute-start.4
  8.5 1.7 %collective-permute-start.5 = (bf16[20,16,128]{2,1,0:T(8,128)(2,1)S(1)}, bf16[20,16,128]{2,1,0:T(8,128)(2,1)S(1)}, u32[]{:S(2)}, u32[]{:S(2)}) collective-permute-start(bf16[20,16,128]{2,1,0:T(8,128)(2,1)S(1)} %get-tuple-element.21), channel_id=1, source_target_pairs={{0,2},{1,3},{2,0},{3,1},{4,6},{5,7},{6,4},{7,5},{8,10},{9,11},{10,... | collective-permute-start | bytes 245768 | tf_op jit(solution)/shard_map/ppermute | solution.py:549
  10.2 0.1 collective-permute-start.6
  10.3 1.7 %collective-permute-start.1 = (bf16[20,16,128]{2,1,0:T(8,128)(2,1)S(1)}, bf16[20,16,128]{2,1,0:T(8,128)(2,1)S(1)}, u32[]{:S(2)}, u32[]{:S(2)}) collective-permute-start(bf16[20,16,128]{2,1,0:T(8,128)(2,1)S(1)} %get-tuple-element.16), channel_id=1, source_target_pairs={{0,2},{1,3},{2,0},{3,1},{4,6},{5,7},{6,4},{7,5},{8,10},{9,11},{10,... | collective-permute-start | bytes 245768 | tf_op jit(solution)/shard_map/ppermute | solution.py:549
  12.1 0.0 collective-permute-done.4.refs_3_
  12.1 0.0 copy-start.3
  12.1 0.0 collective-permute-start.2
  12.1 0.0 collective-permute-done.refs_1_
  12.1 0.0 copy-done
  12.1 0.0 copy-done.1
  12.1 0.0 copy-done.2
  12.1 2.2 %shard_map.73.refs_8_ = bf16[80,16,256]{2,1,0:T(8,128)(2,1)S(1)} custom-call(bf16[20,16,128]{2,1,0:T(8,128)(2,1)S(1)} %get-tuple-element.18.refs_0_, bf16[3,20,16,128]{3,2,1,0:T(8,128)(2,1)S(1)} %collective-permute-done.refs_1_, bf16[20,16,128]{2,1,0:T(8,128)(2,1)S(1)} %collective-permute-done.3.refs_2_, ...), custom_call_target="tpu_custom_call" | custom-call | tf_op jit(solution)/shard_map/pallas_call | solution.py:409
  14.4 0.0 collective-permute-done.5.refs_2_
  14.4 0.4 %collective-permute-done.6.refs_3_ = bf16[20,16,128]{2,1,0:T(8,128)(2,1)S(1)} collective-permute-done((bf16[20,16,128]{2,1,0:T(8,128)(2,1)S(1)}, bf16[20,16,128]{2,1,0:T(8,128)(2,1)S(1)}, u32[]{:S(2)}, u32[]{:S(2)}) %collective-permute-start.6) | collective-permute-done | bytes 81952 | tf_op jit(solution)/shard_map/ppermute | solution.py:549
  14.8 0.0 copy-done.3
  14.8 3.2 %rows.2.refs_10_ = bf16[16,80,128]{2,1,0:T(8,128)(2,1)S(1)} custom-call(bf16[20,16,128]{2,1,0:T(8,128)(2,1)S(1)} %get-tuple-element.20.refs_0_, bf16[3,20,16,128]{3,2,1,0:T(8,128)(2,1)S(1)} %collective-permute-done.refs_1_, bf16[20,16,128]{2,1,0:T(8,128)(2,1)S(1)} %collective-permute-done.5.refs_2_, bf16[20,16,128]{2,1,0:T(8,128)(2,1)S(1)} %collective-permute-done.6.refs_3_, ...), custom_call_target="tpu_custom_call" | custom-call | tf_op jit(solution)/shard_map/rows/pallas_call | solution.py:536
  18.0 0.0 collective-permute-done.1.refs_2_
  18.0 0.3 %collective-permute-done.2.refs_3_ = bf16[20,16,128]{2,1,0:T(8,128)(2,1)S(1)} collective-permute-done((bf16[20,16,128]{2,1,0:T(8,128)(2,1)S(1)}, bf16[20,16,128]{2,1,0:T(8,128)(2,1)S(1)}, u32[]{:S(2)}, u32[]{:S(2)}) %collective-permute-start.2) | collective-permute-done | bytes 81952 | tf_op jit(solution)/shard_map/ppermute | solution.py:549
  18.3 4.0 %rows.3 = bf16[32,80,128]{2,1,0:T(8,128)(2,1)} custom-call(bf16[20,16,128]{2,1,0:T(8,128)(2,1)S(1)} %get-tuple-element.14.refs_0_, bf16[3,20,16,128]{3,2,1,0:T(8,128)(2,1)S(1)} %collective-permute-done.refs_1_, bf16[20,16,128]{2,1,0:T(8,128)(2,1)S(1)} %collective-permute-done.1.refs_2_, bf16[20,16,128]{2,1,0:T(8,128)(2,1)S(1)} %collective-permute-done.2.refs_3_, ...), custom_call_target="tpu_custom_call" | custom-call | tf_op jit(solution)/shard_map/rows/pallas_call | solution.py:536
Async XLA Ops:
  0.0 12.1 %copy-start = (bf16[128,384]{1,0:T(8,128)(2,1)S(1)}, bf16[128,384]{1,0:T(8,128)(2,1)}, u32[]{:S(2)}) copy-start(bf16[128,384]{1,0:T(8,128)(2,1)} %refs_4_.5) | copy-start | bytes 294916
  0.0 12.1 %copy-start.1 = (bf16[128,384]{1,0:T(8,128)(2,1)S(1)}, bf16[128,384]{1,0:T(8,128)(2,1)}, u32[]{:S(2)}) copy-start(bf16[128,384]{1,0:T(8,128)(2,1)} %refs_6_.5) | copy-start | bytes 294916
  0.0 12.1 %copy-start.2 = (bf16[128,128]{1,0:T(8,128)(2,1)S(1)}, bf16[128,128]{1,0:T(8,128)(2,1)}, u32[]{:S(2)}) copy-start(bf16[128,128]{1,0:T(8,128)(2,1)} %refs_5_.5) | copy-start | bytes 98308
  2.3 9.8 %collective-permute-start = (bf16[3,20,16,128]{3,2,1,0:T(8,128)(2,1)S(1)}, bf16[3,20,16,128]{3,2,1,0:T(8,128)(2,1)S(1)}, u32[]{:S(2)}, u32[]{:S(2)}) collective-permute-start(bf16[3,20,16,128]{3,2,1,0:T(8,128)(2,1)S(1)} %get-tuple-element.15), channel_id=1, source_target_pairs={{0,1},{1,0},{2,3},{3,2},{4,5},{5,4},{6,7},{7,6},{8,9},{9,8},{10,11... | collective-permute-start | bytes 737288 | tf_op jit(solution)/shard_map/ppermute | solution.py:549
  2.9 5.6 %collective-permute-start.3 = (bf16[20,16,128]{2,1,0:T(8,128)(2,1)S(1)}, bf16[20,16,128]{2,1,0:T(8,128)(2,1)S(1)}, u32[]{:S(2)}, u32[]{:S(2)}) collective-permute-start(bf16[20,16,128]{2,1,0:T(8,128)(2,1)S(1)} %get-tuple-element.18.refs_0_), channel_id=1, source_target_pairs={{0,2},{1,3},{2,0},{3,1},{4,6},{5,7},{6,4},{7,5},{8,10},{9,11},{10,... | collective-permute-start | bytes 245768 | tf_op jit(solution)/shard_map/ppermute | solution.py:549
  8.5 3.6 %collective-permute-start.4 = (bf16[20,16,128]{2,1,0:T(8,128)(2,1)S(1)}, bf16[20,16,128]{2,1,0:T(8,128)(2,1)S(1)}, u32[]{:S(2)}, u32[]{:S(2)}) collective-permute-start(bf16[20,16,128]{2,1,0:T(8,128)(2,1)S(1)} %collective-permute-done.3.refs_2_), channel_id=1, source_target_pairs={{0,1},{1,0},{2,3},{3,2},{4,5},{5,4},{6,7},{7,6},{8,9},{9,8},{10,11... | collective-permute-start | bytes 245768 | tf_op jit(solution)/shard_map/ppermute | solution.py:549
  8.5 5.9 %collective-permute-start.5 = (bf16[20,16,128]{2,1,0:T(8,128)(2,1)S(1)}, bf16[20,16,128]{2,1,0:T(8,128)(2,1)S(1)}, u32[]{:S(2)}, u32[]{:S(2)}) collective-permute-start(bf16[20,16,128]{2,1,0:T(8,128)(2,1)S(1)} %get-tuple-element.21), channel_id=1, source_target_pairs={{0,2},{1,3},{2,0},{3,1},{4,6},{5,7},{6,4},{7,5},{8,10},{9,11},{10,... | collective-permute-start | bytes 245768 | tf_op jit(solution)/shard_map/ppermute | solution.py:549
  10.2 4.6 %collective-permute-start.6 = (bf16[20,16,128]{2,1,0:T(8,128)(2,1)S(1)}, bf16[20,16,128]{2,1,0:T(8,128)(2,1)S(1)}, u32[]{:S(2)}, u32[]{:S(2)}) collective-permute-start(bf16[20,16,128]{2,1,0:T(8,128)(2,1)S(1)} %get-tuple-element.22), channel_id=1, source_target_pairs={{0,3},{1,2},{2,1},{3,0},{4,7},{5,6},{6,5},{7,4},{8,11},{9,10},{10,... | collective-permute-start | bytes 245768 | tf_op jit(solution)/shard_map/ppermute | solution.py:549
  10.3 7.7 %collective-permute-start.1 = (bf16[20,16,128]{2,1,0:T(8,128)(2,1)S(1)}, bf16[20,16,128]{2,1,0:T(8,128)(2,1)S(1)}, u32[]{:S(2)}, u32[]{:S(2)}) collective-permute-start(bf16[20,16,128]{2,1,0:T(8,128)(2,1)S(1)} %get-tuple-element.16), channel_id=1, source_target_pairs={{0,2},{1,3},{2,0},{3,1},{4,6},{5,7},{6,4},{7,5},{8,10},{9,11},{10,... | collective-permute-start | bytes 245768 | tf_op jit(solution)/shard_map/ppermute | solution.py:549
  12.1 2.7 %copy-start.3 = (bf16[128,128]{1,0:T(8,128)(2,1)S(1)}, bf16[128,128]{1,0:T(8,128)(2,1)}, u32[]{:S(2)}) copy-start(bf16[128,128]{1,0:T(8,128)(2,1)} %refs_7_.3) | copy-start | bytes 98308
  12.1 6.2 %collective-permute-start.2 = (bf16[20,16,128]{2,1,0:T(8,128)(2,1)S(1)}, bf16[20,16,128]{2,1,0:T(8,128)(2,1)S(1)}, u32[]{:S(2)}, u32[]{:S(2)}) collective-permute-start(bf16[20,16,128]{2,1,0:T(8,128)(2,1)S(1)} %get-tuple-element.17), channel_id=1, source_target_pairs={{0,3},{1,2},{2,1},{3,0},{4,7},{5,6},{6,5},{7,4},{8,11},{9,10},{10,... | collective-permute-start | bytes 245768 | tf_op jit(solution)/shard_map/ppermute | solution.py:549

commit v5 on v4

--- a/solution.py
+++ b/solution.py
@@ -180,7 +180,7 @@
     )
 
 
-PIECES = 4
+PIECES = 1
 
 
 def prepare_kernel(chunks, live_in, train_in, cells_in, bias_ref, train_out, *refs):
@@ -333,7 +333,20 @@
     return [jnp.where(mask, tensor, jnp.zeros_like(tensor)) for mask in masks]
 
 
-def attend(queries, keys, values, masks):
+def staggered(stages, count, lag=1):
+    for step in range(count + lag * (len(stages) - 1)):
+        for at, stage in enumerate(stages):
+            if 0 <= step - at * lag < count:
+                stage(step - at * lag)
+
+
+def over_keys(scores, axis):
+    top = jnp.max(scores, axis=axis, keepdims=True)
+    powers = jnp.exp2(scores - top)
+    return powers * (1.0 / jnp.sum(powers, axis=axis, keepdims=True))
+
+
+def feature_shares(queries, keys, masks):
     count = queries.shape[0]
     scores = lax.dot_general(
         jnp.concatenate(by_head(keys, masks), axis=0),
@@ -341,44 +354,80 @@
         (((1,), (1,)), ((), ())),
         preferred_element_type=jnp.float32,
     ).reshape(HEADS, count, count)
-    top = jnp.max(scores, axis=1, keepdims=True)
-    powers = jnp.exp2((scores - top) * SCALE2)
-    shares = powers * (1.0 / jnp.sum(powers, axis=1, keepdims=True))
-    shares = shares.reshape(HEADS * count, count).astype(jnp.bfloat16)
+    return over_keys(scores, 1).reshape(HEADS * count, count).astype(jnp.bfloat16)
+
+
+def feature_values(shares, values, masks):
     return lax.dot_general(
         shares,
         jnp.concatenate(by_head(values, masks), axis=0),
         (((0,), (0,)), ((), ())),
         preferred_element_type=jnp.float32,
-    )
-
-
-def feature_rows(held, mixed_ref, rows, qkv_ref, out_ref):
+    ).astype(jnp.bfloat16)
+
+
+STEP = 4
+
+
+def feature_rows(held, rows, qkv_ref, out_ref, consume):
     feats, width = held.shape[0] // pitch(rows), held.shape[1]
-    cells = [held[pl.ds(row, feats, stride=pitch(rows)), :] for row in range(rows)]
-    projected = jnp.dot(
-        jnp.concatenate(cells, axis=0).astype(jnp.bfloat16),
-        qkv_ref[...],
-        preferred_element_type=jnp.float32,
-    ).astype(jnp.bfloat16)
     masks = head_masks(feats, width)
-    attended = []
-    for row in range(rows):
-        block = projected[row * feats : (row + 1) * feats]
-        attended.append(
-            attend(
-                block[:, :width],
-                block[:, width : 2 * width],
-                block[:, 2 * width :],
+    size = math.gcd(rows, STEP)
+    cells, projected, shares, attended = {}, {}, {}, {}
+
+    def project(group):
+        cells[group] = jnp.concatenate(
+            [
+                held[pl.ds(group * size + row, feats, stride=pitch(rows)), :]
+                for row in range(size)
+            ],
+            axis=0,
+        )
+        every = jnp.dot(
+            cells[group].astype(jnp.bfloat16), qkv_ref[...], preferred_element_type=jnp.float32
+        )
+        projected[group] = [
+            (every[:, :width] * SCALE2).astype(jnp.bfloat16),
+            every[:, width : 2 * width].astype(jnp.bfloat16),
+            every[:, 2 * width :].astype(jnp.bfloat16),
+        ]
+
+    def score(group):
+        queries, keys, _ = projected[group]
+        shares[group] = [
+            feature_shares(
+                queries[row * feats : (row + 1) * feats],
+                keys[row * feats : (row + 1) * feats],
                 masks,
-            ).astype(jnp.bfloat16)
-        )
-    update = jnp.dot(
-        jnp.concatenate(attended, axis=0), out_ref[...], preferred_element_type=jnp.float32
-    )
-    for row in range(rows):
-        mixed = (cells[row] + update[row * feats : (row + 1) * feats]).astype(jnp.bfloat16)
-        mixed_ref[pl.ds(row * pitch(feats), feats), :] = mixed.astype(jnp.float32)
+            )
+            for row in range(size)
+        ]
+
+    def attend(group):
+        values = projected.pop(group)[2]
+        attended[group] = jnp.concatenate(
+            [
+                feature_values(part, values[row * feats : (row + 1) * feats], masks)
+                for row, part in enumerate(shares.pop(group))
+            ],
+            axis=0,
+        )
+
+    def mix(group):
+        update = jnp.dot(
+            attended.pop(group), out_ref[...], preferred_element_type=jnp.float32
+        )
+        consume(group * size, size, (cells.pop(group) + update).astype(jnp.bfloat16))
+
+    staggered([project, score, attend, mix], rows // size, 1)
+
+
+def put_rows(table, first, count, values):
+    feats = values.shape[0] // count
+    for row in range(count):
+        table[pl.ds((first + row) * pitch(feats), feats), :] = values[
+            row * feats : (row + 1) * feats
+        ]
 
 
 def by_feature(mixed_ref, first, count, rows, stride):
@@ -390,17 +439,20 @@
 def key_kernel(*refs):
     feat_devices = lax.axis_size("feat")
     parts = refs[:feat_devices]
-    feat_qkv, feat_out, item_qkv, out_ref, held, mixed_ref = refs[feat_devices:]
+    feat_qkv, feat_out, item_qkv, out_ref, held, key_ref, value_ref = refs[feat_devices:]
     feats, rows, width = out_ref.shape[0], out_ref.shape[1], held.shape[1]
     gather_parts(parts, 0, held)
-    feature_rows(held, mixed_ref, rows, feat_qkv, feat_out)
-    together = 128 // rows
-    for feat in range(0, feats, together):
-        mixed = by_feature(mixed_ref, feat, together, rows, pitch(feats)).astype(jnp.bfloat16)
+
+    def consume(first, count, mixed):
         both = jnp.dot(mixed, item_qkv[:, width:], preferred_element_type=jnp.float32)
-        out_ref[pl.ds(feat, together)] = both.astype(jnp.bfloat16).reshape(
-            together, rows, 2 * width
-        )
+        put_rows(key_ref, first, count, both[:, :width])
+        put_rows(value_ref, first, count, both[:, width:])
+
+    feature_rows(held, rows, feat_qkv, feat_out, consume)
+    for feat in range(feats):
+        here = pl.ds(feat, rows, stride=pitch(feats))
+        out_ref[feat, :, :width] = key_ref[here, :].astype(jnp.bfloat16)
+        out_ref[feat, :, width:] = value_ref[here, :].astype(jnp.bfloat16)
 
 
 def key_rows(parts, feat_qkv, feat_out, item_qkv):
@@ -413,6 +465,7 @@
         [
             pltpu.VMEM((feats * pitch(rows), width), jnp.float32),
             pltpu.VMEM((rows * pitch(feats), width), jnp.float32),
+            pltpu.VMEM((rows * pitch(feats), width), jnp.float32),
         ],
         24,
     )(*parts, feat_qkv, feat_out, item_qkv)
@@ -425,7 +478,7 @@
         feat_devices : feat_devices + 6
     ]
     results = refs[feat_devices + 6 : feat_devices + 6 + earlier]
-    out_ref, held, mixed_ref, query_ref, item_ref, total_ref, *own = refs[
+    out_ref, held, mixed_ref, query_ref, total_ref, *own = refs[
         feat_devices + 6 + earlier :
     ]
     rows, width = parts[0].shape[1], held.shape[1]
@@ -440,7 +493,13 @@
     for at, result in enumerate(results):
         send(result, at * rows, rows)
     gather_parts(parts, 1 + first_row // rows, held)
-    feature_rows(held, mixed_ref, rows, feat_qkv, feat_out)
+
+    def consume(first, count, mixed):
+        put_rows(mixed_ref, first, count, mixed.astype(jnp.float32))
+        queries = jnp.dot(mixed, item_qkv[:, :width], preferred_element_type=jnp.float32)
+        put_rows(query_ref, first, count, queries * SCALE2)
+
+    feature_rows(held, rows, feat_qkv, feat_out, consume)
 
     stride = pitch(feats)
     together = 128 // rows
@@ -453,60 +512,54 @@
     pair_lane = lax.broadcasted_iota(jnp.int32, (2 * rows, 2 * size), 1) // size
     pair_mask = pair_row == pair_lane
 
-    for first in range(0, feats, together):
-        mixed = by_feature(mixed_ref, first, together, rows, stride)
-        query_ref[pl.ds(first * rows, lanes), :] = jnp.dot(
-            mixed.astype(jnp.bfloat16), item_qkv[:, :width], preferred_element_type=jnp.float32
-        ).astype(jnp.bfloat16)
-
-    def item(first):
-        stacked_keys, stacked_values = [], []
-        for inner in range(together):
-            stacked_keys += by_head(keys_ref[first + inner, :, :width], key_masks)
-            stacked_values += by_head(keys_ref[first + inner, :, width:], key_masks)
+    shares, attended = {}, {}
+
+    def score(group):
+        first = group * together
+        stacked_keys = []
+        for feat in range(first, first + together):
+            stacked_keys += by_head(keys_ref[feat, :, :width], key_masks)
         every = lax.dot_general(
             jnp.concatenate(stacked_keys, axis=0),
-            query_ref[pl.ds(pl.multiple_of(first * rows, lanes), lanes), :],
+            by_feature(query_ref, first, together, rows, stride).astype(jnp.bfloat16),
             (((1,), (1,)), ((), ())),
             preferred_element_type=jnp.float32,
         )
         scores = every[:size]
         for inner in range(1, together):
             scores = jnp.where(lane_owner == inner, every[inner * size : (inner + 1) * size], scores)
-        scores = (scores + bias).reshape(HEADS, keys, lanes)
-        top = jnp.max(scores, axis=1, keepdims=True)
-        powers = jnp.exp2((scores - top) * SCALE2)
-        shares = powers * (1.0 / jnp.sum(powers, axis=1, keepdims=True))
-        shares = shares.reshape(size, lanes)
-        shares = jnp.transpose(jnp.concatenate([shares, shares], axis=0)).astype(jnp.bfloat16)
+        part = over_keys((scores + bias).reshape(HEADS, keys, lanes), 1).reshape(size, lanes)
+        shares[group] = jnp.transpose(jnp.concatenate([part, part], axis=0)).astype(jnp.bfloat16)
+
+    def attend(group):
+        part, results = shares.pop(group), []
         for pair in range(together // 2):
-            block = shares[pair * 2 * rows : (pair + 1) * 2 * rows]
-            here = pl.multiple_of((first + pair * 2) * rows, 2 * rows)
-            item_ref[pl.ds(here, 2 * rows), :] = jnp.dot(
-                jnp.where(pair_mask, block, jnp.zeros_like(block)),
-                jnp.concatenate(
-                    stacked_values[pair * 2 * HEADS : (pair + 1) * 2 * HEADS], axis=0
-                ),
-                preferred_element_type=jnp.float32,
-            ).astype(jnp.bfloat16)
-
-    def items(step, carry):
-        for inner in range(ITEM_STEP):
-            item((step * ITEM_STEP + inner) * together)
-        return carry
-
-    lax.fori_loop(0, feats // (together * ITEM_STEP), items, 0)
-    for first in range(0, feats, together):
-        update = jnp.dot(
-            item_ref[pl.ds(first * rows, lanes), :],
-            item_out[...],
-            preferred_element_type=jnp.float32,
-        )
+            block = part[pair * 2 * rows : (pair + 1) * 2 * rows]
+            stacked_values = []
+            for inner in range(2):
+                feat = group * together + pair * 2 + inner
+                stacked_values += by_head(keys_ref[feat, :, width:], key_masks)
+            results.append(
+                jnp.dot(
+                    jnp.where(pair_mask, block, jnp.zeros_like(block)),
+                    jnp.concatenate(stacked_values, axis=0),
+                    preferred_element_type=jnp.float32,
+                ).astype(jnp.bfloat16)
+            )
+        attended[group] = jnp.concatenate(results, axis=0)
+
+    def finish(group):
+        first = group * together
+        update = jnp.dot(attended.pop(group), item_out[...], preferred_element_type=jnp.float32)
         total = by_feature(mixed_ref, first, together, rows, stride) + update
         for inner in range(together):
             total_ref[pl.ds(first + inner, rows, stride=stride), :] = total[
                 inner * rows : (inner + 1) * rows
             ]
+
+    for stage in (score, attend, finish):
+        for group in range(feats // together):
+            stage(group)
     result_ref = own[0] if last else out_ref
     for row in range(rows):
         result_ref[row] = total_ref[pl.ds(row * stride, feats), :].astype(jnp.bfloat16)
@@ -518,7 +571,6 @@
 
 
 OUT_ROWS = 4
-ITEM_STEP = 10
 
 
 def own_rows(parts, feat_qkv, feat_out, item_qkv, item_out, keys, bias, total, first, results):
@@ -527,8 +579,7 @@
     last = first + rows == total
     results = results if last else []
     table = pltpu.VMEM((rows * pitch(feats), width), jnp.float32)
-    packed = pltpu.VMEM((rows * feats, width), jnp.bfloat16)
-    scratch = [pltpu.VMEM((feats * pitch(rows), width), jnp.float32), table, packed, packed, table]
+    scratch = [pltpu.VMEM((feats * pitch(rows), width), jnp.float32), table, table, table]
     if last:
         scratch.append(pltpu.VMEM((rows, feats, width), jnp.bfloat16))
         scratch.append(pltpu.SemaphoreType.DMA((len(results) + rows // OUT_ROWS,)))

time: 22.4 us -> 21.6 us (0.964)
  Pallas kernels: 11.8 us -> 10.2 us
  waiting for transfers between devices: 3.72 us -> 4.4 us
    pallas_call x2, Pallas kernels: 7.24 us -> 6.47 us  [own_rows(): pl.pallas_call(functools.partial(row_kernel, first, len(results), last),...]
    ppermute x7, waiting for transfers between devices: 3.72 us -> 4.4 us  [swap(): lax.ppermute(tensor, 'feat', [(one, one ^ step) for one in range(devices)])]
    pallas_call x1, Pallas kernels: 2.29 us -> 1.83 us  [prepare(): pl.pallas_call(functools.partial(prepare_kernel, chunks), out_shape=shape...]
    pallas_call x1, Pallas kernels: 2.25 us -> 1.93 us  [key_rows(): vmem_kernel(key_kernel, jax.ShapeDtypeStruct((feats, rows, 2 * width), jn...]
  transfers between devices with their start and end apart: 7 -> 7, of which waited for: 3 -> 3; matrix products, arithmetic and copies ran while one was open for 0% -> 0% of each run, Pallas kernels for 25% -> 22%
where the time goes in v5:
time: 21.6 us; the launch traced here: 21.5 us
  Pallas kernels  10.2 us (47%)
  starting transfers between devices  6.72 us (31%)
  waiting for transfers between devices  4.4 us (20%)
    ppermute x7, starting transfers between devices, swap(): lax.ppermute(tensor, 'feat', [(one, one ^ step) for one in range(devices)])  6.72 us
    pallas_call x2, Pallas kernels, own_rows(): pl.pallas_call(functools.partial(row_kernel, first, len(results), last),...  6.47 us
    ppermute x7, waiting for transfers between devices, swap(): lax.ppermute(tensor, 'feat', [(one, one ^ step) for one in range(devices)])  4.4 us
    pallas_call x1, Pallas kernels, key_rows(): vmem_kernel(key_kernel, jax.ShapeDtypeStruct((feats, rows, 2 * width), jn...  1.93 us
    pallas_call x1, Pallas kernels, prepare(): pl.pallas_call(functools.partial(prepare_kernel, chunks), out_shape=shape...  1.83 us
  transfers between devices with their start and end apart: 7, of which 3 were waited for; matrix products, arithmetic and copies ran while one was open for 0% of the time, Pallas kernels for 22%

profile of v5, /device:TPU:0, one launch (start us, length us, event | category | flops | bytes accessed | tf_op | source)
XLA Modules:
  0.0 21.5 jit_solution(353439756493846378)
XLA Ops:
  0.0 0.0 copy-start
  0.0 0.0 copy-start.1
  0.0 0.0 copy-start.2
  0.0 1.8 %prepare.1 = (f32[16,128]{1,0:T(8,128)S(1)}, bf16[20,16,128]{2,1,0:T(8,128)(2,1)S(1)}, bf16[3,20,16,128]{3,2,1,0:T(8,128)(2,1)S(1)}, bf16[20,16,128]{2,1,0:T(8,1...) custom-call(s32[8,128]{1,0:T(8,128)} %bitcast.4, ...), custom_call_target="tpu_custom_call" | custom-call | tf_op jit(solution)/shard_map/prepare/pallas_call | solution.py:288
  1.8 0.6 %collective-permute-start = (bf16[3,20,16,128]{3,2,1,0:T(8,128)(2,1)S(1)}, bf16[3,20,16,128]{3,2,1,0:T(8,128)(2,1)S(1)}, u32[]{:S(2)}, u32[]{:S(2)}) collective-permute-start(bf16[3,20,16,128]{3,2,1,0:T(8,128)(2,1)S(1)} %get-tuple-element.15), channel_id=1, source_target_pairs={{0,1},{1,0},{2,3},{3,2},{4,5},{5,4},{6,7},{7,6},{8,9},{9,8},{10,11... | collective-permute-start | bytes 737288 | tf_op jit(solution)/shard_map/ppermute | solution.py:600
  2.4 2.6 %collective-permute-start.3 = (bf16[20,16,128]{2,1,0:T(8,128)(2,1)S(1)}, bf16[20,16,128]{2,1,0:T(8,128)(2,1)S(1)}, u32[]{:S(2)}, u32[]{:S(2)}) collective-permute-start(bf16[20,16,128]{2,1,0:T(8,128)(2,1)S(1)} %get-tuple-element.18.refs_0_), channel_id=1, source_target_pairs={{0,2},{1,3},{2,0},{3,1},{4,6},{5,7},{6,4},{7,5},{8,10},{9,11},{10,... | collective-permute-start | bytes 245768 | tf_op jit(solution)/shard_map/ppermute | solution.py:600
  5.0 3.0 %collective-permute-done.3.refs_2_ = bf16[20,16,128]{2,1,0:T(8,128)(2,1)S(1)} collective-permute-done((bf16[20,16,128]{2,1,0:T(8,128)(2,1)S(1)}, bf16[20,16,128]{2,1,0:T(8,128)(2,1)S(1)}, u32[]{:S(2)}, u32[]{:S(2)}) %collective-permute-start.3) | collective-permute-done | bytes 81952 | tf_op jit(solution)/shard_map/ppermute | solution.py:600
  8.0 0.0 collective-permute-start.4
  8.0 1.7 %collective-permute-start.5 = (bf16[20,16,128]{2,1,0:T(8,128)(2,1)S(1)}, bf16[20,16,128]{2,1,0:T(8,128)(2,1)S(1)}, u32[]{:S(2)}, u32[]{:S(2)}) collective-permute-start(bf16[20,16,128]{2,1,0:T(8,128)(2,1)S(1)} %get-tuple-element.21), channel_id=1, source_target_pairs={{0,2},{1,3},{2,0},{3,1},{4,6},{5,7},{6,4},{7,5},{8,10},{9,11},{10,... | collective-permute-start | bytes 245768 | tf_op jit(solution)/shard_map/ppermute | solution.py:600
  9.7 0.1 collective-permute-start.6
  9.9 1.7 %collective-permute-start.1 = (bf16[20,16,128]{2,1,0:T(8,128)(2,1)S(1)}, bf16[20,16,128]{2,1,0:T(8,128)(2,1)S(1)}, u32[]{:S(2)}, u32[]{:S(2)}) collective-permute-start(bf16[20,16,128]{2,1,0:T(8,128)(2,1)S(1)} %get-tuple-element.16), channel_id=1, source_target_pairs={{0,2},{1,3},{2,0},{3,1},{4,6},{5,7},{6,4},{7,5},{8,10},{9,11},{10,... | collective-permute-start | bytes 245768 | tf_op jit(solution)/shard_map/ppermute | solution.py:600
  11.6 0.0 collective-permute-done.4.refs_3_
  11.6 0.0 copy-start.3
  11.6 0.0 collective-permute-start.2
  11.6 0.0 collective-permute-done.refs_1_
  11.6 0.0 copy-done
  11.6 0.0 copy-done.1
  11.6 0.0 copy-done.2
  11.7 1.9 %shard_map.73.refs_8_ = bf16[80,16,256]{2,1,0:T(8,128)(2,1)S(1)} custom-call(bf16[20,16,128]{2,1,0:T(8,128)(2,1)S(1)} %get-tuple-element.18.refs_0_, bf16[3,20,16,128]{3,2,1,0:T(8,128)(2,1)S(1)} %collective-permute-done.refs_1_, bf16[20,16,128]{2,1,0:T(8,128)(2,1)S(1)} %collective-permute-done.3.refs_2_, ...), custom_call_target="tpu_custom_call" | custom-call | tf_op jit(solution)/shard_map/pallas_call | solution.py:461
  13.6 0.0 collective-permute-done.5.refs_2_
  13.6 0.7 %collective-permute-done.6.refs_3_ = bf16[20,16,128]{2,1,0:T(8,128)(2,1)S(1)} collective-permute-done((bf16[20,16,128]{2,1,0:T(8,128)(2,1)S(1)}, bf16[20,16,128]{2,1,0:T(8,128)(2,1)S(1)}, u32[]{:S(2)}, u32[]{:S(2)}) %collective-permute-start.6) | collective-permute-done | bytes 81952 | tf_op jit(solution)/shard_map/ppermute | solution.py:600
  14.3 0.0 copy-done.3
  14.3 2.9 %rows.2.refs_10_ = bf16[16,80,128]{2,1,0:T(8,128)(2,1)S(1)} custom-call(bf16[20,16,128]{2,1,0:T(8,128)(2,1)S(1)} %get-tuple-element.20.refs_0_, bf16[3,20,16,128]{3,2,1,0:T(8,128)(2,1)S(1)} %collective-permute-done.refs_1_, bf16[20,16,128]{2,1,0:T(8,128)(2,1)S(1)} %collective-permute-done.5.refs_2_, bf16[20,16,128]{2,1,0:T(8,128)(2,1)S(1)} %collective-permute-done.6.refs_3_, ...), custom_call_target="tpu_custom_call" | custom-call | tf_op jit(solution)/shard_map/rows/pallas_call | solution.py:587
  17.2 0.0 collective-permute-done.1.refs_2_
  17.2 0.6 %collective-permute-done.2.refs_3_ = bf16[20,16,128]{2,1,0:T(8,128)(2,1)S(1)} collective-permute-done((bf16[20,16,128]{2,1,0:T(8,128)(2,1)S(1)}, bf16[20,16,128]{2,1,0:T(8,128)(2,1)S(1)}, u32[]{:S(2)}, u32[]{:S(2)}) %collective-permute-start.2) | collective-permute-done | bytes 81952 | tf_op jit(solution)/shard_map/ppermute | solution.py:600
  17.8 3.6 %rows.3 = bf16[32,80,128]{2,1,0:T(8,128)(2,1)} custom-call(bf16[20,16,128]{2,1,0:T(8,128)(2,1)S(1)} %get-tuple-element.14.refs_0_, bf16[3,20,16,128]{3,2,1,0:T(8,128)(2,1)S(1)} %collective-permute-done.refs_1_, bf16[20,16,128]{2,1,0:T(8,128)(2,1)S(1)} %collective-permute-done.1.refs_2_, bf16[20,16,128]{2,1,0:T(8,128)(2,1)S(1)} %collective-permute-done.2.refs_3_, ...), custom_call_target="tpu_custom_call" | custom-call | tf_op jit(solution)/shard_map/rows/pallas_call | solution.py:587
Async XLA Ops:
  0.0 11.6 %copy-start = (bf16[128,384]{1,0:T(8,128)(2,1)S(1)}, bf16[128,384]{1,0:T(8,128)(2,1)}, u32[]{:S(2)}) copy-start(bf16[128,384]{1,0:T(8,128)(2,1)} %refs_4_.5) | copy-start | bytes 294916
  0.0 11.6 %copy-start.1 = (bf16[128,384]{1,0:T(8,128)(2,1)S(1)}, bf16[128,384]{1,0:T(8,128)(2,1)}, u32[]{:S(2)}) copy-start(bf16[128,384]{1,0:T(8,128)(2,1)} %refs_6_.5) | copy-start | bytes 294916
  0.0 11.6 %copy-start.2 = (bf16[128,128]{1,0:T(8,128)(2,1)S(1)}, bf16[128,128]{1,0:T(8,128)(2,1)}, u32[]{:S(2)}) copy-start(bf16[128,128]{1,0:T(8,128)(2,1)} %refs_5_.5) | copy-start | bytes 98308
  1.8 9.8 %collective-permute-start = (bf16[3,20,16,128]{3,2,1,0:T(8,128)(2,1)S(1)}, bf16[3,20,16,128]{3,2,1,0:T(8,128)(2,1)S(1)}, u32[]{:S(2)}, u32[]{:S(2)}) collective-permute-start(bf16[3,20,16,128]{3,2,1,0:T(8,128)(2,1)S(1)} %get-tuple-element.15), channel_id=1, source_target_pairs={{0,1},{1,0},{2,3},{3,2},{4,5},{5,4},{6,7},{7,6},{8,9},{9,8},{10,11... | collective-permute-start | bytes 737288 | tf_op jit(solution)/shard_map/ppermute | solution.py:600
  2.4 5.6 %collective-permute-start.3 = (bf16[20,16,128]{2,1,0:T(8,128)(2,1)S(1)}, bf16[20,16,128]{2,1,0:T(8,128)(2,1)S(1)}, u32[]{:S(2)}, u32[]{:S(2)}) collective-permute-start(bf16[20,16,128]{2,1,0:T(8,128)(2,1)S(1)} %get-tuple-element.18.refs_0_), channel_id=1, source_target_pairs={{0,2},{1,3},{2,0},{3,1},{4,6},{5,7},{6,4},{7,5},{8,10},{9,11},{10,... | collective-permute-start | bytes 245768 | tf_op jit(solution)/shard_map/ppermute | solution.py:600
  8.0 3.6 %collective-permute-start.4 = (bf16[20,16,128]{2,1,0:T(8,128)(2,1)S(1)}, bf16[20,16,128]{2,1,0:T(8,128)(2,1)S(1)}, u32[]{:S(2)}, u32[]{:S(2)}) collective-permute-start(bf16[20,16,128]{2,1,0:T(8,128)(2,1)S(1)} %collective-permute-done.3.refs_2_), channel_id=1, source_target_pairs={{0,1},{1,0},{2,3},{3,2},{4,5},{5,4},{6,7},{7,6},{8,9},{9,8},{10,11... | collective-permute-start | bytes 245768 | tf_op jit(solution)/shard_map/ppermute | solution.py:600
  8.0 5.6 %collective-permute-start.5 = (bf16[20,16,128]{2,1,0:T(8,128)(2,1)S(1)}, bf16[20,16,128]{2,1,0:T(8,128)(2,1)S(1)}, u32[]{:S(2)}, u32[]{:S(2)}) collective-permute-start(bf16[20,16,128]{2,1,0:T(8,128)(2,1)S(1)} %get-tuple-element.21), channel_id=1, source_target_pairs={{0,2},{1,3},{2,0},{3,1},{4,6},{5,7},{6,4},{7,5},{8,10},{9,11},{10,... | collective-permute-start | bytes 245768 | tf_op jit(solution)/shard_map/ppermute | solution.py:600
  9.7 4.6 %collective-permute-start.6 = (bf16[20,16,128]{2,1,0:T(8,128)(2,1)S(1)}, bf16[20,16,128]{2,1,0:T(8,128)(2,1)S(1)}, u32[]{:S(2)}, u32[]{:S(2)}) collective-permute-start(bf16[20,16,128]{2,1,0:T(8,128)(2,1)S(1)} %get-tuple-element.22), channel_id=1, source_target_pairs={{0,3},{1,2},{2,1},{3,0},{4,7},{5,6},{6,5},{7,4},{8,11},{9,10},{10,... | collective-permute-start | bytes 245768 | tf_op jit(solution)/shard_map/ppermute | solution.py:600
  9.9 7.3 %collective-permute-start.1 = (bf16[20,16,128]{2,1,0:T(8,128)(2,1)S(1)}, bf16[20,16,128]{2,1,0:T(8,128)(2,1)S(1)}, u32[]{:S(2)}, u32[]{:S(2)}) collective-permute-start(bf16[20,16,128]{2,1,0:T(8,128)(2,1)S(1)} %get-tuple-element.16), channel_id=1, source_target_pairs={{0,2},{1,3},{2,0},{3,1},{4,6},{5,7},{6,4},{7,5},{8,10},{9,11},{10,... | collective-permute-start | bytes 245768 | tf_op jit(solution)/shard_map/ppermute | solution.py:600
  11.6 2.7 %copy-start.3 = (bf16[128,128]{1,0:T(8,128)(2,1)S(1)}, bf16[128,128]{1,0:T(8,128)(2,1)}, u32[]{:S(2)}) copy-start(bf16[128,128]{1,0:T(8,128)(2,1)} %refs_7_.3) | copy-start | bytes 98308
  11.6 6.2 %collective-permute-start.2 = (bf16[20,16,128]{2,1,0:T(8,128)(2,1)S(1)}, bf16[20,16,128]{2,1,0:T(8,128)(2,1)S(1)}, u32[]{:S(2)}, u32[]{:S(2)}) collective-permute-start(bf16[20,16,128]{2,1,0:T(8,128)(2,1)S(1)} %get-tuple-element.17), channel_id=1, source_target_pairs={{0,3},{1,2},{2,1},{3,0},{4,7},{5,6},{6,5},{7,4},{8,11},{9,10},{10,... | collective-permute-start | bytes 245768 | tf_op jit(solution)/shard_map/ppermute | solution.py:600

commit v6 on v5

--- a/solution.py
+++ b/solution.py
@@ -439,8 +439,8 @@
 def key_kernel(*refs):
     feat_devices = lax.axis_size("feat")
     parts = refs[:feat_devices]
-    feat_qkv, feat_out, item_qkv, out_ref, held, key_ref, value_ref = refs[feat_devices:]
-    feats, rows, width = out_ref.shape[0], out_ref.shape[1], held.shape[1]
+    feat_qkv, feat_out, item_qkv, key_ref, value_ref, held = refs[feat_devices:]
+    rows, width = parts[0].shape[1], held.shape[1]
     gather_parts(parts, 0, held)
 
     def consume(first, count, mixed):
@@ -449,24 +449,17 @@
         put_rows(value_ref, first, count, both[:, width:])
 
     feature_rows(held, rows, feat_qkv, feat_out, consume)
-    for feat in range(feats):
-        here = pl.ds(feat, rows, stride=pitch(feats))
-        out_ref[feat, :, :width] = key_ref[here, :].astype(jnp.bfloat16)
-        out_ref[feat, :, width:] = value_ref[here, :].astype(jnp.bfloat16)
 
 
 def key_rows(parts, feat_qkv, feat_out, item_qkv):
     feats_here, rows, width = parts[0].shape
     feats = len(parts) * feats_here
+    table = jax.ShapeDtypeStruct((rows * pitch(feats), width), jnp.float32)
     return vmem_kernel(
         key_kernel,
-        jax.ShapeDtypeStruct((feats, rows, 2 * width), jnp.bfloat16),
+        [table, table],
         len(parts) + 3,
-        [
-            pltpu.VMEM((feats * pitch(rows), width), jnp.float32),
-            pltpu.VMEM((rows * pitch(feats), width), jnp.float32),
-            pltpu.VMEM((rows * pitch(feats), width), jnp.float32),
-        ],
+        [pltpu.VMEM((feats * pitch(rows), width), jnp.float32)],
         24,
     )(*parts, feat_qkv, feat_out, item_qkv)
 
@@ -474,15 +467,15 @@
 def row_kernel(first_row, earlier, last, *refs):
     feat_devices = lax.axis_size("feat")
     parts = refs[:feat_devices]
-    (feat_qkv, feat_out, item_qkv, item_out, keys_ref, bias_ref) = refs[
-        feat_devices : feat_devices + 6
+    (feat_qkv, feat_out, item_qkv, item_out, key_ref, value_ref, bias_ref) = refs[
+        feat_devices : feat_devices + 7
     ]
-    results = refs[feat_devices + 6 : feat_devices + 6 + earlier]
+    results = refs[feat_devices + 7 : feat_devices + 7 + earlier]
     out_ref, held, mixed_ref, query_ref, total_ref, *own = refs[
-        feat_devices + 6 + earlier :
+        feat_devices + 7 + earlier :
     ]
     rows, width = parts[0].shape[1], held.shape[1]
-    feats, keys = keys_ref.shape[0], keys_ref.shape[1]
+    feats, keys = feat_devices * parts[0].shape[0], bias_ref.shape[0]
     copies = []
 
     def send(source, at, count):
@@ -518,7 +511,9 @@
         first = group * together
         stacked_keys = []
         for feat in range(first, first + together):
-            stacked_keys += by_head(keys_ref[feat, :, :width], key_masks)
+            stacked_keys += by_head(
+                key_ref[pl.ds(feat, keys, stride=stride), :].astype(jnp.bfloat16), key_masks
+            )
         every = lax.dot_general(
             jnp.concatenate(stacked_keys, axis=0),
             by_feature(query_ref, first, together, rows, stride).astype(jnp.bfloat16),
@@ -538,7 +533,9 @@
             stacked_values = []
             for inner in range(2):
                 feat = group * together + pair * 2 + inner
-                stacked_values += by_head(keys_ref[feat, :, width:], key_masks)
+                stacked_values += by_head(
+                    value_ref[pl.ds(feat, keys, stride=stride), :].astype(jnp.bfloat16), key_masks
+                )
             results.append(
                 jnp.dot(
                     jnp.where(pair_mask, block, jnp.zeros_like(block)),
@@ -587,12 +584,12 @@
     return pl.pallas_call(
         functools.partial(row_kernel, first, len(results), last),
         out_shape=jax.ShapeDtypeStruct((total if last else rows, feats, width), jnp.bfloat16),
-        in_specs=[block] * (len(parts) + 6 + len(results)),
+        in_specs=[block] * (len(parts) + 7 + len(results)),
         out_specs=pl.BlockSpec(memory_space=pltpu.HBM) if last else block,
         scratch_shapes=scratch,
         compiler_params=pltpu.CompilerParams(vmem_limit_bytes=24 << 20),
         name="rows",
-    )(*parts, feat_qkv, feat_out, item_qkv, item_out, keys, bias, *results)
+    )(*parts, feat_qkv, feat_out, item_qkv, item_out, *keys, bias, *results)
 
 
 def swap(tensor, step):

time: 21.6 us -> 21.6 us (level)
  no operation moved by 1% of the time
where the time goes in v6:
time: 21.6 us; the launch traced here: 21.4 us
  Pallas kernels  10.1 us (47%)
  starting transfers between devices  6.72 us (31%)
  waiting for transfers between devices  4.53 us (21%)
    ppermute x7, starting transfers between devices, swap(): lax.ppermute(tensor, 'feat', [(one, one ^ step) for one in range(devices)])  6.72 us
    pallas_call x2, Pallas kernels, own_rows(): pl.pallas_call(functools.partial(row_kernel, first, len(results), last),...  6.45 us
    ppermute x7, waiting for transfers between devices, swap(): lax.ppermute(tensor, 'feat', [(one, one ^ step) for one in range(devices)])  4.53 us
    pallas_call x1, Pallas kernels, prepare(): pl.pallas_call(functools.partial(prepare_kernel, chunks), out_shape=shape...  1.83 us
    pallas_call x1, Pallas kernels, key_rows(): vmem_kernel(key_kernel, [table, table], len(parts) + 3, [pltpu.VMEM((feat...  1.83 us
  transfers between devices with their start and end apart: 7, of which 3 were waited for; matrix products, arithmetic and copies ran while one was open for 0% of the time, Pallas kernels for 22%

profile of v6, /device:TPU:0, one launch (start us, length us, event | category | flops | bytes accessed | tf_op | source)
XLA Modules:
  0.0 21.4 jit_solution(5847832864847316080)
XLA Ops:
  0.0 0.0 copy-start
  0.0 0.0 copy-start.1
  0.0 0.0 copy-start.2
  0.0 1.8 %prepare.1 = (f32[16,128]{1,0:T(8,128)S(1)}, bf16[20,16,128]{2,1,0:T(8,128)(2,1)S(1)}, bf16[3,20,16,128]{3,2,1,0:T(8,128)(2,1)S(1)}, bf16[20,16,128]{2,1,0:T(8,1...) custom-call(s32[8,128]{1,0:T(8,128)} %bitcast.4, ...), custom_call_target="tpu_custom_call" | custom-call | tf_op jit(solution)/shard_map/prepare/pallas_call | solution.py:288
  1.8 0.6 %collective-permute-start = (bf16[3,20,16,128]{3,2,1,0:T(8,128)(2,1)S(1)}, bf16[3,20,16,128]{3,2,1,0:T(8,128)(2,1)S(1)}, u32[]{:S(2)}, u32[]{:S(2)}) collective-permute-start(bf16[3,20,16,128]{3,2,1,0:T(8,128)(2,1)S(1)} %get-tuple-element.17), channel_id=1, source_target_pairs={{0,1},{1,0},{2,3},{3,2},{4,5},{5,4},{6,7},{7,6},{8,9},{9,8},{10,11... | collective-permute-start | bytes 737288 | tf_op jit(solution)/shard_map/ppermute | solution.py:597
  2.4 2.6 %collective-permute-start.3 = (bf16[20,16,128]{2,1,0:T(8,128)(2,1)S(1)}, bf16[20,16,128]{2,1,0:T(8,128)(2,1)S(1)}, u32[]{:S(2)}, u32[]{:S(2)}) collective-permute-start(bf16[20,16,128]{2,1,0:T(8,128)(2,1)S(1)} %get-tuple-element.20.refs_0_), channel_id=1, source_target_pairs={{0,2},{1,3},{2,0},{3,1},{4,6},{5,7},{6,4},{7,5},{8,10},{9,11},{10,... | collective-permute-start | bytes 245768 | tf_op jit(solution)/shard_map/ppermute | solution.py:597
  5.0 3.0 %collective-permute-done.3.refs_2_ = bf16[20,16,128]{2,1,0:T(8,128)(2,1)S(1)} collective-permute-done((bf16[20,16,128]{2,1,0:T(8,128)(2,1)S(1)}, bf16[20,16,128]{2,1,0:T(8,128)(2,1)S(1)}, u32[]{:S(2)}, u32[]{:S(2)}) %collective-permute-start.3) | collective-permute-done | bytes 81952 | tf_op jit(solution)/shard_map/ppermute | solution.py:597
  8.0 0.0 collective-permute-start.4
  8.0 1.7 %collective-permute-start.5 = (bf16[20,16,128]{2,1,0:T(8,128)(2,1)S(1)}, bf16[20,16,128]{2,1,0:T(8,128)(2,1)S(1)}, u32[]{:S(2)}, u32[]{:S(2)}) collective-permute-start(bf16[20,16,128]{2,1,0:T(8,128)(2,1)S(1)} %get-tuple-element.25), channel_id=1, source_target_pairs={{0,2},{1,3},{2,0},{3,1},{4,6},{5,7},{6,4},{7,5},{8,10},{9,11},{10,... | collective-permute-start | bytes 245768 | tf_op jit(solution)/shard_map/ppermute | solution.py:597
  9.7 0.1 collective-permute-start.6
  9.9 1.7 %collective-permute-start.1 = (bf16[20,16,128]{2,1,0:T(8,128)(2,1)S(1)}, bf16[20,16,128]{2,1,0:T(8,128)(2,1)S(1)}, u32[]{:S(2)}, u32[]{:S(2)}) collective-permute-start(bf16[20,16,128]{2,1,0:T(8,128)(2,1)S(1)} %get-tuple-element.18), channel_id=1, source_target_pairs={{0,2},{1,3},{2,0},{3,1},{4,6},{5,7},{6,4},{7,5},{8,10},{9,11},{10,... | collective-permute-start | bytes 245768 | tf_op jit(solution)/shard_map/ppermute | solution.py:597
  11.6 0.0 collective-permute-done.4.refs_3_
  11.6 0.0 copy-start.3
  11.6 0.0 collective-permute-start.2
  11.6 0.0 collective-permute-done.refs_1_
  11.6 0.0 copy-done
  11.6 0.0 copy-done.1
  11.6 0.0 copy-done.2
  11.7 1.8 %shard_map.73 = (f32[1344,128]{1,0:T(8,128)S(1)}, f32[1344,128]{1,0:T(8,128)S(1)}) custom-call(bf16[20,16,128]{2,1,0:T(8,128)(2,1)S(1)} %get-tuple-element.20.refs_0_, bf16[3,20,16,128]{3,2,1,0:T(8,128)(2,1)S(1)} %collective-permute-done.refs_1_, bf16[20,16,128]{2,1,0:T(8,128)(2,1)S(1)} %collective-permute-done.3.refs_2_, ...), custom_call_target="tpu_custom_call" | custom-call | tf_op jit(solution)/shard_map/pallas_call | solution.py:458
  13.5 0.0 collective-permute-done.5.refs_2_
  13.5 0.8 %collective-permute-done.6.refs_3_ = bf16[20,16,128]{2,1,0:T(8,128)(2,1)S(1)} collective-permute-done((bf16[20,16,128]{2,1,0:T(8,128)(2,1)S(1)}, bf16[20,16,128]{2,1,0:T(8,128)(2,1)S(1)}, u32[]{:S(2)}, u32[]{:S(2)}) %collective-permute-start.6) | collective-permute-done | bytes 81952 | tf_op jit(solution)/shard_map/ppermute | solution.py:597
  14.3 0.0 copy-done.3
  14.3 2.8 %rows.2.refs_11_ = bf16[16,80,128]{2,1,0:T(8,128)(2,1)S(1)} custom-call(bf16[20,16,128]{2,1,0:T(8,128)(2,1)S(1)} %get-tuple-element.24.refs_0_, bf16[3,20,16,128]{3,2,1,0:T(8,128)(2,1)S(1)} %collective-permute-done.refs_1_, bf16[20,16,128]{2,1,0:T(8,128)(2,1)S(1)} %collective-permute-done.5.refs_2_, bf16[20,16,128]{2,1,0:T(8,128)(2,1)S(1)} %collective-permute-done.6.refs_3_, ...), custom_call_target="tpu_custom_call" | custom-call | tf_op jit(solution)/shard_map/rows/pallas_call | solution.py:584
  17.2 0.0 collective-permute-done.1.refs_2_
  17.2 0.6 %collective-permute-done.2.refs_3_ = bf16[20,16,128]{2,1,0:T(8,128)(2,1)S(1)} collective-permute-done((bf16[20,16,128]{2,1,0:T(8,128)(2,1)S(1)}, bf16[20,16,128]{2,1,0:T(8,128)(2,1)S(1)}, u32[]{:S(2)}, u32[]{:S(2)}) %collective-permute-start.2) | collective-permute-done | bytes 81952 | tf_op jit(solution)/shard_map/ppermute | solution.py:597
  17.8 3.6 %rows.3 = bf16[32,80,128]{2,1,0:T(8,128)(2,1)} custom-call(bf16[20,16,128]{2,1,0:T(8,128)(2,1)S(1)} %get-tuple-element.16.refs_0_, bf16[3,20,16,128]{3,2,1,0:T(8,128)(2,1)S(1)} %collective-permute-done.refs_1_, bf16[20,16,128]{2,1,0:T(8,128)(2,1)S(1)} %collective-permute-done.1.refs_2_, bf16[20,16,128]{2,1,0:T(8,128)(2,1)S(1)} %collective-permute-done.2.refs_3_, ...), custom_call_target="tpu_custom_call" | custom-call | tf_op jit(solution)/shard_map/rows/pallas_call | solution.py:584
Async XLA Ops:
  0.0 11.6 %copy-start = (bf16[128,384]{1,0:T(8,128)(2,1)S(1)}, bf16[128,384]{1,0:T(8,128)(2,1)}, u32[]{:S(2)}) copy-start(bf16[128,384]{1,0:T(8,128)(2,1)} %refs_4_.5) | copy-start | bytes 294916
  0.0 11.6 %copy-start.1 = (bf16[128,384]{1,0:T(8,128)(2,1)S(1)}, bf16[128,384]{1,0:T(8,128)(2,1)}, u32[]{:S(2)}) copy-start(bf16[128,384]{1,0:T(8,128)(2,1)} %refs_6_.5) | copy-start | bytes 294916
  0.0 11.6 %copy-start.2 = (bf16[128,128]{1,0:T(8,128)(2,1)S(1)}, bf16[128,128]{1,0:T(8,128)(2,1)}, u32[]{:S(2)}) copy-start(bf16[128,128]{1,0:T(8,128)(2,1)} %refs_5_.5) | copy-start | bytes 98308
  1.8 9.8 %collective-permute-start = (bf16[3,20,16,128]{3,2,1,0:T(8,128)(2,1)S(1)}, bf16[3,20,16,128]{3,2,1,0:T(8,128)(2,1)S(1)}, u32[]{:S(2)}, u32[]{:S(2)}) collective-permute-start(bf16[3,20,16,128]{3,2,1,0:T(8,128)(2,1)S(1)} %get-tuple-element.17), channel_id=1, source_target_pairs={{0,1},{1,0},{2,3},{3,2},{4,5},{5,4},{6,7},{7,6},{8,9},{9,8},{10,11... | collective-permute-start | bytes 737288 | tf_op jit(solution)/shard_map/ppermute | solution.py:597
  2.4 5.6 %collective-permute-start.3 = (bf16[20,16,128]{2,1,0:T(8,128)(2,1)S(1)}, bf16[20,16,128]{2,1,0:T(8,128)(2,1)S(1)}, u32[]{:S(2)}, u32[]{:S(2)}) collective-permute-start(bf16[20,16,128]{2,1,0:T(8,128)(2,1)S(1)} %get-tuple-element.20.refs_0_), channel_id=1, source_target_pairs={{0,2},{1,3},{2,0},{3,1},{4,6},{5,7},{6,4},{7,5},{8,10},{9,11},{10,... | collective-permute-start | bytes 245768 | tf_op jit(solution)/shard_map/ppermute | solution.py:597
  8.0 3.6 %collective-permute-start.4 = (bf16[20,16,128]{2,1,0:T(8,128)(2,1)S(1)}, bf16[20,16,128]{2,1,0:T(8,128)(2,1)S(1)}, u32[]{:S(2)}, u32[]{:S(2)}) collective-permute-start(bf16[20,16,128]{2,1,0:T(8,128)(2,1)S(1)} %collective-permute-done.3.refs_2_), channel_id=1, source_target_pairs={{0,1},{1,0},{2,3},{3,2},{4,5},{5,4},{6,7},{7,6},{8,9},{9,8},{10,11... | collective-permute-start | bytes 245768 | tf_op jit(solution)/shard_map/ppermute | solution.py:597
  8.0 5.5 %collective-permute-start.5 = (bf16[20,16,128]{2,1,0:T(8,128)(2,1)S(1)}, bf16[20,16,128]{2,1,0:T(8,128)(2,1)S(1)}, u32[]{:S(2)}, u32[]{:S(2)}) collective-permute-start(bf16[20,16,128]{2,1,0:T(8,128)(2,1)S(1)} %get-tuple-element.25), channel_id=1, source_target_pairs={{0,2},{1,3},{2,0},{3,1},{4,6},{5,7},{6,4},{7,5},{8,10},{9,11},{10,... | collective-permute-start | bytes 245768 | tf_op jit(solution)/shard_map/ppermute | solution.py:597
  9.7 4.6 %collective-permute-start.6 = (bf16[20,16,128]{2,1,0:T(8,128)(2,1)S(1)}, bf16[20,16,128]{2,1,0:T(8,128)(2,1)S(1)}, u32[]{:S(2)}, u32[]{:S(2)}) collective-permute-start(bf16[20,16,128]{2,1,0:T(8,128)(2,1)S(1)} %get-tuple-element.26), channel_id=1, source_target_pairs={{0,3},{1,2},{2,1},{3,0},{4,7},{5,6},{6,5},{7,4},{8,11},{9,10},{10,... | collective-permute-start | bytes 245768 | tf_op jit(solution)/shard_map/ppermute | solution.py:597
  9.9 7.3 %collective-permute-start.1 = (bf16[20,16,128]{2,1,0:T(8,128)(2,1)S(1)}, bf16[20,16,128]{2,1,0:T(8,128)(2,1)S(1)}, u32[]{:S(2)}, u32[]{:S(2)}) collective-permute-start(bf16[20,16,128]{2,1,0:T(8,128)(2,1)S(1)} %get-tuple-element.18), channel_id=1, source_target_pairs={{0,2},{1,3},{2,0},{3,1},{4,6},{5,7},{6,4},{7,5},{8,10},{9,11},{10,... | collective-permute-start | bytes 245768 | tf_op jit(solution)/shard_map/ppermute | solution.py:597
  11.6 2.7 %copy-start.3 = (bf16[128,128]{1,0:T(8,128)(2,1)S(1)}, bf16[128,128]{1,0:T(8,128)(2,1)}, u32[]{:S(2)}) copy-start(bf16[128,128]{1,0:T(8,128)(2,1)} %refs_7_.3) | copy-start | bytes 98308
  11.6 6.2 %collective-permute-start.2 = (bf16[20,16,128]{2,1,0:T(8,128)(2,1)S(1)}, bf16[20,16,128]{2,1,0:T(8,128)(2,1)S(1)}, u32[]{:S(2)}, u32[]{:S(2)}) collective-permute-start(bf16[20,16,128]{2,1,0:T(8,128)(2,1)S(1)} %get-tuple-element.19), channel_id=1, source_target_pairs={{0,3},{1,2},{2,1},{3,0},{4,7},{5,6},{6,5},{7,4},{8,11},{9,10},{10,... | collective-permute-start | bytes 245768 | tf_op jit(solution)/shard_map/ppermute | solution.py:597
